TPU v7x, 32 devices: a whole 2x2x4 slice. The times are simulated.
32 devices in a mesh: member: 2 (over y), slab: 4 (over z), chan: 2 (over x), mode: 2 (over core).
Axes of the slice: x: 2, y: 2, z: 4, core: 2. Of those that a mesh axis runs over, the one named last changes fastest.
Arguments:
- source_field: float32 [128, 1024, 1024], P(('member', 'chan'), 'slab', 'mode'), parts along dimension 0, may hold values from -6 to 6
- cotangent: float32 [128, 1024, 1024], P(('member', 'chan'), 'slab', 'mode'), parts along dimension 0, may hold values from -6 to 6
- spectral_weight: float32 [128, 64, 32, 2, 64], P(('member', 'chan'), None, 'mode', None, 'slab'), parts along dimension 0, may hold values from -12 to 12
- skip_gain: float32 [128], P(('member', 'chan')), parts along dimension 0, may hold values from 0.5 to 2
- channel_bias: float32 [128], P(('member', 'chan')), parts along dimension 0, may hold values from -0.5 to 0.5
- mode_limit: int32 [128, 2], P('member'), parts along dimension 0, may hold values from 16 to 32
- width_limit: int32 [128], P('member'), parts along dimension 0, may hold values from 32 to 64
Outputs:
- output: float32 [128, 1024, 1024], P(('member', 'chan'), 'slab', 'mode'), parts along dimension 0
- field_grad: float32 [128, 1024, 1024], P(('member', 'chan'), 'slab', 'mode'), parts along dimension 0
- spectral_grad: float32 [128, 64, 32, 2, 64], P(('member', 'chan'), None, 'mode', None, 'slab'), parts along dimension 0
- gate_grad: float32 [128], P(('member', 'chan')), parts along dimension 0
- bias_grad: float32 [128], P(('member', 'chan')), parts along dimension 0
There are 2 independent parts, one for each index of `member`. A program takes and returns all parts, laid end to end along the dimension named above; each array names one. Nothing has to cross between parts.
Inputs may be any that keep to these rules, and one draw needn't show every extreme that they name: `mode_limit`: never more than 32. `width_limit`: never more than 64.
All inputs are finite; a program needn't handle non-finite values.
Results may differ from a plain program's by a relative error of at most 0.00018.
Values sent between devices are 32-bit elements; how exact they have to be, the bound alone decides.
No kernel may reach another device: no remote copies, remote signals or barrier semaphores. Data moves between devices by JAX's collectives and lax.ppermute only.
A program may use at most 192 MiB of HBM per device.

v0:
```python
import math

import jax
import jax.numpy as jnp
from jax import lax
from jax.sharding import PartitionSpec as P

precise = lax.Precision.HIGHEST


def column_table(extent, freq_count, first_cell, cell_count):
    cell_index = first_cell + jnp.arange(cell_count, dtype=jnp.int32)
    wave_index = jnp.arange(freq_count, dtype=jnp.int32)
    products = (cell_index[:, None] * wave_index[None, :] % extent).astype(jnp.float32)
    angles = products * (2.0 * math.pi / extent)
    return jnp.stack([jnp.cos(angles), -jnp.sin(angles)], axis=-1).reshape(
        cell_count, 2 * freq_count
    )


def row_tables(extent, freq_count, first_cell, cell_count):
    cell_index = first_cell + jnp.arange(cell_count, dtype=jnp.int32)
    column = jnp.arange(2 * freq_count, dtype=jnp.int32)
    wave_index = column + jnp.where(column >= freq_count, extent - 2 * freq_count, 0)
    products = (cell_index[:, None] * wave_index[None, :] % extent).astype(jnp.float32)
    angles = products * (2.0 * math.pi / extent)
    return (jnp.cos(angles), jnp.sin(angles))


def row_forward(lined, row_cos, row_sin):
    line_real = lined[:, 0]
    line_imag = lined[:, 1]
    out_real = jnp.dot(line_real, row_cos, precision=precise) + jnp.dot(
        line_imag, row_sin, precision=precise
    )
    out_imag = jnp.dot(line_imag, row_cos, precision=precise) - jnp.dot(
        line_real, row_sin, precision=precise
    )
    return jnp.stack([out_real, out_imag], axis=1)


def row_inverse(modes_in, row_cos, row_sin):
    mode_real = modes_in[:, 0]
    mode_imag = modes_in[:, 1]
    back_real = jnp.dot(mode_real, row_cos.T, precision=precise) - jnp.dot(
        mode_imag, row_sin.T, precision=precise
    )
    back_imag = jnp.dot(mode_real, row_sin.T, precision=precise) + jnp.dot(
        mode_imag, row_cos.T, precision=precise
    )
    return jnp.stack([back_real, back_imag], axis=1)


def contract(spectra, weight):
    spec_real = spectra[:, :, 0]
    spec_imag = spectra[:, :, 1]
    weight_real = weight[:, :, :, 0]
    weight_imag = weight[:, :, :, 1]
    out_real = jnp.einsum("iyx,ioyx->oyx", spec_real, weight_real, precision=precise) - jnp.einsum(
        "iyx,ioyx->oyx", spec_imag, weight_imag, precision=precise
    )
    out_imag = jnp.einsum("iyx,ioyx->oyx", spec_real, weight_imag, precision=precise) + jnp.einsum(
        "iyx,ioyx->oyx", spec_imag, weight_real, precision=precise
    )
    return jnp.stack([out_real, out_imag], axis=2)


def contract_back(grads, weight):
    grad_real = grads[:, :, 0]
    grad_imag = grads[:, :, 1]
    weight_real = weight[:, :, :, 0]
    weight_imag = weight[:, :, :, 1]
    back_real = jnp.einsum("oyx,ioyx->iyx", grad_real, weight_real, precision=precise) + jnp.einsum(
        "oyx,ioyx->iyx", grad_imag, weight_imag, precision=precise
    )
    back_imag = jnp.einsum("oyx,ioyx->iyx", grad_imag, weight_real, precision=precise) - jnp.einsum(
        "oyx,ioyx->iyx", grad_real, weight_imag, precision=precise
    )
    return jnp.stack([back_real, back_imag], axis=2)


def outer_grad(spectra, grads):
    spec_real = spectra[:, :, 0]
    spec_imag = spectra[:, :, 1]
    grad_real = grads[:, :, 0]
    grad_imag = grads[:, :, 1]
    real_side = jnp.einsum("iyx,oyx->ioyx", spec_real, grad_real) + jnp.einsum(
        "iyx,oyx->ioyx", spec_imag, grad_imag
    )
    imag_side = jnp.einsum("iyx,oyx->ioyx", spec_real, grad_imag) - jnp.einsum(
        "iyx,oyx->ioyx", spec_imag, grad_real
    )
    return jnp.stack([real_side, imag_side], axis=3)


def mode_weights(limit_rows, col_freq, row_freq, kx_count, cells_total):
    keep_cols = col_freq[None, :] < limit_rows[:, 0:1]
    keep_rows = (row_freq[None, :] < limit_rows[:, 1:2]) | (
        (kx_count - row_freq)[None, :] < limit_rows[:, 1:2]
    )
    scales = jnp.where(col_freq == 0, 1.0, 2.0).astype(jnp.float32) / cells_total
    joined = keep_cols[:, :, None] & keep_rows[:, None, :]
    return (joined.astype(jnp.float32) * scales[None, :, None])[:, :, None, :]


def read_mask(in_index, width_limit):
    return (in_index[:, None] < width_limit[None, :]).astype(jnp.float32)[:, :, None, None, None]


def local(
    source_field, cotangent, spectral_weight, skip_gain, channel_bias, mode_limit, width_limit
):
    channels, row_count, col_count = source_field.shape
    slab_count = lax.axis_size("slab")
    mode_count = lax.axis_size("mode")
    slab_index = lax.axis_index("slab")
    mode_index = lax.axis_index("mode")
    chan_index = lax.axis_index("chan")
    local_freq = spectral_weight.shape[2]
    local_kx = spectral_weight.shape[4]
    freq_count = local_freq * mode_count
    kx_count = local_kx * slab_count
    all_rows = row_count * slab_count
    all_cols = col_count * mode_count
    column_tab = column_table(all_cols, freq_count, mode_index * col_count, col_count)
    row_cos, row_sin = row_tables(all_rows, freq_count, slab_index * row_count, row_count)

    def spectrum(values):
        partial_cols = jnp.einsum("chw,wk->ckh", values, column_tab, precision=precise)
        summed_cols = lax.psum_scatter(partial_cols, "mode", scatter_dimension=1, tiled=True)
        paired = summed_cols.reshape(values.shape[0] * local_freq, 2, row_count)
        spectra = lax.psum_scatter(
            row_forward(paired, row_cos, row_sin), "slab", scatter_dimension=2, tiled=True
        )
        return spectra.reshape(values.shape[0], local_freq, 2, local_kx)

    def synthesis(modes_in):
        whole_modes = lax.all_gather(modes_in, "slab", axis=3, tiled=True)
        rebuilt = row_inverse(
            whole_modes.reshape(channels * local_freq, 2, kx_count), row_cos, row_sin
        )
        rebuilt = rebuilt.reshape(channels, 2 * local_freq, row_count)
        gathered = lax.all_gather(rebuilt, "mode", axis=1, tiled=True)
        return jnp.einsum("ckh,wk->chw", gathered, column_tab, precision=precise)

    in_index = chan_index * channels + jnp.arange(channels, dtype=jnp.int32)
    col_freq = mode_index * local_freq + jnp.arange(local_freq, dtype=jnp.int32)
    row_freq = slab_index * local_kx + jnp.arange(local_kx, dtype=jnp.int32)
    limit_rows = lax.dynamic_slice_in_dim(mode_limit, chan_index * channels, channels, 0)
    weights = mode_weights(limit_rows, col_freq, row_freq, kx_count, all_rows * all_cols)
    reads = read_mask(in_index, width_limit)
    masked_weight = spectral_weight * reads
    spectra = spectrum(source_field)
    out_modes = (
        lax.psum_scatter(contract(spectra, masked_weight), "chan", scatter_dimension=0, tiled=True)
        * weights
    )
    branch = synthesis(out_modes)
    skip_scale = skip_gain[:, None, None]
    summed = branch + skip_scale * source_field + channel_bias[:, None, None]
    output, gelu_back = jax.vjp(jax.nn.gelu, summed)
    grad_sum = gelu_back(cotangent)[0]
    grad_modes = spectrum(grad_sum) * weights
    all_grads = lax.all_gather(grad_modes, "chan", axis=0, tiled=True)
    spectral_grad = outer_grad(spectra, all_grads) * reads
    field_grad = synthesis(contract_back(all_grads, masked_weight)) + skip_scale * grad_sum
    gate_grad, bias_grad = lax.psum(
        (jnp.sum(grad_sum * source_field, axis=(1, 2)), jnp.sum(grad_sum, axis=(1, 2))),
        ("slab", "mode"),
    )
    return (output, field_grad, spectral_grad, gate_grad, bias_grad)


def solution(mesh):
    in_specs = (
        P(("member", "chan"), "slab", "mode"),
        P(("member", "chan"), "slab", "mode"),
        P(("member", "chan"), None, "mode", None, "slab"),
        P(("member", "chan")),
        P(("member", "chan")),
        P("member", None),
        P("member"),
    )
    out_specs = (
        P(("member", "chan"), "slab", "mode"),
        P(("member", "chan"), "slab", "mode"),
        P(("member", "chan"), None, "mode", None, "slab"),
        P(("member", "chan")),
        P(("member", "chan")),
    )
    return jax.shard_map(local, mesh=mesh, in_specs=in_specs, out_specs=out_specs, check_vma=False)
```

profile of v0, /device:TPU:0, one launch (start us, length us, event | category | flops | bytes accessed | tf_op | source)
XLA Modules:
  0.0 418.1 jit_solution(5773580187036393755)
XLA Ops:
  7.8 20.7 %convolution_bitcast_fusion.1 = f32[32,64,256]{2,1,0:T(8,128)} fusion(f32[512,64,1]{0,1,2:T(8,128)S(1)} %reshape.294, f32[32,256,512]{2,1,0:T(8,128)} %param.7), kind=kOutput, calls=%fused_computation.35 | convolution fusion | flops 3221225472 | bytes 19005440 | tf_op jit(solution)/shard_map/chw,wk->ckh/dot_general | solution.py:129
  29.8 8.5 %broadcast_multiply_fusion = f32[32,64,16,2,16]{1,4,3,2,0:T(8,128)} fusion(f32[32,64,16,2,16]{1,4,3,2,0:T(8,128)} %param.9, f32[32,64]{1,0:T(8,128)S(1)} %compare_convert_fusion), kind=kLoop, calls=%fused_computation.17 | loop fusion | flops 1048576 | bytes 8396800 | tf_op jit(solution)/shard_map/mul | solution.py:152
  49.5 7.8 %slice_bitcast_fusion.1 = (f32[32,64,16,16]{1,3,2,0:T(8,128)}, f32[32,64,16,16]{1,3,2,0:T(8,128)}) fusion(f32[32,64,16,2,16]{1,4,3,2,0:T(8,128)} %broadcast_multiply_fusion), kind=kLoop, calls=%fused_computation.14 | loop fusion | bytes 8388608 | tf_op jit(solution)/shard_map/squeeze | solution.py:57
  57.3 13.4 %reduce-scatter.8.cloned.1.call-done = f32[512,2,16]{0,2,1:T(8,128)} async-done(((f32[512,2,64]{0,2,1:T(8,128)}), f32[512,2,16]{0,2,1:T(8,128)}) %reduce-scatter.8.cloned.1.call-update) | async-done | bytes 65552 | tf_op jit(solution)/shard_map/reduce_scatter | solution.py:132
  72.1 8.3 %fusion.18 = f32[16,16,1,64]{3,2,1,0:T(1,128)S(1)} fusion(f32[32,16,16,1]{0,3,2,1:T(1,128)S(1)} %copy.60, f32[32,64,16,16]{1,3,2,0:T(8,128)} %get-tuple-element.11), kind=kOutput, calls=%fused_computation.30 | convolution fusion | flops 6291456 | bytes 2195456 | tf_op jit(solution)/shard_map/iyx,ioyx->oyx/dot_general | solution.py:62
  80.5 8.6 %fusion.12 = f32[16,16,1,64]{3,2,1,0:T(1,128)S(1)} fusion(f32[32,16,16,1]{0,3,2,1:T(1,128)S(1)} %copy.60, f32[32,64,16,16]{1,3,2,0:T(8,128)} %get-tuple-element.12), kind=kOutput, calls=%fused_computation.24 | convolution fusion | flops 6291456 | bytes 2195456 | tf_op jit(solution)/shard_map/iyx,ioyx->oyx/dot_general | solution.py:59
  89.1 6.0 %fusion.20 = f32[16,16,1,64]{3,2,1,0:T(1,128)S(1)} fusion(f32[32,16,16,1]{0,3,2,1:T(1,128)S(1)} %copy.57, f32[32,64,16,16]{1,3,2,0:T(8,128)S(1)} %copy-done.3), kind=kOutput, calls=%fused_computation.32 | convolution fusion | flops 6291456 | bytes 2195456 | tf_op jit(solution)/shard_map/iyx,ioyx->oyx/dot_general | solution.py:59
  95.2 6.2 %fusion.10 = f32[16,16,1,64]{3,2,1,0:T(1,128)S(1)} fusion(f32[32,16,16,1]{0,3,2,1:T(1,128)S(1)} %copy.57, f32[32,64,16,16]{1,3,2,0:T(8,128)S(1)} %copy-done.2), kind=kOutput, calls=%fused_computation.22 | convolution fusion | flops 6291456 | bytes 2195456 | tf_op jit(solution)/shard_map/iyx,ioyx->oyx/dot_general | solution.py:62
  103.0 18.5 %reduce-scatter.10.cloned.1.call-done = f32[32,16,2,16]{1,0,3,2:T(8,128)} async-done(((f32[64,16,2,16]{1,0,3,2:T(8,128)}), f32[32,16,2,16]{1,0,3,2:T(8,128)}) %reduce-scatter.10.cloned.1.call-update) | async-done | bytes 65552 | tf_op jit(solution)/shard_map/reduce_scatter | solution.py:155
  122.7 38.4 %all_gather.15 = f32[32,16,2,64]{1,0,3,2:T(8,128)S(1)} all-gather(f32[32,16,2,16]{1,0,3,2:T(8,128)S(1)} %broadcast_multiply_fusion.2), channel_id=1, replica_groups=mesh['member'=2,'slab'=4,'chan'=2,'mode'=2] {'slab'}, dimensions={3}, use_global_device_ids=true | all-gather | bytes 327680 | tf_op jit(solution)/shard_map/all_gather | solution.py:138
  169.7 11.1 %all-gather.3.cloned.1.call-done = f32[32,64,256]{2,1,0:T(8,128)} async-done(((f32[32,32,256]{2,1,0:T(8,128)}), f32[32,64,256]{2,1,0:T(8,128)}) %all-gather.3.cloned.1.call-update) | async-done | bytes 2097168 | tf_op jit(solution)/shard_map/all_gather | solution.py:143
  180.9 36.1 %fusion.150 = (f32[32]{0:T(128)}, f32[32]{0:T(128)}, f32[32,256,512]{2,1,0:T(8,128)S(1)}, f32[32,256,512]{2,1,0:T(8,128)}) fusion(f32[32,256,512]{2,1,0:T(8,128)} %param.7, f32[32,256,512]{2,1,0:T(8,128)} %param.8, f32[32]{0:T(128)S(1)} %copy-done.9, f32[32]{0:T(128)S(1)} %copy-done.7, f32[32,64,256]{2,1,0:T(8,128)} %all-gather.3.cloned.1.call-done, ...), kind=kOutput, calls=%fused_computation.205 | convolution fusion | flops 3330277376 | bytes 69337600 | tf_op jit(solution)/shard_map/ckh,wk->chw/dot_general | solution.py:144
  216.9 6.2 %copy-done.4 = f32[32,256,512]{2,1,0:T(8,128)} copy-done((f32[32,256,512]{2,1,0:T(8,128)}, f32[32,256,512]{2,1,0:T(8,128)S(1)}, u32[]{:S(2)}) %copy-start.4) | copy-done | bytes 16777240
  223.1 17.8 %convolution_bitcast_fusion = f32[32,64,256]{2,1,0:T(8,128)} fusion(f32[512,64,1]{0,1,2:T(8,128)S(1)} %reshape.294, f32[32,256,512]{2,1,0:T(8,128)S(1)} %get-tuple-element.9), kind=kOutput, calls=%fused_computation.34 | convolution fusion | flops 3221225472 | bytes 19005440 | tf_op jit(solution)/shard_map/chw,wk->ckh/dot_general | solution.py:129
  241.0 10.9 %reduce-scatter.12.cloned.1.call-done = f32[32,32,256]{2,1,0:T(8,128)} async-done(((f32[32,64,256]{2,1,0:T(8,128)}), f32[32,32,256]{2,1,0:T(8,128)}) %reduce-scatter.12.cloned.1.call-update) | async-done | bytes 1048592 | tf_op jit(solution)/shard_map/reduce_scatter | solution.py:130
  260.1 21.4 %reduce-scatter.14.cloned.1.call-done = f32[512,2,16]{0,2,1:T(8,128)} async-done(((f32[512,2,64]{0,2,1:T(8,128)}), f32[512,2,16]{0,2,1:T(8,128)}) %reduce-scatter.14.cloned.1.call-update) | async-done | bytes 65552 | tf_op jit(solution)/shard_map/reduce_scatter | solution.py:132
  282.6 11.9 %all_gather.17 = f32[64,16,2,16]{1,0,3,2:T(8,128)S(1)} all-gather(f32[32,16,2,16]{1,0,3,2:T(8,128)S(1)} %broadcast_multiply_fusion.1), channel_id=1, replica_groups=mesh['member'=2,'slab'=4,'chan'=2,'mode'=2] {'chan'}, dimensions={0}, use_global_device_ids=true | all-gather | bytes 196608 | tf_op jit(solution)/shard_map/all_gather | solution.py:164
  295.0 11.1 %fusion.16 = f32[16,16,1,32]{3,2,1,0:T(1,128)S(1)} fusion(f32[64,16,16,1]{0,3,2,1:T(1,128)S(1)} %copy.64, f32[32,64,16,16]{1,3,2,0:T(8,128)} %get-tuple-element.11), kind=kOutput, calls=%fused_computation.28 | convolution fusion | flops 6291456 | bytes 2195456 | tf_op jit(solution)/shard_map/oyx,ioyx->iyx/dot_general | solution.py:73
  306.0 10.9 %fusion.6 = f32[16,16,1,32]{3,2,1,0:T(1,128)S(1)} fusion(f32[64,16,16,1]{0,3,2,1:T(1,128)S(1)} %copy.64, f32[32,64,16,16]{1,3,2,0:T(8,128)} %get-tuple-element.12), kind=kOutput, calls=%fused_computation.18 | convolution fusion | flops 6291456 | bytes 2195456 | tf_op jit(solution)/shard_map/oyx,ioyx->iyx/dot_general | solution.py:76
  317.1 11.1 %fusion.14 = f32[16,16,1,32]{3,2,1,0:T(1,128)S(1)} fusion(f32[64,16,16,1]{0,3,2,1:T(1,128)S(1)} %copy.66, f32[32,64,16,16]{1,3,2,0:T(8,128)} %get-tuple-element.11), kind=kOutput, calls=%fused_computation.26 | convolution fusion | flops 6291456 | bytes 2195456 | tf_op jit(solution)/shard_map/oyx,ioyx->iyx/dot_general | solution.py:76
  328.2 10.9 %fusion.8 = f32[16,16,1,32]{3,2,1,0:T(1,128)S(1)} fusion(f32[64,16,16,1]{0,3,2,1:T(1,128)S(1)} %copy.66, f32[32,64,16,16]{1,3,2,0:T(8,128)} %get-tuple-element.12), kind=kOutput, calls=%fused_computation.20 | convolution fusion | flops 6291456 | bytes 2195456 | tf_op jit(solution)/shard_map/oyx,ioyx->iyx/dot_general | solution.py:73
  339.3 19.9 %all_gather.18 = f32[32,16,2,64]{0,1,2,3:T(8,128)S(1)} all-gather(f32[32,16,2,16]{0,1,2,3:T(8,128)S(1)} %pad_maximum_fusion.5), channel_id=1, replica_groups=mesh['member'=2,'slab'=4,'chan'=2,'mode'=2] {'slab'}, dimensions={3}, use_global_device_ids=true | all-gather | bytes 327680 | tf_op jit(solution)/shard_map/all_gather | solution.py:138
  367.7 14.5 %all-reduce = (f32[32]{0:T(128)}, f32[32]{0:T(128)}) all-reduce(f32[32]{0:T(128)} %get-tuple-element.6, f32[32]{0:T(128)S(1)} %copy-done.10), channel_id=1, replica_groups=mesh['member'=2,'slab'=4,'chan'=2,'mode'=2] {'slab','mode'}, use_global_device_ids=true, to_apply=%region_6.7 | all-reduce | flops 64 | bytes 512 | tf_op jit(solution)/shard_map/psum | solution.py:167
  389.5 21.3 %multiply_add_fusion = f32[32,256,512]{2,1,0:T(8,128)} fusion(f32[32,256,512]{2,1,0:T(8,128)} %copy-done.4, f32[32,64,256]{2,1,0:T(8,128)} %all-gather.5.cloned.1.call-done, f32[512,64,1]{0,1,2:T(8,128)S(1)} %reshape.294, f32[32]{0:T(128)S(1)} %copy-done.7), kind=kOutput, calls=%fused_computation.9 | convolution fusion | flops 3229614080 | bytes 35782784 | tf_op jit(solution)/shard_map/ckh,wk->chw/dot_general | solution.py:144
  (106 shorter events, 51.3 us)
Async XLA Ops:
  7.2 21.7 %copy-start = (s32[64,2]{0,1:T(2,128)S(1)}, s32[64,2]{0,1:T(2,128)}, u32[]{:S(2)}) copy-start(s32[64,2]{0,1:T(2,128)} %param.12) | copy-start | bytes 1540
  7.2 33.9 %reduce-scatter.6.cloned.1.call-start = ((), (), s32[]{:S(2)}) async-start(), calls=%async_computation.5 | async-start | bytes 3145728 | tf_op jit(solution)/shard_map/reduce_scatter | solution.py:130
  7.8 21.3 %copy-start.8 = (s32[64]{0:T(128)S(1)}, s32[64]{0:T(128)}, u32[]{:S(2)}) copy-start(s32[64]{0:T(128)} %param.13) | copy-start | bytes 772
  28.5 42.1 %reduce-scatter.8.cloned.1.call-start = ((), (), s32[]{:S(2)}) async-start(), calls=%async_computation.6 | async-start | bytes 327680 | tf_op jit(solution)/shard_map/reduce_scatter | solution.py:132
  29.2 0.6 copy-start.5
  49.2 72.4 %reduce-scatter.10.cloned.1.call-start = ((), (), s32[]{:S(2)}) async-start(), calls=%async_computation.7 | async-start | bytes 1572864 | tf_op jit(solution)/shard_map/reduce_scatter | solution.py:155
  72.1 17.0 %copy-start.3 = (f32[32,64,16,16]{1,3,2,0:T(8,128)S(1)}, f32[32,64,16,16]{1,3,2,0:T(8,128)}, u32[]{:S(2)}) copy-start(f32[32,64,16,16]{1,3,2,0:T(8,128)} %get-tuple-element.11) | copy-start | bytes 6291460
  72.1 23.1 %copy-start.2 = (f32[32,64,16,16]{1,3,2,0:T(8,128)S(1)}, f32[32,64,16,16]{1,3,2,0:T(8,128)}, u32[]{:S(2)}) copy-start(f32[32,64,16,16]{1,3,2,0:T(8,128)} %get-tuple-element.12) | copy-start | bytes 6291460
  102.8 78.0 %all-gather.3.cloned.1.call-start = ((), (), s32[]{:S(2)}) async-start(), calls=%async_computation.8 | async-start | bytes 3145728 | tf_op jit(solution)/shard_map/all_gather | solution.py:143
  122.7 58.1 %copy-start.7 = (f32[32]{0:T(128)S(1)}, f32[32]{0:T(128)}, u32[]{:S(2)}) copy-start(f32[32]{0:T(128)} %param.10) | copy-start | bytes 388
  122.7 58.1 %copy-start.9 = (f32[32]{0:T(128)S(1)}, f32[32]{0:T(128)}, u32[]{:S(2)}) copy-start(f32[32]{0:T(128)} %param.11) | copy-start | bytes 388
  169.7 82.2 %reduce-scatter.12.cloned.1.call-start = ((), (), s32[]{:S(2)}) async-start(), calls=%async_computation.9 | async-start | bytes 3145728 | tf_op jit(solution)/shard_map/reduce_scatter | solution.py:130
  216.9 6.2 %copy-start.4 = (f32[32,256,512]{2,1,0:T(8,128)}, f32[32,256,512]{2,1,0:T(8,128)S(1)}, u32[]{:S(2)}) copy-start(f32[32,256,512]{2,1,0:T(8,128)S(1)} %get-tuple-element.9) | copy-start | bytes 50331652
  240.9 40.6 %reduce-scatter.14.cloned.1.call-start = ((), (), s32[]{:S(2)}) async-start(), calls=%async_computation.10 | async-start | bytes 327680 | tf_op jit(solution)/shard_map/reduce_scatter | solution.py:132
  260.0 129.5 %all-gather.5.cloned.1.call-start = ((), (), s32[]{:S(2)}) async-start(), calls=%async_computation.11 | async-start | bytes 3145728 | tf_op jit(solution)/shard_map/all_gather | solution.py:143
  339.1 28.6 %copy-start.10 = (f32[32]{0:T(128)S(1)}, f32[32]{0:T(128)}, u32[]{:S(2)}) copy-start(f32[32]{0:T(128)} %get-tuple-element.5) | copy-start | bytes 388
  364.7 20.2 %copy-start.6 = (f32[32,64]{1,0:T(8,128)S(1)}, f32[32,64]{1,0:T(8,128)}, u32[]{:S(2)}) copy-start(f32[32,64]{1,0:T(8,128)} %copy-done.5) | copy-start | bytes 24580
  389.5 21.3 %copy-start.1 = (s32[64,2]{0,1:T(2,128)S(1)}, s32[64,2]{0,1:T(2,128)}, u32[]{:S(2)}) copy-start(s32[64,2]{0,1:T(2,128)} %param.12) | copy-start | bytes 1540
Sparse Core Ops, SparseCore 0:
  28.6 12.3 reduce-scatter.5
  49.3 21.2 reduce-scatter.7
  103.0 18.5 reduce-scatter.9
  169.8 11.0 all-gather.2
  241.0 10.7 reduce-scatter.11
  260.1 21.2 reduce-scatter.13
  367.4 10.3 all-gather.4
where the time goes:
time: 424 us; the launch traced here: 418 us
  matrix products  188 us (44%)
  blocking collectives  84.8 us (20%)
  waiting for transfers between devices  78.2 us (18%)
  local copies, waits for them, and re-layouts  32.6 us (8%)
  other arithmetic  19.1 us (5%)
  between operations  15.1 us (4%)
    all_gather x2, blocking collectives, synthesis(): whole_modes = lax.all_gather(modes_in, 'slab', axis=3, tiled=True)  58.4 us
    dot_general x2, matrix products, synthesis(): return jnp.einsum('ckh,wk->chw', gathered, column_tab, precision=precise)  57.4 us
    dot_general x2, matrix products, spectrum(): jnp.einsum('chw,wk->ckh', values, column_tab, precision=precise)  38.5 us
    reduce_scatter x2, waiting for transfers between devices, spectrum(): lax.psum_scatter(row_forward(paired, row_cos, row_sin), 'slab', scatter_d...  34.8 us
    reduce_scatter x1, waiting for transfers between devices, local(): lax.psum_scatter(contract(spectra, masked_weight), 'chan', scatter_dimens...  18.5 us
    psum x1, blocking collectives, local(): lax.psum((jnp.sum(grad_sum * source_field, axis=(1, 2)), jnp.sum(grad_sum...  14.5 us
    reduce_scatter x2, waiting for transfers between devices, spectrum(): lax.psum_scatter(partial_cols, 'mode', scatter_dimension=1, tiled=True)  13.6 us
    all_gather x1, blocking collectives, local(): all_grads = lax.all_gather(grad_modes, 'chan', axis=0, tiled=True)  11.9 us
  transfers between devices with their start and end apart: 7, of which 6 were waited for; matrix products, arithmetic and copies ran while one was open for 6% of the time, Pallas kernels for 0%

commit v1 on v0

--- a/solution.py
+++ b/solution.py
@@ -1,9 +1,496 @@
+import functools
 import math
 
 import jax
 import jax.numpy as jnp
 from jax import lax
+from jax.experimental import pallas as pl
+from jax.experimental.pallas import tpu as pltpu
 from jax.sharding import PartitionSpec as P
+
+F32 = jnp.float32
+BF16 = jnp.bfloat16
+LANES = 128
+GELU_A = math.sqrt(2.0 / math.pi)
+GELU_B = GELU_A * 0.044715
+
+
+def split(x):
+    high = x.astype(BF16)
+    return high, (x - high.astype(F32)).astype(BF16)
+
+
+def split_table(x):
+    high = lax.reduce_precision(x, 8, 7)
+    return high.astype(BF16), (x - high).astype(BF16)
+
+
+def mm(a, b):
+    return jnp.dot(a, b, preferred_element_type=F32)
+
+
+def angles(cells, freqs, extent):
+    products = (cells[:, None] * freqs[None, :] % extent).astype(F32)
+    return products * (2.0 * math.pi / extent)
+
+
+def plan_tables(geo):
+    col_cell = geo.mode * geo.cols + jnp.arange(geo.cols, dtype=jnp.int32)
+    rel_mode = (geo.mode + jnp.arange(geo.modes, dtype=jnp.int32)) % geo.modes
+    freq = (rel_mode[:, None] * geo.freq + jnp.arange(geo.freq, dtype=jnp.int32)[None, :])
+    theta = angles(col_cell, freq.reshape(-1), geo.all_cols).reshape(geo.cols, geo.modes, geo.freq)
+    cos, sin = jnp.cos(theta), jnp.sin(theta)
+    first = jnp.stack([cos, -sin], axis=2).reshape(geo.cols, -1)
+    second = jnp.stack([-sin, -cos], axis=2).reshape(geo.cols, -1)
+    first_h, first_l = split_table(first)
+    second_h, second_l = split_table(second)
+    forward_cols = jnp.concatenate([first_h, first_l, second_h, second_l], axis=1)
+    inverse_cols = jnp.stack(
+        [
+            jnp.concatenate([high.T, high.T, low.T, low.T], axis=0)
+            for high, low in ((first_h, first_l), (second_h, second_l))
+        ]
+    )
+    row_cell = geo.slab * geo.rows + jnp.arange(geo.rows, dtype=jnp.int32)
+    rel_slab = (geo.slab + jnp.arange(geo.slabs, dtype=jnp.int32)) % geo.slabs
+    place = (rel_slab[:, None] * geo.kx + jnp.arange(geo.kx, dtype=jnp.int32)[None, :]).reshape(-1)
+    half = geo.slabs * geo.kx // 2
+    wave = jnp.where(place < half, place, place - 2 * half)
+    theta = angles(wave % geo.all_rows, row_cell, geo.all_rows)
+    forward_h, forward_l = split_table(jnp.concatenate([jnp.cos(theta), jnp.sin(theta)], axis=1))
+    forward_rows = jnp.concatenate([forward_h, forward_l], axis=0)
+    kept = jnp.arange(geo.fold // 2, dtype=jnp.int32)
+    theta = angles(row_cell, kept, geo.all_rows)
+    live = (kept <= half)[None, :]
+    inverse_h, inverse_l = split_table(
+        jnp.concatenate(
+            [jnp.where(live, jnp.cos(theta), 0.0), jnp.where(live, jnp.sin(theta), 0.0)], axis=1
+        )
+    )
+    rest = jnp.zeros((geo.rows, 256 - 3 * geo.fold), BF16)
+    inverse_rows = jnp.concatenate([inverse_h, inverse_h, inverse_l, rest], axis=1)
+    same = (jnp.abs(wave)[None, :] == kept[:, None]).astype(F32)
+    fold = jnp.concatenate([same, same * jnp.sign(wave).astype(F32)[None, :]], axis=0).astype(BF16)
+    return forward_cols, forward_rows, inverse_cols, inverse_rows, jnp.concatenate([fold, fold], axis=1)
+
+
+def lane_group(shape, width):
+    return lax.broadcasted_iota(jnp.int32, shape, 1) // width
+
+
+def emit_spectrum(parts, row_tab, own_ref, other_ref):
+    kx_all = row_tab.shape[0] // 2
+    doubled = []
+    for first in range(0, len(parts), 2):
+        pair = jnp.concatenate(
+            [jnp.concatenate([a[:, :LANES], a[:, LANES:]], axis=0) for a in parts[first : first + 2]],
+            axis=1,
+        )
+        high, low = split(pair)
+        both = mm(row_tab, high)
+        total = both[:kx_all] + both[kx_all:] + mm(row_tab[:kx_all], low)
+        for lane in (0, LANES):
+            one = total[:, lane : lane + LANES]
+            doubled.append(one + pltpu.roll(one, 64, 1))
+    turned = [pltpu.roll(s, 32, 1) for s in doubled]
+    group = lane_group(doubled[0].shape, 32)
+
+    def weave(arrays):
+        return jnp.where(
+            group == 0,
+            arrays[0],
+            jnp.where(group == 1, arrays[1], jnp.where(group == 2, arrays[2], arrays[3])),
+        )
+
+    own = weave([doubled[0], turned[1], doubled[2], turned[3]])
+    other = weave([turned[0], doubled[1], turned[2], doubled[3]])
+    slabs, _, kx, _ = own_ref.shape
+    for q in range(slabs):
+        own_ref[q, 0] = own[q * kx : (q + 1) * kx]
+        other_ref[q, 0] = other[q * kx : (q + 1) * kx]
+
+
+def forward_kernel(x_ref, col_ref, row_ref, own_ref, other_ref):
+    parts = []
+    for c in range(x_ref.shape[0]):
+        high, low = split(x_ref[c])
+        parts.append(mm(high, col_ref[...]) + mm(low, col_ref[...]))
+    emit_spectrum(parts, row_ref[...], own_ref, other_ref)
+
+
+def stack_modes(piece_refs, fold_ref, inv_col_ref, add=None):
+    slabs = len(piece_refs) // 2
+    halves = [
+        jnp.concatenate([r[0] for r in piece_refs[m * slabs : (m + 1) * slabs]], axis=0) for m in (0, 1)
+    ]
+    high, low = split(jnp.concatenate(halves, axis=1))
+    folded = mm(fold_ref[...], jnp.concatenate([high, low], axis=0))
+    fold = folded.shape[0]
+    group = lane_group((fold, LANES), 32)
+    a, b = folded[:, :LANES], folded[:, LANES:]
+    rows = []
+    for c in range(4):
+        a_at = [a if (t - c) % 4 == 0 else pltpu.roll(a, 32 * ((t - c) % 4), 1) for t in (0, 2)]
+        b_at = [b if (t - c) % 4 == 0 else pltpu.roll(b, 32 * ((t - c) % 4), 1) for t in (1, 3)]
+        one = jnp.where(
+            group == 0, a_at[0], jnp.where(group == 1, b_at[0], jnp.where(group == 2, a_at[1], b_at[1]))
+        )
+        top = one.astype(BF16).astype(F32)
+        rows.append(jnp.where(group < 2, top, one - top))
+    half = fold // 2
+    spread = []
+    for side in (0, 1):
+        lhs = jnp.concatenate([r[side * half : (side + 1) * half] for r in rows], axis=0).astype(BF16)
+        spread.append(mm(jnp.concatenate([lhs, lhs], axis=1), inv_col_ref[side]))
+    out = []
+    for c in range(4):
+        plus = spread[0][c * half : (c + 1) * half]
+        if add is not None:
+            plus = plus + jnp.where(lax.broadcasted_iota(jnp.int32, plus.shape, 0) == 0, add[c], 0.0)
+        both = jnp.concatenate([plus, spread[1][c * half : (c + 1) * half]], axis=0)
+        high, low = split(both)
+        rest = jnp.zeros((256 - 3 * fold, both.shape[1]), BF16)
+        out.append(jnp.concatenate([high, low, high, rest], axis=0))
+    return out
+
+
+CHUNK = 8
+
+
+def middle_kernel(skip_ref, bias_ref, *refs, pieces):
+    piece_refs = refs[:pieces]
+    x_ref, ct_ref, fold_ref, inv_col_ref, inv_row_ref, col_ref, row_ref = refs[pieces : pieces + 7]
+    out_ref, gs_ref, own_ref, other_ref, sums_ref, branch, high_ref, low_ref = refs[pieces + 7 :]
+    step = pl.program_id(0)
+    skips = [skip_ref[step * 4 + c] for c in range(4)]
+    stacked = stack_modes(piece_refs, fold_ref, inv_col_ref, [bias_ref[step * 4 + c] for c in range(4)])
+    rows, cols = x_ref.shape[1:]
+    parts = []
+    gate_rows, bias_rows = [], []
+    for c in range(4):
+        branch[c] = mm(inv_row_ref[...], stacked[c])
+        gate = jnp.zeros((CHUNK, cols), F32)
+        bias = jnp.zeros((CHUNK, cols), F32)
+        for r in range(0, rows, CHUNK):
+            x = x_ref[c, r : r + CHUNK]
+            v = branch[c, r : r + CHUNK] + skips[c] * x
+            q = v * v
+            t = jnp.tanh(v * (q * GELU_B + GELU_A))
+            s = 0.5 * t + 0.5
+            out = v * s
+            out_ref[c, r : r + CHUNK] = out
+            slope = s + out * (1.0 - s) * (q * (6.0 * GELU_B) + 2.0 * GELU_A)
+            grad = ct_ref[c, r : r + CHUNK] * slope
+            gs_ref[c, r : r + CHUNK] = grad
+            gate = gate + grad * x
+            bias = bias + grad
+            top = grad.astype(BF16)
+            high_ref[c, r : r + CHUNK] = top
+            low_ref[c, r : r + CHUNK] = (grad - top.astype(F32)).astype(BF16)
+        parts.append(mm(high_ref[c], col_ref[...]) + mm(low_ref[c], col_ref[...]))
+        for total, kept in ((gate, gate_rows), (bias, bias_rows)):
+            line = jnp.sum(total, axis=0, keepdims=True)
+            kept.append(sum(line[:, k : k + LANES] for k in range(0, cols, LANES)))
+    emit_spectrum(parts, row_ref[...], own_ref, other_ref)
+    sums_ref[0] = jnp.concatenate(gate_rows + bias_rows, axis=0)
+
+
+def last_kernel(skip_ref, *refs, pieces):
+    piece_refs = refs[:pieces]
+    gs_ref, fold_ref, inv_col_ref, inv_row_ref, out_ref = refs[pieces:]
+    step = pl.program_id(0)
+    stacked = stack_modes(piece_refs, fold_ref, inv_col_ref)
+    for c in range(4):
+        out_ref[c] = mm(inv_row_ref[...], stacked[c]) + skip_ref[step * 4 + c] * gs_ref[c]
+
+
+def limits_mask(place_ref, limit_ref, y, kx, kx_all, scale_cells, shape):
+    col = place_ref[0] + y
+    row = place_ref[1] + lax.broadcasted_iota(jnp.int32, shape, 0)
+    wide = jnp.broadcast_to(limit_ref[0:1, :], shape)
+    tall = jnp.broadcast_to(limit_ref[1:2, :], shape)
+    keep = (col < wide) & ((row < tall) | (kx_all - row < tall))
+    scale = jnp.where(col == 0, 1.0 / scale_cells, 2.0 / scale_cells).astype(F32)
+    return jnp.where(keep, scale, 0.0)
+
+
+def mix_kernel(place_ref, r0, r1, r2, r3, w_ref, limit_ref, width_ref, out_ref, spec_ref, acc, *, geo):
+    freq = geo.freq
+    block = w_ref.shape[1]
+    step = pl.program_id(0)
+
+    @pl.when(step == 0)
+    def _():
+        spec_ref[...] = r0[...] + r1[...] + r2[...] + r3[...]
+
+    groups = spec_ref.shape[0]
+    kx = geo.kx
+    outs = w_ref.shape[4]
+    for k in range(block):
+        y = step * block + k
+        shift = (LANES - y) % LANES
+        re = jnp.zeros((kx, outs), F32)
+        im = jnp.zeros((kx, outs), F32)
+        for g in range(groups):
+            line = pltpu.roll(spec_ref[g], shift, 1)
+            for c in range(4):
+                i = g * 4 + c
+                sr = jnp.broadcast_to(line[:, 32 * c : 32 * c + 1], (kx, outs))
+                si = jnp.broadcast_to(line[:, 32 * c + freq : 32 * c + freq + 1], (kx, outs))
+                reads = jnp.broadcast_to(place_ref[2] + i < width_ref[0:1, :], (kx, outs))
+                wr = jnp.where(reads, w_ref[i, k, 0], 0.0)
+                wi = jnp.where(reads, w_ref[i, k, 1], 0.0)
+                re = re + (sr * wr - si * wi)
+                im = im + (sr * wi + si * wr)
+        mask = limits_mask(place_ref, limit_ref, y, kx, geo.kx_all, geo.cells, (kx, outs))
+        out_ref[k, 0] = re * mask
+        out_ref[k, 1] = im * mask
+
+
+def back_kernel(place_ref, g_ref, w_ref, limit_ref, width_ref, out_ref, gm_ref, *, geo):
+    freq = geo.freq
+    block = w_ref.shape[1]
+    step = pl.program_id(0)
+    kx = geo.kx
+    outs = w_ref.shape[4]
+    groups = out_ref.shape[0]
+    lane = lax.broadcasted_iota(jnp.int32, (kx, LANES), 1)
+
+    @pl.when(step == 0)
+    def _():
+        out_ref[...] = jnp.zeros_like(out_ref)
+
+    for k in range(block):
+        y = step * block + k
+        mask = limits_mask(place_ref, limit_ref, y, kx, geo.kx_all, geo.cells, (kx, outs))
+        gr = g_ref[k, 0] * mask
+        gi = g_ref[k, 1] * mask
+        gm_ref[k, 0] = gr
+        gm_ref[k, 1] = gi
+        for g in range(groups):
+            line = out_ref[g]
+            for c in range(4):
+                i = g * 4 + c
+                reads = jnp.broadcast_to(place_ref[2] + i < width_ref[0:1, :], (kx, outs))
+                wr = jnp.where(reads, w_ref[i, k, 0], 0.0)
+                wi = jnp.where(reads, w_ref[i, k, 1], 0.0)
+                br = jnp.sum(gr * wr + gi * wi, axis=1, keepdims=True)
+                bi = jnp.sum(gi * wr - gr * wi, axis=1, keepdims=True)
+                line = jnp.where(lane == 32 * c + y, jnp.broadcast_to(br, (kx, LANES)), line)
+                line = jnp.where(lane == 32 * c + freq + y, jnp.broadcast_to(bi, (kx, LANES)), line)
+            out_ref[g] = line
+
+
+def outer_kernel(place_ref, spec_ref, gm_ref, width_ref, out_ref, *, geo):
+    freq = geo.freq
+    block = out_ref.shape[1]
+    step = pl.program_id(0)
+    kx = geo.kx
+    outs = out_ref.shape[4]
+    for k in range(block):
+        y = step * block + k
+        shift = (LANES - y) % LANES
+        gr = gm_ref[k, 0]
+        gi = gm_ref[k, 1]
+        for g in range(spec_ref.shape[0]):
+            line = pltpu.roll(spec_ref[g], shift, 1)
+            for c in range(4):
+                i = g * 4 + c
+                sr = jnp.broadcast_to(line[:, 32 * c : 32 * c + 1], (kx, outs))
+                si = jnp.broadcast_to(line[:, 32 * c + freq : 32 * c + freq + 1], (kx, outs))
+                reads = jnp.broadcast_to(place_ref[2] + i < width_ref[0:1, :], (kx, outs))
+                out_ref[i, k, 0] = jnp.where(reads, sr * gr + si * gi, 0.0)
+                out_ref[i, k, 1] = jnp.where(reads, sr * gi - si * gr, 0.0)
+
+
+class Geometry:
+    def __init__(self, field, weight):
+        self.channels, self.rows, self.cols = field.shape
+        self.outs, self.freq, self.kx = weight.shape[1], weight.shape[2], weight.shape[4]
+        self.slabs = lax.axis_size("slab")
+        self.modes = lax.axis_size("mode")
+        self.chans = lax.axis_size("chan")
+        self.slab = lax.axis_index("slab")
+        self.mode = lax.axis_index("mode")
+        self.chan = lax.axis_index("chan")
+        self.kx_all = self.kx * self.slabs
+        self.all_rows = self.rows * self.slabs
+        self.all_cols = self.cols * self.modes
+        self.cells = float(self.all_rows * self.all_cols)
+        self.fold = 16 * ((2 * (self.kx_all // 2 + 1) + 15) // 16)
+
+    def fits(self):
+        return (
+            self.modes == 2
+            and self.chans == 2
+            and self.slabs == 4
+            and self.freq == 16
+            and self.kx_all == 64
+            and self.kx % 8 == 0
+            and self.channels % 4 == 0
+            and self.rows % 16 == 0
+            and self.cols % LANES == 0
+            and 3 * self.fold <= 256
+        )
+
+
+def swap(x, name):
+    n = lax.axis_size(name)
+    return lax.ppermute(x, name, [(i, (i + 1) % n) for i in range(n)])
+
+
+def fetch(x, name, distance):
+    n = lax.axis_size(name)
+    return lax.ppermute(x, name, [((i + distance) % n, i) for i in range(n)])
+
+
+def send(x, name, distance):
+    n = lax.axis_size(name)
+    return lax.ppermute(x, name, [(i, (i + distance) % n) for i in range(n)])
+
+
+def whole(shape):
+    return pl.BlockSpec(shape, lambda *_: (0,) * len(shape))
+
+
+SMEM = pl.BlockSpec(memory_space=pltpu.SMEM)
+
+
+def params(limit):
+    return pltpu.CompilerParams(dimension_semantics=("arbitrary",), vmem_limit_bytes=limit)
+
+
+def spectrum_shapes(geo):
+    groups = geo.channels // 4
+    shape = (geo.slabs, groups, geo.kx, LANES)
+    block = (geo.slabs, 1, geo.kx, LANES)
+    return [jax.ShapeDtypeStruct(shape, F32)] * 2, [pl.BlockSpec(block, lambda s: (0, s, 0, 0))] * 2
+
+
+def reduce_spectrum(own, other, geo):
+    own = own + swap(other, "mode")
+    return [own[0]] + [send(own[d], "slab", d) for d in range(1, geo.slabs)]
+
+
+def gather_modes(mine, geo):
+    near = [mine] + [fetch(mine, "slab", d) for d in range(1, geo.slabs)]
+    return near + [swap(piece, "mode") for piece in near]
+
+
+def fast_local(
+    source_field, cotangent, spectral_weight, skip_gain, channel_bias, mode_limit, width_limit, geo
+):
+    channels, rows, cols = source_field.shape
+    groups = channels // 4
+    fwd_cols, fwd_rows, inv_cols, inv_rows, fold = plan_tables(geo)
+    weight = jnp.transpose(spectral_weight, (0, 2, 3, 4, 1))
+    field_spec = pl.BlockSpec((4, rows, cols), lambda s: (s, 0, 0))
+    piece_spec = pl.BlockSpec((1, geo.kx, LANES), lambda s: (s, 0, 0))
+    spec_shapes, spec_specs = spectrum_shapes(geo)
+    place = jnp.stack([geo.mode * geo.freq, geo.slab * geo.kx, geo.chan * channels]).astype(jnp.int32)
+    limits = jnp.transpose(mode_limit)
+    widths = width_limit[None, :]
+
+    own, other = pl.pallas_call(
+        forward_kernel,
+        grid=(groups,),
+        in_specs=[field_spec, whole(fwd_cols.shape), whole(fwd_rows.shape)],
+        out_specs=spec_specs,
+        out_shape=spec_shapes,
+        compiler_params=params(40 << 20),
+        name="forward",
+    )(source_field, fwd_cols, fwd_rows)
+    parts = reduce_spectrum(own, other, geo)
+
+    block = 4
+    steps = geo.freq // block
+    w_spec = pl.BlockSpec((channels, block, 2, geo.kx, geo.outs), lambda s: (0, s, 0, 0, 0))
+    g_spec = pl.BlockSpec((block, 2, geo.kx, geo.outs), lambda s: (s, 0, 0, 0))
+    piece = (groups, geo.kx, LANES)
+    piece_shape = jax.ShapeDtypeStruct(piece, F32)
+    modes_shape = jax.ShapeDtypeStruct((geo.freq, 2, geo.kx, geo.outs), F32)
+    mixed, spectra = pl.pallas_call(
+        functools.partial(mix_kernel, geo=geo),
+        grid=(steps,),
+        in_specs=[SMEM] + [whole(piece)] * 4 + [w_spec, whole(limits.shape), whole(widths.shape)],
+        out_specs=[g_spec, whole(piece)],
+        out_shape=[modes_shape, piece_shape],
+        scratch_shapes=[pltpu.VMEM((8, LANES), F32)],
+        compiler_params=params(40 << 20),
+        name="mix",
+    )(place, *parts, weight, limits, widths)
+    laid = mixed.reshape(geo.freq, 2, geo.kx, geo.chans, groups, 4)
+    laid = laid.transpose(3, 4, 2, 5, 1, 0).reshape((geo.chans,) + piece)
+    mine = lax.dynamic_index_in_dim(laid, geo.chan, 0, keepdims=False)
+    theirs = lax.dynamic_index_in_dim(laid, 1 - geo.chan, 0, keepdims=False)
+    pieces = gather_modes(mine + swap(theirs, "chan"), geo)
+
+    out_field = jax.ShapeDtypeStruct(source_field.shape, F32)
+    output, grad_sum, own, other, sums = pl.pallas_call(
+        functools.partial(middle_kernel, pieces=len(pieces)),
+        grid=(groups,),
+        in_specs=[SMEM, SMEM]
+        + [piece_spec] * len(pieces)
+        + [field_spec, field_spec]
+        + [whole(t.shape) for t in (fold, inv_cols, inv_rows, fwd_cols, fwd_rows)],
+        out_specs=[field_spec, field_spec] + spec_specs + [pl.BlockSpec((1, 8, LANES), lambda s: (s, 0, 0))],
+        out_shape=[out_field, out_field] + spec_shapes + [jax.ShapeDtypeStruct((groups, 8, LANES), F32)],
+        scratch_shapes=[
+            pltpu.VMEM((4, rows, cols), F32),
+            pltpu.VMEM((4, rows, cols), BF16),
+            pltpu.VMEM((4, rows, cols), BF16),
+        ],
+        compiler_params=params(56 << 20),
+        name="middle",
+    )(
+        skip_gain, channel_bias, *pieces, source_field, cotangent, fold, inv_cols, inv_rows, fwd_cols, fwd_rows
+    )
+    parts = reduce_spectrum(own, other, geo)
+    grads = parts[0] + parts[1] + parts[2] + parts[3]
+    peer = swap(grads, "chan")
+    first = geo.chan == 0
+    laid = jnp.stack([jnp.where(first, grads, peer), jnp.where(first, peer, grads)])
+    laid = laid.reshape(geo.chans, groups, geo.kx, 4, 2, geo.freq).transpose(5, 4, 2, 0, 1, 3)
+    laid = laid.reshape(geo.freq, 2, geo.kx, geo.outs)
+    back, grad_modes = pl.pallas_call(
+        functools.partial(back_kernel, geo=geo),
+        grid=(steps,),
+        in_specs=[SMEM, g_spec, w_spec, whole(limits.shape), whole(widths.shape)],
+        out_specs=[whole(piece), g_spec],
+        out_shape=[piece_shape, modes_shape],
+        compiler_params=params(40 << 20),
+        name="back",
+    )(place, laid, weight, limits, widths)
+    pieces = gather_modes(back, geo)
+    spectral_grad = pl.pallas_call(
+        functools.partial(outer_kernel, geo=geo),
+        grid=(steps,),
+        in_specs=[SMEM, whole(piece), g_spec, whole(widths.shape)],
+        out_specs=w_spec,
+        out_shape=jax.ShapeDtypeStruct(weight.shape, F32),
+        compiler_params=params(40 << 20),
+        cost_estimate=pl.CostEstimate(flops=200_000_000, bytes_accessed=8 << 20, transcendentals=0),
+        name="outer",
+    )(place, spectra, grad_modes, widths)
+    field_grad = pl.pallas_call(
+        functools.partial(last_kernel, pieces=len(pieces)),
+        grid=(groups,),
+        in_specs=[SMEM]
+        + [piece_spec] * len(pieces)
+        + [field_spec]
+        + [whole(t.shape) for t in (fold, inv_cols, inv_rows)],
+        out_specs=field_spec,
+        out_shape=out_field,
+        compiler_params=params(48 << 20),
+        name="last",
+    )(skip_gain, *pieces, grad_sum, fold, inv_cols, inv_rows)
+    sums = jnp.sum(sums, axis=2)
+    sums = sums + swap(sums, "mode")
+    sums = sums + send(sums, "slab", 1) + send(sums, "slab", 2) + send(sums, "slab", 3)
+    gate_grad = sums[:, :4].reshape(channels)
+    bias_grad = sums[:, 4:].reshape(channels)
+    return (output, field_grad, jnp.transpose(spectral_grad, (0, 4, 1, 2, 3)), gate_grad, bias_grad)
+
 
 precise = lax.Precision.HIGHEST
 
@@ -107,7 +594,7 @@
     return (in_index[:, None] < width_limit[None, :]).astype(jnp.float32)[:, :, None, None, None]
 
 
-def local(
+def plain_local(
     source_field, cotangent, spectral_weight, skip_gain, channel_bias, mode_limit, width_limit
 ):
     channels, row_count, col_count = source_field.shape
@@ -171,6 +658,13 @@
     return (output, field_grad, spectral_grad, gate_grad, bias_grad)
 
 
+def local(*args):
+    geo = Geometry(args[0], args[2])
+    if geo.fits():
+        return fast_local(*args, geo)
+    return plain_local(*args)
+
+
 def solution(mesh):
     in_specs = (
         P(("member", "chan"), "slab", "mode"),

time: 424 us -> 162 us (0.38); the launches traced: 418 us -> 162 us
  matrix products: 188 us -> 0 us
  Pallas kernels: 0 us -> 88.9 us
  blocking collectives: 84.8 us -> 0 us
  waiting for transfers between devices: 78.2 us -> 23.7 us
  starting transfers between devices: 0.75 us -> 27.5 us
  local copies, waits for them, and re-layouts: 32.6 us -> 14.4 us
  between operations: 15.1 us -> 1.12 us
  other arithmetic: 19.1 us -> 6.12 us
    dot_general x28 -> x0, matrix products: 188 us -> none  [the longest x2 57.4 us: synthesis(): return jnp.einsum('ckh,wk->chw', gathered, column_tab, precision=precise)]
    pallas_call x0 -> x6, Pallas kernels: none -> 88.9 us  [the longest x1 28.5 us: fast_local(): pl.pallas_call(functools.partial(middle_kernel, pieces=len(pieces)), grid...]
    all_gather x3 -> x0, blocking collectives: 70.3 us -> none  [the longest x2 58.4 us: synthesis(): whole_modes = lax.all_gather(modes_in, 'slab', axis=3, tiled=True)]
    reduce_scatter x5 -> x0, waiting for transfers between devices: 66.9 us -> none  [the longest x2 34.8 us: spectrum(): lax.psum_scatter(row_forward(paired, row_cos, row_sin), 'slab', scatter_d...]
    ppermute x0 -> x28, starting transfers between devices: none -> 27.5 us  [the longest x9 12.4 us: send(): return lax.ppermute(x, name, [(i, (i + distance) % n) for i in range(n)])]
    ppermute x0 -> x28, waiting for transfers between devices: none -> 23.7 us  [the longest x9 12.2 us: send(): return lax.ppermute(x, name, [(i, (i + distance) % n) for i in range(n)])]
    psum x1 -> x0, blocking collectives: 14.5 us -> none  [local(): lax.psum((jnp.sum(grad_sum * source_field, axis=(1, 2)), jnp.sum(grad_sum...]
    mul x5 -> x2, other arithmetic: 14.4 us -> 0.02 us  [the longest x1 0.01 us: plan_tables(): rel_slab[:, None] * geo.kx + jnp.arange(geo.kx, dtype=jnp.int32)[None, :]]
  transfers between devices with their start and end apart: 7 -> 28, of which waited for: 6 -> 12; matrix products, arithmetic and copies ran while one was open for 6% -> 5% of each run, Pallas kernels for 0% -> 11%
where the time goes in v1:
time: 162 us
  Pallas kernels  88.9 us (55%)
  starting transfers between devices  27.5 us (17%)
  waiting for transfers between devices  23.7 us (15%)
  local copies, waits for them, and re-layouts  14.4 us (9%)
  other arithmetic  6.12 us (4%)
    pallas_call x1, Pallas kernels, fast_local(): pl.pallas_call(functools.partial(middle_kernel, pieces=len(pieces)), grid...  28.5 us
    pallas_call x1, Pallas kernels, fast_local(): pl.pallas_call(functools.partial(last_kernel, pieces=len(pieces)), grid=(...  16.7 us
    pallas_call x1, Pallas kernels, fast_local(): pl.pallas_call(functools.partial(outer_kernel, geo=geo), grid=(steps,), i...  14.4 us
    pallas_call x1, Pallas kernels, fast_local(): pl.pallas_call(functools.partial(mix_kernel, geo=geo), grid=(steps,), in_...  13.2 us
    pallas_call x1, Pallas kernels, fast_local(): pl.pallas_call(forward_kernel, grid=(groups,), in_specs=[field_spec, whol...  12.5 us
    ppermute x9, starting transfers between devices, send(): return lax.ppermute(x, name, [(i, (i + distance) % n) for i in range(n)])  12.4 us
    ppermute x9, waiting for transfers between devices, send(): return lax.ppermute(x, name, [(i, (i + distance) % n) for i in range(n)])  12.2 us
    ppermute x6, starting transfers between devices, fetch(): return lax.ppermute(x, name, [((i + distance) % n, i) for i in range(n)])  10.2 us
  transfers between devices with their start and end apart: 28, of which 12 were waited for; matrix products, arithmetic and copies ran while one was open for 5% of the time, Pallas kernels for 11%

profile of v1, /device:TPU:0, one launch (start us, length us, event | category | flops | bytes accessed | tf_op | source)
XLA Modules:
  0.0 161.7 jit_solution(14537284295343040793)
XLA Ops:
  2.0 12.5 %forward.1 = (f32[4,8,16,128]{3,2,1,0:T(8,128)S(1)}, f32[4,8,16,128]{3,2,1,0:T(8,128)S(1)}) custom-call(f32[32,256,512]{2,1,0:T(8,128)} %refs_8_.1, bf16[512,256]{1,0:T(8,128)(2,1)S(1)} %copy.23.col_ref.refs_13_, bf16[128,512]{1,0:T(8,128)(2,1)S(1)} %pad_maximum_fusion.6.row_ref.refs_14_), custom_call_target="tpu_custom_call" | custom-call | tf_op jit(solution)/shard_map/forward/pallas_call | solution.py:394
  16.7 4.7 %collective-permute-start.3 = (f32[8,16,128]{2,1,0:T(8,128)S(1)}, f32[8,16,128]{2,1,0:T(8,128)S(1)}, u32[]{:S(2)}, u32[]{:S(2)}) collective-permute-start(f32[8,16,128]{2,1,0:T(8,128)S(1)} %get-tuple-element.32), channel_id=1, source_target_pairs={{0,12},{4,0},{8,4},{12,8},{1,13},{5,1},{9,5},{13,9},{2,14},{6,2},{... | collective-permute-start | bytes 196616 | tf_op jit(solution)/shard_map/ppermute | solution.py:349
  22.5 1.4 collective-permute-done.3.r3
  23.9 4.6 %collective-permute-done.2.r2 = f32[8,16,128]{2,1,0:T(8,128)S(1)} collective-permute-done((f32[8,16,128]{2,1,0:T(8,128)S(1)}, f32[8,16,128]{2,1,0:T(8,128)S(1)}, u32[]{:S(2)}, u32[]{:S(2)}) %collective-permute-start.2) | collective-permute-done | bytes 65568 | tf_op jit(solution)/shard_map/ppermute | solution.py:349
  28.5 3.4 %copy-done = f32[32,64,16,2,16]{1,4,3,2,0:T(8,128)S(1)} copy-done((f32[32,64,16,2,16]{1,4,3,2,0:T(8,128)S(1)}, f32[32,64,16,2,16]{1,4,3,2,0:T(8,128)}, u32[]{:S(2)}) %copy-start) | copy-done | bytes 4194328
  31.9 13.2 %mix.1 = (f32[16,2,16,64]{3,2,1,0:T(8,128)S(1)}, f32[8,16,128]{2,1,0:T(8,128)S(1)}) custom-call(s32[3]{0:T(128)S(1)} %pad_add_fusion.place_ref, f32[8,16,128]{2,1,0:T(8,128)S(1)} %get-tuple-element.35.r0, f32[8,16,128]{2,1,0:T(8,128)S(1)} %collective-permute-done.1.r1, f32[8,16,128]{2,1,0:T(8,128)S(1)} %collective-permute-done.2.r2, ...), custom_call_target="tpu_custom_call" | custom-call | tf_op jit(solution)/shard_map/mix/pallas_call | solution.py:412
  47.7 1.6 collective-permute-start.4
  49.3 2.7 %collective-permute-done.4 = f32[8,16,128]{2,1,0:T(8,128)S(1)} collective-permute-done((f32[8,16,128]{2,1,0:T(8,128)S(1)}, f32[8,16,128]{2,1,0:T(8,128)S(1)}, u32[]{:S(2)}, u32[]{:S(2)}) %collective-permute-start.4) | collective-permute-done | bytes 65568 | tf_op jit(solution)/shard_map/ppermute | solution.py:339
  52.3 2.2 %collective-permute-start.6 = (f32[8,16,128]{2,1,0:T(8,128)S(1)}, f32[8,16,128]{2,1,0:T(8,128)S(1)}, u32[]{:S(2)}, u32[]{:S(2)}) collective-permute-start(f32[8,16,128]{2,1,0:T(8,128)S(1)} %bitcast_add_fusion.refs_0_), channel_id=1, source_target_pairs={{8,0},{12,4},{0,8},{4,12},{9,1},{13,5},{1,9},{5,13},{10,2},{14,6},... | collective-permute-start | bytes 196616 | tf_op jit(solution)/shard_map/ppermute | solution.py:344
  54.6 2.3 %collective-permute-start.5 = (f32[8,16,128]{2,1,0:T(8,128)S(1)}, f32[8,16,128]{2,1,0:T(8,128)S(1)}, u32[]{:S(2)}, u32[]{:S(2)}) collective-permute-start(f32[8,16,128]{2,1,0:T(8,128)S(1)} %bitcast_add_fusion.refs_0_), channel_id=1, source_target_pairs={{4,0},{8,4},{12,8},{0,12},{5,1},{9,5},{13,9},{1,13},{6,2},{10,6},{... | collective-permute-start | bytes 196616 | tf_op jit(solution)/shard_map/ppermute | solution.py:344
  62.1 28.5 %middle.1 = (f32[32,256,512]{2,1,0:T(8,128)}, f32[32,256,512]{2,1,0:T(8,128)}, f32[4,8,16,128]{3,2,1,0:T(8,128)}, f32[4,8,16,128]{3,2,1,0:T(8,128)}, f32[8,8,128]{2,1,0:T(8,128)}) custom-call(f32[32]{0:T(128)} %skip_ref.3, f32[32]{0:T(128)} %bias_ref.1, f32[8,16,128]{2,1,0:T(8,128)} %copy-done.10, f32[8,16,128]{2,1,0:T(8,128)} %copy-done.13, ...), custom_call_target="tpu_custom_call" | custom-call | tf_op jit(solution)/shard_map/middle/pallas_call | solution.py:429
  90.8 1.6 collective-permute-done.12
  94.4 2.9 %collective-permute-start.15 = (f32[8,16,128]{2,1,0:T(8,128)S(1)}, f32[8,16,128]{2,1,0:T(8,128)S(1)}, u32[]{:S(2)}, u32[]{:S(2)}) collective-permute-start(f32[8,16,128]{2,1,0:T(8,128)S(1)} %get-tuple-element.28), channel_id=1, source_target_pairs={{0,12},{4,0},{8,4},{12,8},{1,13},{5,1},{9,5},{13,9},{2,14},{6,2},{... | collective-permute-start | bytes 196616 | tf_op jit(solution)/shard_map/ppermute | solution.py:349
  97.3 2.7 %collective-permute-done.13 = f32[8,16,128]{2,1,0:T(8,128)S(1)} collective-permute-done((f32[8,16,128]{2,1,0:T(8,128)S(1)}, f32[8,16,128]{2,1,0:T(8,128)S(1)}, u32[]{:S(2)}, u32[]{:S(2)}) %collective-permute-start.13) | collective-permute-done | bytes 65568 | tf_op jit(solution)/shard_map/ppermute | solution.py:349
  100.1 3.5 %collective-permute-done.14 = f32[8,16,128]{2,1,0:T(8,128)S(1)} collective-permute-done((f32[8,16,128]{2,1,0:T(8,128)S(1)}, f32[8,16,128]{2,1,0:T(8,128)S(1)}, u32[]{:S(2)}, u32[]{:S(2)}) %collective-permute-start.14) | collective-permute-done | bytes 65568 | tf_op jit(solution)/shard_map/ppermute | solution.py:349
  103.6 1.6 collective-permute-start.16
  107.1 2.3 %collective-permute-start.27 = (f32[8,8]{1,0:T(8,128)S(1)}, f32[8,8]{1,0:T(8,128)S(1)}, u32[]{:S(2)}, u32[]{:S(2)}) collective-permute-start(f32[8,8]{1,0:T(8,128)S(1)} %add.232), channel_id=1, source_target_pairs={{0,12},{4,0},{8,4},{12,8},{1,13},{5,1},{9,5},{13,9},{2,14},{6,2},{... | collective-permute-start | bytes 776 | tf_op jit(solution)/shard_map/ppermute | solution.py:349
  112.5 3.4 %copy-done.1 = f32[32,64,16,2,16]{1,4,3,2,0:T(8,128)S(1)} copy-done((f32[32,64,16,2,16]{1,4,3,2,0:T(8,128)S(1)}, f32[32,64,16,2,16]{1,4,3,2,0:T(8,128)}, u32[]{:S(2)}) %copy-start.1) | copy-done | bytes 4194328
  115.8 3.6 %back.1 = (f32[8,16,128]{2,1,0:T(8,128)S(1)}, f32[16,2,16,64]{3,2,1,0:T(8,128)S(1)}) custom-call(s32[3]{0:T(128)S(1)} %pad_add_fusion.place_ref, f32[16,2,16,64]{3,2,1,0:T(8,128)S(1)} %copy.29.g_ref, f32[32,16,2,16,64]{4,3,2,1,0:T(8,128)S(1)} %bitcast.54, s32[2,64]{1,0:T(2,128)S(1)} %bitcast.59, s32[1,64]{1,0:T(1,128)S(1)} %bitcast.56), custom_call_target="tpu_custom_call" | custom-call | tf_op jit(solution)/shard_map/back/pallas_call | solution.py:455
  119.4 3.0 %collective-permute-start.19 = (f32[8,16,128]{2,1,0:T(8,128)S(1)}, f32[8,16,128]{2,1,0:T(8,128)S(1)}, u32[]{:S(2)}, u32[]{:S(2)}) collective-permute-start(f32[8,16,128]{2,1,0:T(8,128)S(1)} %get-tuple-element.22.refs_0_), channel_id=1, source_target_pairs={{12,0},{0,4},{4,8},{8,12},{13,1},{1,5},{5,9},{9,13},{14,2},{2,6},{... | collective-permute-start | bytes 196616 | tf_op jit(solution)/shard_map/ppermute | solution.py:344
  123.3 1.5 collective-permute-start.17
  126.2 2.5 %collective-permute-done.18.refs_2_ = f32[8,16,128]{2,1,0:T(8,128)S(1)} collective-permute-done((f32[8,16,128]{2,1,0:T(8,128)S(1)}, f32[8,16,128]{2,1,0:T(8,128)S(1)}, u32[]{:S(2)}, u32[]{:S(2)}) %collective-permute-start.18) | collective-permute-done | bytes 65568 | tf_op jit(solution)/shard_map/ppermute | solution.py:344
  130.5 14.4 %outer.1 = f32[32,16,2,16,64]{4,3,2,1,0:T(8,128)} custom-call(s32[3]{0:T(128)S(1)} %pad_add_fusion.place_ref, f32[8,16,128]{2,1,0:T(8,128)S(1)} %get-tuple-element.24.spec_ref, f32[16,2,16,64]{3,2,1,0:T(8,128)S(1)} %get-tuple-element.25.gm_ref, s32[1,64]{1,0:T(1,128)S(1)} %bitcast.57), custom_call_target="tpu_custom_call" | custom-call | flops 200000000 | bytes 8388608 | tf_op jit(solution)/shard_map/outer/pallas_call | solution.py:465
  145.0 16.7 %last.1 = f32[32,256,512]{2,1,0:T(8,128)} custom-call(f32[32]{0:T(128)S(1)} %copy-done.9, f32[8,16,128]{2,1,0:T(8,128)S(1)} %get-tuple-element.22.refs_0_, f32[8,16,128]{2,1,0:T(8,128)S(1)} %collective-permute-done.17.refs_1_, f32[8,16,128]{2,1,0:T(8,128)S(1)} %collective-permute-done.18.refs_2_, f32[8,16,128]{2,1,0:T(8,128)S(1)} %collective-permute-done.19.refs_3_, ...), custom_call_target="tpu_custom_call" | custom-call | tf_op jit(solution)/shard_map/last/pallas_call | solution.py:475
  (126 shorter events, 23.9 us)
Async XLA Ops:
  14.5 2.2 %collective-permute-start = (f32[4,8,16,128]{3,2,1,0:T(8,128)S(1)}, f32[4,8,16,128]{3,2,1,0:T(8,128)S(1)}, u32[]{:S(2)}, u32[]{:S(2)}) collective-permute-start(f32[4,8,16,128]{3,2,1,0:T(8,128)S(1)} %get-tuple-element.17), channel_id=1, source_target_pairs={{0,1},{1,0},{2,3},{3,2},{4,5},{5,4},{6,7},{7,6},{8,9},{9,8},{10,11... | collective-permute-start | bytes 786440 | tf_op jit(solution)/shard_map/ppermute | solution.py:339
  16.7 7.2 %collective-permute-start.3 = (f32[8,16,128]{2,1,0:T(8,128)S(1)}, f32[8,16,128]{2,1,0:T(8,128)S(1)}, u32[]{:S(2)}, u32[]{:S(2)}) collective-permute-start(f32[8,16,128]{2,1,0:T(8,128)S(1)} %get-tuple-element.32), channel_id=1, source_target_pairs={{0,12},{4,0},{8,4},{12,8},{1,13},{5,1},{9,5},{13,9},{2,14},{6,2},{... | collective-permute-start | bytes 196616 | tf_op jit(solution)/shard_map/ppermute | solution.py:349
  21.4 7.1 %collective-permute-start.2 = (f32[8,16,128]{2,1,0:T(8,128)S(1)}, f32[8,16,128]{2,1,0:T(8,128)S(1)}, u32[]{:S(2)}, u32[]{:S(2)}) collective-permute-start(f32[8,16,128]{2,1,0:T(8,128)S(1)} %get-tuple-element.33), channel_id=1, source_target_pairs={{0,8},{4,12},{8,0},{12,4},{1,9},{5,13},{9,1},{13,5},{2,10},{6,14},... | collective-permute-start | bytes 196616 | tf_op jit(solution)/shard_map/ppermute | solution.py:349
  21.4 7.1 %collective-permute-start.1 = (f32[8,16,128]{2,1,0:T(8,128)S(1)}, f32[8,16,128]{2,1,0:T(8,128)S(1)}, u32[]{:S(2)}, u32[]{:S(2)}) collective-permute-start(f32[8,16,128]{2,1,0:T(8,128)S(1)} %get-tuple-element.34), channel_id=1, source_target_pairs={{0,4},{4,8},{8,12},{12,0},{1,5},{5,9},{9,13},{13,1},{2,6},{6,10},{... | collective-permute-start | bytes 196616 | tf_op jit(solution)/shard_map/ppermute | solution.py:349
  47.7 4.3 %collective-permute-start.4 = (f32[8,16,128]{2,1,0:T(8,128)S(1)}, f32[8,16,128]{2,1,0:T(8,128)S(1)}, u32[]{:S(2)}, u32[]{:S(2)}) collective-permute-start(f32[8,16,128]{2,1,0:T(8,128)S(1)} %dynamic-slice_bitcast_fusion), channel_id=1, source_target_pairs={{0,2},{2,0},{1,3},{3,1},{4,6},{6,4},{5,7},{7,5},{8,10},{10,8},{9,1... | collective-permute-start | bytes 196616 | tf_op jit(solution)/shard_map/ppermute | solution.py:339
  52.1 6.2 %collective-permute-start.7 = (f32[8,16,128]{2,1,0:T(8,128)S(1)}, f32[8,16,128]{2,1,0:T(8,128)S(1)}, u32[]{:S(2)}, u32[]{:S(2)}) collective-permute-start(f32[8,16,128]{2,1,0:T(8,128)S(1)} %bitcast_add_fusion.refs_0_), channel_id=1, source_target_pairs={{12,0},{0,4},{4,8},{8,12},{13,1},{1,5},{5,9},{9,13},{14,2},{2,6},{... | collective-permute-start | bytes 196616 | tf_op jit(solution)/shard_map/ppermute | solution.py:344
  52.3 7.3 %collective-permute-start.6 = (f32[8,16,128]{2,1,0:T(8,128)S(1)}, f32[8,16,128]{2,1,0:T(8,128)S(1)}, u32[]{:S(2)}, u32[]{:S(2)}) collective-permute-start(f32[8,16,128]{2,1,0:T(8,128)S(1)} %bitcast_add_fusion.refs_0_), channel_id=1, source_target_pairs={{8,0},{12,4},{0,8},{4,12},{9,1},{13,5},{1,9},{5,13},{10,2},{14,6},... | collective-permute-start | bytes 196616 | tf_op jit(solution)/shard_map/ppermute | solution.py:344
  54.6 5.0 %collective-permute-start.5 = (f32[8,16,128]{2,1,0:T(8,128)S(1)}, f32[8,16,128]{2,1,0:T(8,128)S(1)}, u32[]{:S(2)}, u32[]{:S(2)}) collective-permute-start(f32[8,16,128]{2,1,0:T(8,128)S(1)} %bitcast_add_fusion.refs_0_), channel_id=1, source_target_pairs={{4,0},{8,4},{12,8},{0,12},{5,1},{9,5},{13,9},{1,13},{6,2},{10,6},{... | collective-permute-start | bytes 196616 | tf_op jit(solution)/shard_map/ppermute | solution.py:344
  57.7 3.1 %collective-permute-start.8 = (f32[8,16,128]{2,1,0:T(8,128)S(1)}, f32[8,16,128]{2,1,0:T(8,128)S(1)}, u32[]{:S(2)}, u32[]{:S(2)}) collective-permute-start(f32[8,16,128]{2,1,0:T(8,128)S(1)} %bitcast_add_fusion.refs_0_), channel_id=1, source_target_pairs={{0,1},{1,0},{2,3},{3,2},{4,5},{5,4},{6,7},{7,6},{8,9},{9,8},{10,11... | collective-permute-start | bytes 196616 | tf_op jit(solution)/shard_map/ppermute | solution.py:339
  58.3 2.5 %collective-permute-start.11 = (f32[8,16,128]{2,1,0:T(8,128)S(1)}, f32[8,16,128]{2,1,0:T(8,128)S(1)}, u32[]{:S(2)}, u32[]{:S(2)}) collective-permute-start(f32[8,16,128]{2,1,0:T(8,128)S(1)} %collective-permute-done.7.refs_3_), channel_id=1, source_target_pairs={{0,1},{1,0},{2,3},{3,2},{4,5},{5,4},{6,7},{7,6},{8,9},{9,8},{10,11... | collective-permute-start | bytes 196616 | tf_op jit(solution)/shard_map/ppermute | solution.py:339
  93.5 6.6 %collective-permute-start.13 = (f32[8,16,128]{2,1,0:T(8,128)S(1)}, f32[8,16,128]{2,1,0:T(8,128)S(1)}, u32[]{:S(2)}, u32[]{:S(2)}) collective-permute-start(f32[8,16,128]{2,1,0:T(8,128)S(1)} %get-tuple-element.27), channel_id=1, source_target_pairs={{0,4},{4,8},{8,12},{12,0},{1,5},{5,9},{9,13},{13,1},{2,6},{6,10},{... | collective-permute-start | bytes 196616 | tf_op jit(solution)/shard_map/ppermute | solution.py:349
  94.4 5.7 %collective-permute-start.15 = (f32[8,16,128]{2,1,0:T(8,128)S(1)}, f32[8,16,128]{2,1,0:T(8,128)S(1)}, u32[]{:S(2)}, u32[]{:S(2)}) collective-permute-start(f32[8,16,128]{2,1,0:T(8,128)S(1)} %get-tuple-element.28), channel_id=1, source_target_pairs={{0,12},{4,0},{8,4},{12,8},{1,13},{5,1},{9,5},{13,9},{2,14},{6,2},{... | collective-permute-start | bytes 196616 | tf_op jit(solution)/shard_map/ppermute | solution.py:349
  97.3 6.2 %collective-permute-start.14 = (f32[8,16,128]{2,1,0:T(8,128)S(1)}, f32[8,16,128]{2,1,0:T(8,128)S(1)}, u32[]{:S(2)}, u32[]{:S(2)}) collective-permute-start(f32[8,16,128]{2,1,0:T(8,128)S(1)} %get-tuple-element.29), channel_id=1, source_target_pairs={{0,8},{4,12},{8,0},{12,4},{1,9},{5,13},{9,1},{13,5},{2,10},{6,14},... | collective-permute-start | bytes 196616 | tf_op jit(solution)/shard_map/ppermute | solution.py:349
  103.6 6.4 %collective-permute-start.16 = (f32[8,16,128]{2,1,0:T(8,128)S(1)}, f32[8,16,128]{2,1,0:T(8,128)S(1)}, u32[]{:S(2)}, u32[]{:S(2)}) collective-permute-start(f32[8,16,128]{2,1,0:T(8,128)S(1)} %fusion.18), channel_id=1, source_target_pairs={{0,2},{2,0},{1,3},{3,1},{4,6},{6,4},{5,7},{7,5},{8,10},{10,8},{9,1... | collective-permute-start | bytes 196616 | tf_op jit(solution)/shard_map/ppermute | solution.py:339
  107.1 16.2 %collective-permute-start.27 = (f32[8,8]{1,0:T(8,128)S(1)}, f32[8,8]{1,0:T(8,128)S(1)}, u32[]{:S(2)}, u32[]{:S(2)}) collective-permute-start(f32[8,8]{1,0:T(8,128)S(1)} %add.232), channel_id=1, source_target_pairs={{0,12},{4,0},{8,4},{12,8},{1,13},{5,1},{9,5},{13,9},{2,14},{6,2},{... | collective-permute-start | bytes 776 | tf_op jit(solution)/shard_map/ppermute | solution.py:349
  109.4 15.4 %collective-permute-start.26 = (f32[8,8]{1,0:T(8,128)S(1)}, f32[8,8]{1,0:T(8,128)S(1)}, u32[]{:S(2)}, u32[]{:S(2)}) collective-permute-start(f32[8,8]{1,0:T(8,128)S(1)} %add.232), channel_id=1, source_target_pairs={{0,8},{4,12},{8,0},{12,4},{1,9},{5,13},{9,1},{13,5},{2,10},{6,14},... | collective-permute-start | bytes 776 | tf_op jit(solution)/shard_map/ppermute | solution.py:349
  109.4 15.4 %collective-permute-start.25 = (f32[8,8]{1,0:T(8,128)S(1)}, f32[8,8]{1,0:T(8,128)S(1)}, u32[]{:S(2)}, u32[]{:S(2)}) collective-permute-start(f32[8,8]{1,0:T(8,128)S(1)} %add.232), channel_id=1, source_target_pairs={{0,4},{4,8},{8,12},{12,0},{1,5},{5,9},{9,13},{13,1},{2,6},{6,10},{... | collective-permute-start | bytes 776 | tf_op jit(solution)/shard_map/ppermute | solution.py:349
  119.4 6.8 %collective-permute-start.19 = (f32[8,16,128]{2,1,0:T(8,128)S(1)}, f32[8,16,128]{2,1,0:T(8,128)S(1)}, u32[]{:S(2)}, u32[]{:S(2)}) collective-permute-start(f32[8,16,128]{2,1,0:T(8,128)S(1)} %get-tuple-element.22.refs_0_), channel_id=1, source_target_pairs={{12,0},{0,4},{4,8},{8,12},{13,1},{1,5},{5,9},{9,13},{14,2},{2,6},{... | collective-permute-start | bytes 196616 | tf_op jit(solution)/shard_map/ppermute | solution.py:344
  122.4 6.3 %collective-permute-start.18 = (f32[8,16,128]{2,1,0:T(8,128)S(1)}, f32[8,16,128]{2,1,0:T(8,128)S(1)}, u32[]{:S(2)}, u32[]{:S(2)}) collective-permute-start(f32[8,16,128]{2,1,0:T(8,128)S(1)} %get-tuple-element.22.refs_0_), channel_id=1, source_target_pairs={{8,0},{12,4},{0,8},{4,12},{9,1},{13,5},{1,9},{5,13},{10,2},{14,6},... | collective-permute-start | bytes 196616 | tf_op jit(solution)/shard_map/ppermute | solution.py:344
  123.3 5.4 %collective-permute-start.17 = (f32[8,16,128]{2,1,0:T(8,128)S(1)}, f32[8,16,128]{2,1,0:T(8,128)S(1)}, u32[]{:S(2)}, u32[]{:S(2)}) collective-permute-start(f32[8,16,128]{2,1,0:T(8,128)S(1)} %get-tuple-element.22.refs_0_), channel_id=1, source_target_pairs={{4,0},{8,4},{12,8},{0,12},{5,1},{9,5},{13,9},{1,13},{6,2},{10,6},{... | collective-permute-start | bytes 196616 | tf_op jit(solution)/shard_map/ppermute | solution.py:344
  124.8 20.1 %collective-permute-start.20 = (f32[8,16,128]{2,1,0:T(8,128)S(1)}, f32[8,16,128]{2,1,0:T(8,128)S(1)}, u32[]{:S(2)}, u32[]{:S(2)}) collective-permute-start(f32[8,16,128]{2,1,0:T(8,128)S(1)} %get-tuple-element.22.refs_0_), channel_id=1, source_target_pairs={{0,1},{1,0},{2,3},{3,2},{4,5},{5,4},{6,7},{7,6},{8,9},{9,8},{10,11... | collective-permute-start | bytes 196616 | tf_op jit(solution)/shard_map/ppermute | solution.py:339
  126.2 18.7 %collective-permute-start.23 = (f32[8,16,128]{2,1,0:T(8,128)S(1)}, f32[8,16,128]{2,1,0:T(8,128)S(1)}, u32[]{:S(2)}, u32[]{:S(2)}) collective-permute-start(f32[8,16,128]{2,1,0:T(8,128)S(1)} %collective-permute-done.19.refs_3_), channel_id=1, source_target_pairs={{0,1},{1,0},{2,3},{3,2},{4,5},{5,4},{6,7},{7,6},{8,9},{9,8},{10,11... | collective-permute-start | bytes 196616 | tf_op jit(solution)/shard_map/ppermute | solution.py:339
  128.7 16.2 %collective-permute-start.22 = (f32[8,16,128]{2,1,0:T(8,128)S(1)}, f32[8,16,128]{2,1,0:T(8,128)S(1)}, u32[]{:S(2)}, u32[]{:S(2)}) collective-permute-start(f32[8,16,128]{2,1,0:T(8,128)S(1)} %collective-permute-done.18.refs_2_), channel_id=1, source_target_pairs={{0,1},{1,0},{2,3},{3,2},{4,5},{5,4},{6,7},{7,6},{8,9},{9,8},{10,11... | collective-permute-start | bytes 196616 | tf_op jit(solution)/shard_map/ppermute | solution.py:339
  128.7 16.2 %collective-permute-start.21 = (f32[8,16,128]{2,1,0:T(8,128)S(1)}, f32[8,16,128]{2,1,0:T(8,128)S(1)}, u32[]{:S(2)}, u32[]{:S(2)}) collective-permute-start(f32[8,16,128]{2,1,0:T(8,128)S(1)} %collective-permute-done.17.refs_1_), channel_id=1, source_target_pairs={{0,1},{1,0},{2,3},{3,2},{4,5},{5,4},{6,7},{7,6},{8,9},{9,8},{10,11... | collective-permute-start | bytes 196616 | tf_op jit(solution)/shard_map/ppermute | solution.py:339
  (22 other events, 396.1 us)

commit v2 on v1

--- a/solution.py
+++ b/solution.py
@@ -78,102 +78,181 @@
     return lax.broadcasted_iota(jnp.int32, shape, 1) // width
 
 
-def emit_spectrum(parts, row_tab, own_ref, other_ref):
+def pair_spectra(first, second, row_tab):
     kx_all = row_tab.shape[0] // 2
-    doubled = []
-    for first in range(0, len(parts), 2):
-        pair = jnp.concatenate(
-            [jnp.concatenate([a[:, :LANES], a[:, LANES:]], axis=0) for a in parts[first : first + 2]],
-            axis=1,
-        )
-        high, low = split(pair)
-        both = mm(row_tab, high)
-        total = both[:kx_all] + both[kx_all:] + mm(row_tab[:kx_all], low)
-        for lane in (0, LANES):
-            one = total[:, lane : lane + LANES]
-            doubled.append(one + pltpu.roll(one, 64, 1))
+    pair = jnp.concatenate(
+        [jnp.concatenate([a[:, :LANES], a[:, LANES:]], axis=0) for a in (first, second)], axis=1
+    )
+    high, low = split(pair)
+    both = mm(row_tab, high)
+    total = both[:kx_all] + both[kx_all:] + mm(row_tab[:kx_all], low)
+    halves = [total[:, lane : lane + LANES] for lane in (0, LANES)]
+    return [one + pltpu.roll(one, 64, 1) for one in halves]
+
+
+def write_spectra(doubled, own_ref, other_ref, group):
     turned = [pltpu.roll(s, 32, 1) for s in doubled]
-    group = lane_group(doubled[0].shape, 32)
+    place = lane_group(doubled[0].shape, 32)
 
     def weave(arrays):
         return jnp.where(
-            group == 0,
+            place == 0,
             arrays[0],
-            jnp.where(group == 1, arrays[1], jnp.where(group == 2, arrays[2], arrays[3])),
+            jnp.where(place == 1, arrays[1], jnp.where(place == 2, arrays[2], arrays[3])),
         )
 
     own = weave([doubled[0], turned[1], doubled[2], turned[3]])
     other = weave([turned[0], doubled[1], turned[2], doubled[3]])
     slabs, _, kx, _ = own_ref.shape
     for q in range(slabs):
-        own_ref[q, 0] = own[q * kx : (q + 1) * kx]
-        other_ref[q, 0] = other[q * kx : (q + 1) * kx]
-
-
-def forward_kernel(x_ref, col_ref, row_ref, own_ref, other_ref):
+        own_ref[q, group] = own[q * kx : (q + 1) * kx]
+        other_ref[q, group] = other[q * kx : (q + 1) * kx]
+
+
+def forward_kernel(place_ref, x_ref, col_ref, row_ref, own_ref, other_ref, keep_ref, sems):
+    del place_ref
+    step = pl.program_id(0)
+
+    def fetching(at):
+        four = pl.ds(at * 4, 4)
+        return pltpu.make_async_copy(x_ref.at[four], keep_ref.at[four], sems.at[at])
+
+    @pl.when(step == 0)
+    def _():
+        for at in range(sems.shape[0]):
+            fetching(at).start()
+
+    fetching(step).wait()
     parts = []
-    for c in range(x_ref.shape[0]):
-        high, low = split(x_ref[c])
+    for c in range(4):
+        high, low = split(keep_ref[step * 4 + c])
         parts.append(mm(high, col_ref[...]) + mm(low, col_ref[...]))
-    emit_spectrum(parts, row_ref[...], own_ref, other_ref)
-
-
-def stack_modes(piece_refs, fold_ref, inv_col_ref, add=None):
+    doubled = pair_spectra(*parts[:2], row_ref[...]) + pair_spectra(*parts[2:], row_ref[...])
+    write_spectra(doubled, own_ref, other_ref, step)
+
+
+def fold_modes(piece_refs, step, fold_ref):
     slabs = len(piece_refs) // 2
     halves = [
-        jnp.concatenate([r[0] for r in piece_refs[m * slabs : (m + 1) * slabs]], axis=0) for m in (0, 1)
+        jnp.concatenate([r[step] for r in piece_refs[m * slabs : (m + 1) * slabs]], axis=0) for m in (0, 1)
     ]
     high, low = split(jnp.concatenate(halves, axis=1))
-    folded = mm(fold_ref[...], jnp.concatenate([high, low], axis=0))
-    fold = folded.shape[0]
-    group = lane_group((fold, LANES), 32)
+    return mm(fold_ref[...], jnp.concatenate([high, low], axis=0))
+
+
+def line_up(folded, c):
+    group = lane_group((folded.shape[0], LANES), 32)
     a, b = folded[:, :LANES], folded[:, LANES:]
-    rows = []
-    for c in range(4):
-        a_at = [a if (t - c) % 4 == 0 else pltpu.roll(a, 32 * ((t - c) % 4), 1) for t in (0, 2)]
-        b_at = [b if (t - c) % 4 == 0 else pltpu.roll(b, 32 * ((t - c) % 4), 1) for t in (1, 3)]
-        one = jnp.where(
-            group == 0, a_at[0], jnp.where(group == 1, b_at[0], jnp.where(group == 2, a_at[1], b_at[1]))
-        )
-        top = one.astype(BF16).astype(F32)
-        rows.append(jnp.where(group < 2, top, one - top))
-    half = fold // 2
-    spread = []
-    for side in (0, 1):
-        lhs = jnp.concatenate([r[side * half : (side + 1) * half] for r in rows], axis=0).astype(BF16)
-        spread.append(mm(jnp.concatenate([lhs, lhs], axis=1), inv_col_ref[side]))
-    out = []
-    for c in range(4):
-        plus = spread[0][c * half : (c + 1) * half]
-        if add is not None:
-            plus = plus + jnp.where(lax.broadcasted_iota(jnp.int32, plus.shape, 0) == 0, add[c], 0.0)
-        both = jnp.concatenate([plus, spread[1][c * half : (c + 1) * half]], axis=0)
-        high, low = split(both)
-        rest = jnp.zeros((256 - 3 * fold, both.shape[1]), BF16)
-        out.append(jnp.concatenate([high, low, high, rest], axis=0))
-    return out
-
-
-CHUNK = 8
+    a_at = [a if (t - c) % 4 == 0 else pltpu.roll(a, 32 * ((t - c) % 4), 1) for t in (0, 2)]
+    b_at = [b if (t - c) % 4 == 0 else pltpu.roll(b, 32 * ((t - c) % 4), 1) for t in (1, 3)]
+    one = jnp.where(
+        group == 0, a_at[0], jnp.where(group == 1, b_at[0], jnp.where(group == 2, a_at[1], b_at[1]))
+    )
+    top = one.astype(BF16).astype(F32)
+    return jnp.where(group < 2, top, one - top)
+
+
+def spread_columns(rows, side, inv_col_ref):
+    half = rows[0].shape[0] // 2
+    lhs = jnp.concatenate([r[side * half : (side + 1) * half] for r in rows], axis=0).astype(BF16)
+    return mm(jnp.concatenate([lhs, lhs], axis=1), inv_col_ref[side])
+
+
+def stack_operand(plus, minus, add=None):
+    if add is not None:
+        plus = plus + jnp.where(lax.broadcasted_iota(jnp.int32, plus.shape, 0) == 0, add, 0.0)
+    high, low = split(jnp.concatenate([plus, minus], axis=0))
+    rest = jnp.zeros((256 - 3 * high.shape[0], high.shape[1]), BF16)
+    return jnp.concatenate([high, low, high, rest], axis=0)
+
+
+def stack_modes(piece_refs, step, fold_ref, inv_col_ref):
+    folded = fold_modes(piece_refs, step, fold_ref)
+    half = folded.shape[0] // 2
+    rows = [line_up(folded, c) for c in range(4)]
+    sides = [spread_columns(rows, side, inv_col_ref) for side in (0, 1)]
+    return [stack_operand(*(s[c * half : (c + 1) * half] for s in sides)) for c in range(4)]
+
+
+CHUNK = 16
 
 
 def middle_kernel(skip_ref, bias_ref, *refs, pieces):
     piece_refs = refs[:pieces]
     x_ref, ct_ref, fold_ref, inv_col_ref, inv_row_ref, col_ref, row_ref = refs[pieces : pieces + 7]
-    out_ref, gs_ref, own_ref, other_ref, sums_ref, branch, high_ref, low_ref = refs[pieces + 7 :]
+    out_ref, gs_ref, own_ref, other_ref, ready, wide_ref, branch, high_ref, low_ref, part_ref = refs[pieces + 7 :]
     step = pl.program_id(0)
-    skips = [skip_ref[step * 4 + c] for c in range(4)]
-    stacked = stack_modes(piece_refs, fold_ref, inv_col_ref, [bias_ref[step * 4 + c] for c in range(4)])
+    last = pl.num_programs(0) - 1
     rows, cols = x_ref.shape[1:]
-    parts = []
-    gate_rows, bias_rows = [], []
+    sums = own_ref.shape[1] - 1
+    half = fold_ref.shape[0] // 2
+
+    def preparing(at):
+        held = {}
+
+        def begin():
+            held["folded"] = fold_modes(piece_refs, at, fold_ref)
+
+        def line(c):
+            held[c] = line_up(held["folded"], c)
+
+        def spread(side):
+            wide_ref[side] = spread_columns([held[c] for c in range(4)], side, inv_col_ref)
+
+        def stack(c):
+            plus, minus = (wide_ref[side, c * half : (c + 1) * half] for side in (0, 1))
+            ready[c] = stack_operand(plus, minus, bias_ref[at * 4 + c])
+
+        early = [begin] + [functools.partial(line, c) for c in range(4)]
+        early += [functools.partial(spread, side) for side in (0, 1)]
+        return early, [functools.partial(stack, c) for c in range(4)]
+
+    def emitting(at):
+        held = {}
+
+        def pair(k):
+            held[k] = pair_spectra(part_ref[2 * k], part_ref[2 * k + 1], row_ref[...])
+
+        def write():
+            write_spectra(held[0] + held[1], own_ref, other_ref, at)
+
+        return [functools.partial(pair, 0), functools.partial(pair, 1), write]
+
+    @pl.when(step == 0)
+    def _():
+        early, late = preparing(0)
+        for task in early + late:
+            task()
+        part_ref[...] = jnp.zeros_like(part_ref)
+        own_ref[0, sums] = jnp.zeros(own_ref.shape[2:], F32)
+
+    early, late = preparing(jnp.minimum(step + 1, last))
+    emits = emitting(jnp.maximum(step - 1, 0))
+    chunks = rows // CHUNK
+    plan = {(0, 1): emits[0], (0, 5): emits[1], (0, 10): emits[2]}
+    for k, task in enumerate(early):
+        plan[(1 + k // 4, 2 + 3 * (k % 4))] = task
+    for k, task in enumerate(late):
+        plan[(3, 2 + 3 * k)] = task
+    tile = own_ref[0, sums]
+    row = lax.broadcasted_iota(jnp.int32, tile.shape, 0)
+    lane = lax.broadcasted_iota(jnp.int32, tile.shape, 1)
+    branch[0] = mm(inv_row_ref[...], ready[0])
     for c in range(4):
-        branch[c] = mm(inv_row_ref[...], stacked[c])
+        channel = step * 4 + c
+        skip = skip_ref[channel]
         gate = jnp.zeros((CHUNK, cols), F32)
         bias = jnp.zeros((CHUNK, cols), F32)
-        for r in range(0, rows, CHUNK):
-            x = x_ref[c, r : r + CHUNK]
-            v = branch[c, r : r + CHUNK] + skips[c] * x
+        for k in range(chunks):
+            r = k * CHUNK
+            if (c, k) in plan:
+                plan[(c, k)]()
+            if k == 0 and c < 3:
+                branch[c + 1] = mm(inv_row_ref[...], ready[c + 1])
+            if k == 1 and c > 0:
+                part_ref[c - 1] = mm(high_ref[c - 1], col_ref[...]) + mm(low_ref[c - 1], col_ref[...])
+            x = x_ref[channel, r : r + CHUNK]
+            v = branch[c, r : r + CHUNK] + skip * x
             q = v * v
             t = jnp.tanh(v * (q * GELU_B + GELU_A))
             s = 0.5 * t + 0.5
@@ -181,27 +260,38 @@
             out_ref[c, r : r + CHUNK] = out
             slope = s + out * (1.0 - s) * (q * (6.0 * GELU_B) + 2.0 * GELU_A)
             grad = ct_ref[c, r : r + CHUNK] * slope
-            gs_ref[c, r : r + CHUNK] = grad
+            gs_ref[channel, r : r + CHUNK] = grad
             gate = gate + grad * x
             bias = bias + grad
             top = grad.astype(BF16)
             high_ref[c, r : r + CHUNK] = top
             low_ref[c, r : r + CHUNK] = (grad - top.astype(F32)).astype(BF16)
-        parts.append(mm(high_ref[c], col_ref[...]) + mm(low_ref[c], col_ref[...]))
-        for total, kept in ((gate, gate_rows), (bias, bias_rows)):
+        for at, total in ((0, gate), (1, bias)):
             line = jnp.sum(total, axis=0, keepdims=True)
-            kept.append(sum(line[:, k : k + LANES] for k in range(0, cols, LANES)))
-    emit_spectrum(parts, row_ref[...], own_ref, other_ref)
-    sums_ref[0] = jnp.concatenate(gate_rows + bias_rows, axis=0)
+            value = jnp.sum(sum(line[:, k : k + LANES] for k in range(0, cols, LANES)), axis=1, keepdims=True)
+            tile = jnp.where((row == at) & (lane == channel), jnp.broadcast_to(value, tile.shape), tile)
+    part_ref[3] = mm(high_ref[3], col_ref[...]) + mm(low_ref[3], col_ref[...])
+    own_ref[0, sums] = tile
+
+    @pl.when(step == last)
+    def _():
+        for task in emitting(last):
+            task()
+        for q in range(own_ref.shape[0]):
+            own_ref[q, sums] = tile
+            other_ref[q, sums] = tile
 
 
 def last_kernel(skip_ref, *refs, pieces):
     piece_refs = refs[:pieces]
     gs_ref, fold_ref, inv_col_ref, inv_row_ref, out_ref = refs[pieces:]
     step = pl.program_id(0)
-    stacked = stack_modes(piece_refs, fold_ref, inv_col_ref)
-    for c in range(4):
-        out_ref[c] = mm(inv_row_ref[...], stacked[c]) + skip_ref[step * 4 + c] * gs_ref[c]
+    block = out_ref.shape[0]
+    for first in range(0, block, 4):
+        stacked = stack_modes(piece_refs, step * (block // 4) + first // 4, fold_ref, inv_col_ref)
+        for c in range(4):
+            channel = step * block + first + c
+            out_ref[first + c] = mm(inv_row_ref[...], stacked[c]) + skip_ref[channel] * gs_ref[channel]
 
 
 def limits_mask(place_ref, limit_ref, y, kx, kx_all, scale_cells, shape):
@@ -214,66 +304,103 @@
     return jnp.where(keep, scale, 0.0)
 
 
-def mix_kernel(place_ref, r0, r1, r2, r3, w_ref, limit_ref, width_ref, out_ref, spec_ref, acc, *, geo):
-    freq = geo.freq
-    block = w_ref.shape[1]
+def pick_table(geo):
+    source = lax.broadcasted_iota(jnp.int32, (2 * LANES, 8 * LANES), 0) % LANES
+    target = lax.broadcasted_iota(jnp.int32, (2 * LANES, 8 * LANES), 1) // LANES
+    return (source == target * geo.freq).astype(BF16)
+
+
+def spread_lanes(spec, y, pick_ref):
+    turned = pltpu.roll(spec, LANES - y, 1)
+    high, low = split(turned)
+    lhs = jnp.concatenate([high, low], axis=1)
+    return [mm(lhs, pick_ref[:, 2 * LANES * c : 2 * LANES * (c + 1)]) for c in range(4)]
+
+
+def mix_kernel(
+    place_ref, r0, r1, r2, r3, w_ref, limit_ref, width_ref, pick_ref, held_ref, mine_ref, theirs_ref, spec_ref, made, turn, laid, *, geo, block
+):
+    freq, kx, outs = geo.freq, geo.kx, geo.outs
+    groups = spec_ref.shape[0]
     step = pl.program_id(0)
+    half = groups * kx
 
     @pl.when(step == 0)
     def _():
         spec_ref[...] = r0[...] + r1[...] + r2[...] + r3[...]
 
-    groups = spec_ref.shape[0]
-    kx = geo.kx
-    outs = w_ref.shape[4]
+    widths = width_ref[0:1, :] - place_ref[2]
+    spec = spec_ref[...].reshape(half, LANES)
     for k in range(block):
         y = step * block + k
-        shift = (LANES - y) % LANES
         re = jnp.zeros((kx, outs), F32)
         im = jnp.zeros((kx, outs), F32)
-        for g in range(groups):
-            line = pltpu.roll(spec_ref[g], shift, 1)
-            for c in range(4):
+        spread = spread_lanes(spec, y, pick_ref)
+        for c in range(4):
+            for g in range(groups):
                 i = g * 4 + c
-                sr = jnp.broadcast_to(line[:, 32 * c : 32 * c + 1], (kx, outs))
-                si = jnp.broadcast_to(line[:, 32 * c + freq : 32 * c + freq + 1], (kx, outs))
-                reads = jnp.broadcast_to(place_ref[2] + i < width_ref[0:1, :], (kx, outs))
-                wr = jnp.where(reads, w_ref[i, k, 0], 0.0)
-                wi = jnp.where(reads, w_ref[i, k, 1], 0.0)
+                sr = spread[c][g * kx : (g + 1) * kx, :outs]
+                si = spread[c][g * kx : (g + 1) * kx, LANES : LANES + outs]
+                reads = jnp.broadcast_to(widths > i, (kx, outs))
+                wr = jnp.where(reads, w_ref[i, y, 0], 0.0)
+                wi = jnp.where(reads, w_ref[i, y, 1], 0.0)
                 re = re + (sr * wr - si * wi)
                 im = im + (sr * wi + si * wr)
         mask = limits_mask(place_ref, limit_ref, y, kx, geo.kx_all, geo.cells, (kx, outs))
-        out_ref[k, 0] = re * mask
-        out_ref[k, 1] = im * mask
-
-
-def back_kernel(place_ref, g_ref, w_ref, limit_ref, width_ref, out_ref, gm_ref, *, geo):
-    freq = geo.freq
-    block = w_ref.shape[1]
+        made[pl.ds(y * kx, kx), :outs] = re * mask
+        made[pl.ds((freq + y) * kx, kx), :outs] = im * mask
+
+    @pl.when(step == pl.num_programs(0) - 1)
+    def _():
+        place = lane_group((2 * groups, LANES), 2 * freq)
+        for j in range(kx):
+            slot = j % turn.shape[0]
+            turn[slot, :, : 2 * freq] = made[pl.ds(j, 2 * freq, stride=kx), :].T
+            line = jnp.zeros((2 * groups, LANES), F32)
+            for c in range(4):
+                one = turn[slot, pl.ds(c, 2 * groups, stride=4), :]
+                line = jnp.where(place == c, pltpu.roll(one, 2 * freq * c, 1) if c else one, line)
+            laid[pl.ds(j, 2 * groups, stride=kx), :] = line
+        mine_ref[...] = laid[pl.ds(place_ref[3] * half, half), :].reshape(mine_ref.shape)
+        theirs_ref[...] = laid[pl.ds((1 - place_ref[3]) * half, half), :].reshape(mine_ref.shape)
+
+
+def back_kernel(place_ref, own_ref, peer_ref, w_ref, limit_ref, width_ref, held_ref, out_ref, gm_ref, made, turn, laid, *, geo, block):
+    freq, kx, outs = geo.freq, geo.kx, geo.outs
     step = pl.program_id(0)
-    kx = geo.kx
-    outs = w_ref.shape[4]
     groups = out_ref.shape[0]
+    half = groups * kx
     lane = lax.broadcasted_iota(jnp.int32, (kx, LANES), 1)
 
     @pl.when(step == 0)
     def _():
+        laid[pl.ds(place_ref[3] * half, half), :] = own_ref[...].reshape(half, LANES)
+        laid[pl.ds((1 - place_ref[3]) * half, half), :] = peer_ref[...].reshape(half, LANES)
+        for j in range(kx):
+            slot = j % turn.shape[0]
+            line = laid[pl.ds(j, 2 * groups, stride=kx), :]
+            for c in range(4):
+                turn[slot, pl.ds(c, 2 * groups, stride=4), :] = (
+                    pltpu.roll(line, LANES - 2 * freq * c, 1) if c else line
+                )
+            made[pl.ds(j, 2 * freq, stride=kx), :] = turn[slot].T[: 2 * freq]
         out_ref[...] = jnp.zeros_like(out_ref)
 
+    widths = width_ref[0:1, :] - place_ref[2]
     for k in range(block):
         y = step * block + k
         mask = limits_mask(place_ref, limit_ref, y, kx, geo.kx_all, geo.cells, (kx, outs))
-        gr = g_ref[k, 0] * mask
-        gi = g_ref[k, 1] * mask
+        gr = made[pl.ds(y * kx, kx), :outs] * mask
+        gi = made[pl.ds((freq + y) * kx, kx), :outs] * mask
         gm_ref[k, 0] = gr
         gm_ref[k, 1] = gi
         for g in range(groups):
             line = out_ref[g]
             for c in range(4):
                 i = g * 4 + c
-                reads = jnp.broadcast_to(place_ref[2] + i < width_ref[0:1, :], (kx, outs))
-                wr = jnp.where(reads, w_ref[i, k, 0], 0.0)
-                wi = jnp.where(reads, w_ref[i, k, 1], 0.0)
+                reads = jnp.broadcast_to(widths > i, (kx, outs))
+                wr = jnp.where(reads, w_ref[i, y, 0], 0.0)
+                wi = jnp.where(reads, w_ref[i, y, 1], 0.0)
                 br = jnp.sum(gr * wr + gi * wi, axis=1, keepdims=True)
                 bi = jnp.sum(gi * wr - gr * wi, axis=1, keepdims=True)
                 line = jnp.where(lane == 32 * c + y, jnp.broadcast_to(br, (kx, LANES)), line)
@@ -281,26 +408,46 @@
             out_ref[g] = line
 
 
-def outer_kernel(place_ref, spec_ref, gm_ref, width_ref, out_ref, *, geo):
-    freq = geo.freq
+def outer_kernel(place_ref, spec_ref, gm_ref, width_ref, pick_ref, held_ref, out_ref, *, geo):
+    kx, outs = geo.kx, geo.outs
     block = out_ref.shape[1]
     step = pl.program_id(0)
-    kx = geo.kx
-    outs = out_ref.shape[4]
+    groups = spec_ref.shape[0]
+    widths = width_ref[0:1, :] - place_ref[2]
+    spec = spec_ref[...].reshape(groups * kx, LANES)
     for k in range(block):
-        y = step * block + k
-        shift = (LANES - y) % LANES
         gr = gm_ref[k, 0]
         gi = gm_ref[k, 1]
-        for g in range(spec_ref.shape[0]):
-            line = pltpu.roll(spec_ref[g], shift, 1)
-            for c in range(4):
+        spread = spread_lanes(spec, step * block + k, pick_ref)
+        for c in range(4):
+            for g in range(groups):
                 i = g * 4 + c
-                sr = jnp.broadcast_to(line[:, 32 * c : 32 * c + 1], (kx, outs))
-                si = jnp.broadcast_to(line[:, 32 * c + freq : 32 * c + freq + 1], (kx, outs))
-                reads = jnp.broadcast_to(place_ref[2] + i < width_ref[0:1, :], (kx, outs))
+                sr = spread[c][g * kx : (g + 1) * kx, :outs]
+                si = spread[c][g * kx : (g + 1) * kx, LANES : LANES + outs]
+                reads = jnp.broadcast_to(widths > i, (kx, outs))
                 out_ref[i, k, 0] = jnp.where(reads, sr * gr + si * gi, 0.0)
                 out_ref[i, k, 1] = jnp.where(reads, sr * gi - si * gr, 0.0)
+
+
+def prefetch_kernel(after_ref, held_ref, source_ref, target_ref, sem):
+    del after_ref, held_ref
+    copy = pltpu.make_async_copy(source_ref, target_ref, sem)
+    copy.start()
+    copy.wait()
+
+
+def prefetch(x, after, held):
+    anywhere = pl.BlockSpec(memory_space=pl.ANY)
+    return pl.pallas_call(
+        prefetch_kernel,
+        in_specs=[anywhere] * 3,
+        out_specs=anywhere,
+        out_shape=pltpu.VMEM(x.shape, x.dtype),
+        scratch_shapes=[pltpu.SemaphoreType.DMA],
+        compiler_params=pltpu.CompilerParams(vmem_limit_bytes=1 << 20),
+        cost_estimate=cost(4),
+        name="prefetch",
+    )(after, resident(held), streamed(x))
 
 
 class Geometry:
@@ -327,7 +474,7 @@
             and self.freq == 16
             and self.kx_all == 64
             and self.kx % 8 == 0
-            and self.channels % 4 == 0
+            and self.channels % 8 == 0
             and self.rows % 16 == 0
             and self.cols % LANES == 0
             and 3 * self.fold <= 256
@@ -356,15 +503,31 @@
 SMEM = pl.BlockSpec(memory_space=pltpu.SMEM)
 
 
+FORWARD_LIMIT = 16 << 20
+MIX_LIMIT = 16 << 20
+MIDDLE_LIMIT = 24 << 20
+LAST_LIMIT = 24 << 20
+LAST_GROUPS = 2
+
+
+def cost(micros):
+    return pl.CostEstimate(flops=int(micros * 1.0e8), bytes_accessed=1 << 20, transcendentals=0)
+
+
 def params(limit):
     return pltpu.CompilerParams(dimension_semantics=("arbitrary",), vmem_limit_bytes=limit)
 
 
-def spectrum_shapes(geo):
-    groups = geo.channels // 4
-    shape = (geo.slabs, groups, geo.kx, LANES)
-    block = (geo.slabs, 1, geo.kx, LANES)
-    return [jax.ShapeDtypeStruct(shape, F32)] * 2, [pl.BlockSpec(block, lambda s: (0, s, 0, 0))] * 2
+VMEM = pl.BlockSpec(memory_space=pltpu.VMEM)
+ANYWHERE = pl.BlockSpec(memory_space=pl.ANY)
+
+
+def streamed(x):
+    return pltpu.with_memory_space_constraint(x, pltpu.HBM)
+
+
+def resident(x):
+    return pltpu.with_memory_space_constraint(x, pltpu.VMEM)
 
 
 def reduce_spectrum(own, other, geo):
@@ -372,8 +535,11 @@
     return [own[0]] + [send(own[d], "slab", d) for d in range(1, geo.slabs)]
 
 
-def gather_modes(mine, geo):
-    near = [mine] + [fetch(mine, "slab", d) for d in range(1, geo.slabs)]
+def gather_slabs(mine, geo):
+    return [mine] + [fetch(mine, "slab", d) for d in range(1, geo.slabs)]
+
+
+def gather_halves(near):
     return near + [swap(piece, "mode") for piece in near]
 
 
@@ -383,113 +549,122 @@
     channels, rows, cols = source_field.shape
     groups = channels // 4
     fwd_cols, fwd_rows, inv_cols, inv_rows, fold = plan_tables(geo)
+    pick = pick_table(geo)
     weight = jnp.transpose(spectral_weight, (0, 2, 3, 4, 1))
+    field = source_field.shape
     field_spec = pl.BlockSpec((4, rows, cols), lambda s: (s, 0, 0))
-    piece_spec = pl.BlockSpec((1, geo.kx, LANES), lambda s: (s, 0, 0))
-    spec_shapes, spec_specs = spectrum_shapes(geo)
-    place = jnp.stack([geo.mode * geo.freq, geo.slab * geo.kx, geo.chan * channels]).astype(jnp.int32)
+    piece = (groups, geo.kx, LANES)
+    piece_shape = jax.ShapeDtypeStruct(piece, F32)
+    place = jnp.stack([geo.mode * geo.freq, geo.slab * geo.kx, geo.chan * channels, geo.chan]).astype(jnp.int32)
     limits = jnp.transpose(mode_limit)
     widths = width_limit[None, :]
 
-    own, other = pl.pallas_call(
+    own, other, kept = pl.pallas_call(
         forward_kernel,
         grid=(groups,),
-        in_specs=[field_spec, whole(fwd_cols.shape), whole(fwd_rows.shape)],
-        out_specs=spec_specs,
-        out_shape=spec_shapes,
-        compiler_params=params(40 << 20),
+        in_specs=[SMEM, ANYWHERE, VMEM, VMEM],
+        out_specs=[VMEM] * 3,
+        out_shape=[jax.ShapeDtypeStruct((geo.slabs,) + piece, F32)] * 2 + [pltpu.VMEM(field, F32)],
+        scratch_shapes=[pltpu.SemaphoreType.DMA((groups,))],
+        compiler_params=params(FORWARD_LIMIT),
+        cost_estimate=cost(6),
         name="forward",
-    )(source_field, fwd_cols, fwd_rows)
+    )(place, streamed(source_field), fwd_cols, fwd_rows)
     parts = reduce_spectrum(own, other, geo)
+    near_weight = prefetch(weight, parts[0], kept)
 
     block = 4
     steps = geo.freq // block
-    w_spec = pl.BlockSpec((channels, block, 2, geo.kx, geo.outs), lambda s: (0, s, 0, 0, 0))
+    w_out = pl.BlockSpec((channels, block, 2, geo.kx, geo.outs), lambda s: (0, s, 0, 0, 0))
     g_spec = pl.BlockSpec((block, 2, geo.kx, geo.outs), lambda s: (s, 0, 0, 0))
-    piece = (groups, geo.kx, LANES)
-    piece_shape = jax.ShapeDtypeStruct(piece, F32)
     modes_shape = jax.ShapeDtypeStruct((geo.freq, 2, geo.kx, geo.outs), F32)
-    mixed, spectra = pl.pallas_call(
-        functools.partial(mix_kernel, geo=geo),
+    relay = [
+        pltpu.VMEM((2 * geo.freq * geo.kx, LANES), F32),
+        pltpu.VMEM((4, LANES, LANES), F32),
+        pltpu.VMEM((2 * groups * geo.kx, LANES), F32),
+    ]
+    mine, theirs, spectra = pl.pallas_call(
+        functools.partial(mix_kernel, geo=geo, block=block),
         grid=(steps,),
-        in_specs=[SMEM] + [whole(piece)] * 4 + [w_spec, whole(limits.shape), whole(widths.shape)],
-        out_specs=[g_spec, whole(piece)],
-        out_shape=[modes_shape, piece_shape],
-        scratch_shapes=[pltpu.VMEM((8, LANES), F32)],
-        compiler_params=params(40 << 20),
+        in_specs=[SMEM] + [VMEM] * 8 + [ANYWHERE],
+        out_specs=[VMEM] * 3,
+        out_shape=[piece_shape] * 3,
+        scratch_shapes=relay,
+        compiler_params=params(MIX_LIMIT),
+        cost_estimate=cost(3),
         name="mix",
-    )(place, *parts, weight, limits, widths)
-    laid = mixed.reshape(geo.freq, 2, geo.kx, geo.chans, groups, 4)
-    laid = laid.transpose(3, 4, 2, 5, 1, 0).reshape((geo.chans,) + piece)
-    mine = lax.dynamic_index_in_dim(laid, geo.chan, 0, keepdims=False)
-    theirs = lax.dynamic_index_in_dim(laid, 1 - geo.chan, 0, keepdims=False)
-    pieces = gather_modes(mine + swap(theirs, "chan"), geo)
-
-    out_field = jax.ShapeDtypeStruct(source_field.shape, F32)
-    output, grad_sum, own, other, sums = pl.pallas_call(
+    )(place, *parts, resident(near_weight), limits, widths, pick, resident(kept))
+    pieces = gather_halves(gather_slabs(mine + swap(theirs, "chan"), geo))
+
+    wide = jax.ShapeDtypeStruct((geo.slabs, groups + 1) + piece[1:], F32)
+    fields = len(pieces) + 2
+    output, grad_sum, own, other = pl.pallas_call(
         functools.partial(middle_kernel, pieces=len(pieces)),
         grid=(groups,),
-        in_specs=[SMEM, SMEM]
-        + [piece_spec] * len(pieces)
-        + [field_spec, field_spec]
-        + [whole(t.shape) for t in (fold, inv_cols, inv_rows, fwd_cols, fwd_rows)],
-        out_specs=[field_spec, field_spec] + spec_specs + [pl.BlockSpec((1, 8, LANES), lambda s: (s, 0, 0))],
-        out_shape=[out_field, out_field] + spec_shapes + [jax.ShapeDtypeStruct((groups, 8, LANES), F32)],
+        in_specs=[SMEM, SMEM] + [VMEM] * (len(pieces) + 1) + [field_spec] + [VMEM] * 5,
+        out_specs=[field_spec, VMEM, VMEM, VMEM],
+        out_shape=[jax.ShapeDtypeStruct(field, F32), pltpu.VMEM(field, F32), wide, wide],
         scratch_shapes=[
+            pltpu.VMEM((4, 256, cols), BF16),
+            pltpu.VMEM((2, 2 * geo.fold, cols), F32),
             pltpu.VMEM((4, rows, cols), F32),
             pltpu.VMEM((4, rows, cols), BF16),
             pltpu.VMEM((4, rows, cols), BF16),
+            pltpu.VMEM((4, rows, 2 * LANES), F32),
         ],
-        compiler_params=params(56 << 20),
+        input_output_aliases={fields: 1},
+        compiler_params=params(MIDDLE_LIMIT),
+        cost_estimate=cost(20),
         name="middle",
     )(
-        skip_gain, channel_bias, *pieces, source_field, cotangent, fold, inv_cols, inv_rows, fwd_cols, fwd_rows
+        skip_gain, channel_bias, *pieces, resident(kept), streamed(cotangent), fold, inv_cols, inv_rows, fwd_cols, fwd_rows
     )
     parts = reduce_spectrum(own, other, geo)
+    near_weight = prefetch(weight, parts[0], grad_sum)
     grads = parts[0] + parts[1] + parts[2] + parts[3]
-    peer = swap(grads, "chan")
-    first = geo.chan == 0
-    laid = jnp.stack([jnp.where(first, grads, peer), jnp.where(first, peer, grads)])
-    laid = laid.reshape(geo.chans, groups, geo.kx, 4, 2, geo.freq).transpose(5, 4, 2, 0, 1, 3)
-    laid = laid.reshape(geo.freq, 2, geo.kx, geo.outs)
+    sums = grads[groups]
+    grads = grads[:groups]
     back, grad_modes = pl.pallas_call(
-        functools.partial(back_kernel, geo=geo),
+        functools.partial(back_kernel, geo=geo, block=block),
         grid=(steps,),
-        in_specs=[SMEM, g_spec, w_spec, whole(limits.shape), whole(widths.shape)],
-        out_specs=[whole(piece), g_spec],
+        in_specs=[SMEM] + [VMEM] * 5 + [ANYWHERE],
+        out_specs=[VMEM, g_spec],
         out_shape=[piece_shape, modes_shape],
-        compiler_params=params(40 << 20),
+        scratch_shapes=relay,
+        compiler_params=params(MIX_LIMIT),
+        cost_estimate=cost(3),
         name="back",
-    )(place, laid, weight, limits, widths)
-    pieces = gather_modes(back, geo)
+    )(place, grads, swap(grads, "chan"), resident(near_weight), limits, widths, resident(grad_sum))
+    near = gather_slabs(back, geo)
     spectral_grad = pl.pallas_call(
         functools.partial(outer_kernel, geo=geo),
         grid=(steps,),
-        in_specs=[SMEM, whole(piece), g_spec, whole(widths.shape)],
-        out_specs=w_spec,
+        in_specs=[SMEM, VMEM, g_spec, VMEM, VMEM, ANYWHERE],
+        out_specs=w_out,
         out_shape=jax.ShapeDtypeStruct(weight.shape, F32),
-        compiler_params=params(40 << 20),
-        cost_estimate=pl.CostEstimate(flops=200_000_000, bytes_accessed=8 << 20, transcendentals=0),
+        compiler_params=params(MIX_LIMIT),
+        cost_estimate=cost(4),
         name="outer",
-    )(place, spectra, grad_modes, widths)
+    )(place, spectra, grad_modes, widths, pick, resident(grad_sum))
+    near, spectral_grad = lax.optimization_barrier((near, spectral_grad))
+    pieces = gather_halves(near)
     field_grad = pl.pallas_call(
         functools.partial(last_kernel, pieces=len(pieces)),
-        grid=(groups,),
-        in_specs=[SMEM]
-        + [piece_spec] * len(pieces)
-        + [field_spec]
-        + [whole(t.shape) for t in (fold, inv_cols, inv_rows)],
-        out_specs=field_spec,
-        out_shape=out_field,
-        compiler_params=params(48 << 20),
+        grid=(groups // LAST_GROUPS,),
+        in_specs=[SMEM] + [VMEM] * (len(pieces) + 4),
+        out_specs=pl.BlockSpec((4 * LAST_GROUPS, rows, cols), lambda s: (s, 0, 0)),
+        out_shape=jax.ShapeDtypeStruct(field, F32),
+        compiler_params=params(LAST_LIMIT),
+        cost_estimate=cost(7),
         name="last",
-    )(skip_gain, *pieces, grad_sum, fold, inv_cols, inv_rows)
-    sums = jnp.sum(sums, axis=2)
-    sums = sums + swap(sums, "mode")
-    sums = sums + send(sums, "slab", 1) + send(sums, "slab", 2) + send(sums, "slab", 3)
-    gate_grad = sums[:, :4].reshape(channels)
-    bias_grad = sums[:, 4:].reshape(channels)
-    return (output, field_grad, jnp.transpose(spectral_grad, (0, 4, 1, 2, 3)), gate_grad, bias_grad)
+    )(skip_gain, *pieces, resident(grad_sum), fold, inv_cols, inv_rows)
+    return (
+        output,
+        field_grad,
+        jnp.transpose(spectral_grad, (0, 4, 1, 2, 3)),
+        sums[0, :channels],
+        sums[1, :channels],
+    )
 
 
 precise = lax.Precision.HIGHEST

time: 162 us -> 114 us (0.70)
  Pallas kernels: 88.9 us -> 68 us
  local copies, waits for them, and re-layouts: 14.4 us -> 0.89 us
  waiting for transfers between devices: 23.7 us -> 16.7 us
  other arithmetic: 6.12 us -> 2.39 us
  starting transfers between devices: 27.5 us -> 25.1 us
    pallas_call x1, Pallas kernels: 14.4 us -> 5.06 us  [fast_local(): pl.pallas_call(functools.partial(outer_kernel, geo=geo), grid=(steps,), i...]
    unnamed x36 -> x8, local copies, waits for them, and re-layouts: 7.89 us -> 0.03 us
    pallas_call x1, Pallas kernels: 16.7 us -> 9.34 us  [fast_local(): pl.pallas_call(functools.partial(last_kernel, pieces=len(pieces)), grid=(...]
    pallas_call x3 -> x5, Pallas kernels: 29.3 us -> 26 us  [the longest x1 11.5 us: fast_local(): pl.pallas_call(forward_kernel, grid=(groups,), in_specs=[SMEM, ANYWHERE,...]
    ppermute x9 -> x6, waiting for transfers between devices: 12.2 us -> 9.01 us  [send(): return lax.ppermute(x, name, [(i, (i + distance) % n) for i in range(n)])]
    ppermute x6, waiting for transfers between devices: 5.72 us -> 2.52 us  [fetch(): return lax.ppermute(x, name, [((i + distance) % n, i) for i in range(n)])]
    reshape x4 -> x0, local copies, waits for them, and re-layouts: 2.96 us -> none  [the longest x1 1.29 us: fast_local(): laid = laid.transpose(3, 4, 2, 5, 1, 0).reshape((geo.chans,) + piece)]
    ppermute x9 -> x6, starting transfers between devices: 12.4 us -> 9.91 us  [send(): return lax.ppermute(x, name, [(i, (i + distance) % n) for i in range(n)])]
  transfers between devices with their start and end apart: 28 -> 24, of which waited for: 12 -> 11; matrix products, arithmetic and copies ran while one was open for 5% -> 2% of each run, Pallas kernels for 11% -> 10%
where the time goes in v2:
time: 114 us
  Pallas kernels  68 us (60%)
  starting transfers between devices  25.1 us (22%)
  waiting for transfers between devices  16.7 us (15%)
  other arithmetic  2.39 us (2%)
    pallas_call x1, Pallas kernels, fast_local(): pl.pallas_call(functools.partial(middle_kernel, pieces=len(pieces)), grid...  27.6 us
    pallas_call x1, Pallas kernels, fast_local(): pl.pallas_call(forward_kernel, grid=(groups,), in_specs=[SMEM, ANYWHERE,...  11.5 us
    ppermute x6, starting transfers between devices, send(): return lax.ppermute(x, name, [(i, (i + distance) % n) for i in range(n)])  9.91 us
    ppermute x6, starting transfers between devices, fetch(): return lax.ppermute(x, name, [((i + distance) % n, i) for i in range(n)])  9.55 us
    pallas_call x1, Pallas kernels, fast_local(): pl.pallas_call(functools.partial(last_kernel, pieces=len(pieces)), grid=(...  9.34 us
    ppermute x6, waiting for transfers between devices, send(): return lax.ppermute(x, name, [(i, (i + distance) % n) for i in range(n)])  9.01 us
    pallas_call x2, Pallas kernels, prefetch(): pl.pallas_call(prefetch_kernel, in_specs=[anywhere] * 3, out_specs=anywhe...  6.79 us
    ppermute x12, starting transfers between devices, swap(): return lax.ppermute(x, name, [(i, (i + 1) % n) for i in range(n)])  5.68 us
  transfers between devices with their start and end apart: 24, of which 11 were waited for; matrix products, arithmetic and copies ran while one was open for 2% of the time, Pallas kernels for 10%

profile of v2, /device:TPU:0, one launch (start us, length us, event | category | flops | bytes accessed | tf_op | source)
XLA Modules:
  0.0 114.1 jit_solution(5310525652286273923)
XLA Ops:
  2.0 11.5 %forward.1 = (f32[4,8,16,128]{3,2,1,0:T(8,128)S(1)}, f32[4,8,16,128]{3,2,1,0:T(8,128)S(1)}, f32[32,256,512]{2,1,0:T(8,128)S(1)}) custom-call(s32[4]{0:T(128)S(1)} %pad_add_fusion.place_ref, f32[32,256,512]{2,1,0:T(8,128)} %x_ref.1, bf16[512,256]{1,0:T(8,128)(2,1)S(1)} %copy.13.col_ref.refs_13_, bf16[128,512]{1,0:T(8,128)(2,1)S(1)} %pad_maximum_fusion.5.row_ref.refs_14_), custom_call_target="tpu_custom_call" | custom-call | flops 600000000 | bytes 1048576 | tf_op jit(solution)/shard_map/forward/pallas_call | solution.py:562
  15.3 5.0 %collective-permute-start.3 = (f32[8,16,128]{2,1,0:T(8,128)S(1)}, f32[8,16,128]{2,1,0:T(8,128)S(1)}, u32[]{:S(2)}, u32[]{:S(2)}) collective-permute-start(f32[8,16,128]{2,1,0:T(8,128)S(1)} %get-tuple-element.45), channel_id=1, source_target_pairs={{0,12},{4,0},{8,4},{12,8},{1,13},{5,1},{9,5},{13,9},{2,14},{6,2},{... | collective-permute-start | bytes 196616 | tf_op jit(solution)/shard_map/ppermute | solution.py:496
  20.3 1.0 collective-permute-start.1
  21.3 3.4 %prefetch.2.w_ref = f32[32,16,2,16,64]{4,3,2,1,0:T(8,128)S(1)} custom-call(f32[8,16,128]{2,1,0:T(8,128)S(1)} %get-tuple-element.48.after_ref.r0, f32[32,256,512]{2,1,0:T(8,128)S(1)} %get-tuple-element.24.held_ref.refs_8_, f32[32,16,2,16,64]{4,3,2,1,0:T(8,128)} %bitcast.51), custom_call_target="tpu_custom_call" | custom-call | flops 400000000 | bytes 1048576 | tf_op jit(solution)/shard_map/prefetch/pallas_call | solution.py:441
  24.8 2.3 %collective-permute-done.2.r2 = f32[8,16,128]{2,1,0:T(8,128)S(1)} collective-permute-done((f32[8,16,128]{2,1,0:T(8,128)S(1)}, f32[8,16,128]{2,1,0:T(8,128)S(1)}, u32[]{:S(2)}, u32[]{:S(2)}) %collective-permute-start.2) | collective-permute-done | bytes 65568 | tf_op jit(solution)/shard_map/ppermute | solution.py:496
  27.1 4.1 %mix.1 = (f32[8,16,128]{2,1,0:T(8,128)S(1)}, f32[8,16,128]{2,1,0:T(8,128)S(1)}, f32[8,16,128]{2,1,0:T(8,128)S(1)}) custom-call(s32[4]{0:T(128)S(1)} %pad_add_fusion.place_ref, f32[8,16,128]{2,1,0:T(8,128)S(1)} %get-tuple-element.48.after_ref.r0, f32[8,16,128]{2,1,0:T(8,128)S(1)} %collective-permute-done.1.r1, f32[8,16,128]{2,1,0:T(8,128)S(1)} %collective-permute-done.2.r2, ...), custom_call_target="tpu_custom_call" | custom-call | flops 300000000 | bytes 1048576 | tf_op jit(solution)/shard_map/mix/pallas_call | solution.py:586
  31.2 1.6 %collective-permute-start.4 = (f32[8,16,128]{2,1,0:T(8,128)S(1)}, f32[8,16,128]{2,1,0:T(8,128)S(1)}, u32[]{:S(2)}, u32[]{:S(2)}) collective-permute-start(f32[8,16,128]{2,1,0:T(8,128)S(1)} %get-tuple-element.26), channel_id=1, source_target_pairs={{0,2},{2,0},{1,3},{3,1},{4,6},{6,4},{5,7},{7,5},{8,10},{10,8},{9,1... | collective-permute-start | bytes 196616 | tf_op jit(solution)/shard_map/ppermute | solution.py:486
  32.8 2.7 %collective-permute-done.4 = f32[8,16,128]{2,1,0:T(8,128)S(1)} collective-permute-done((f32[8,16,128]{2,1,0:T(8,128)S(1)}, f32[8,16,128]{2,1,0:T(8,128)S(1)}, u32[]{:S(2)}, u32[]{:S(2)}) %collective-permute-start.4) | collective-permute-done | bytes 65568 | tf_op jit(solution)/shard_map/ppermute | solution.py:486
  35.8 2.2 %collective-permute-start.6 = (f32[8,16,128]{2,1,0:T(8,128)S(1)}, f32[8,16,128]{2,1,0:T(8,128)S(1)}, u32[]{:S(2)}, u32[]{:S(2)}) collective-permute-start(f32[8,16,128]{2,1,0:T(8,128)S(1)} %add.216.refs_0_), channel_id=1, source_target_pairs={{8,0},{12,4},{0,8},{4,12},{9,1},{13,5},{1,9},{5,13},{10,2},{14,6},... | collective-permute-start | bytes 196616 | tf_op jit(solution)/shard_map/ppermute | solution.py:491
  38.1 2.2 %collective-permute-start.5 = (f32[8,16,128]{2,1,0:T(8,128)S(1)}, f32[8,16,128]{2,1,0:T(8,128)S(1)}, u32[]{:S(2)}, u32[]{:S(2)}) collective-permute-start(f32[8,16,128]{2,1,0:T(8,128)S(1)} %add.216.refs_0_), channel_id=1, source_target_pairs={{4,0},{8,4},{12,8},{0,12},{5,1},{9,5},{13,9},{1,13},{6,2},{10,6},{... | collective-permute-start | bytes 196616 | tf_op jit(solution)/shard_map/ppermute | solution.py:491
  40.4 1.4 %collective-permute-done.7.refs_3_ = f32[8,16,128]{2,1,0:T(8,128)S(1)} collective-permute-done((f32[8,16,128]{2,1,0:T(8,128)S(1)}, f32[8,16,128]{2,1,0:T(8,128)S(1)}, u32[]{:S(2)}, u32[]{:S(2)}) %collective-permute-start.7) | collective-permute-done | bytes 65568 | tf_op jit(solution)/shard_map/ppermute | solution.py:491
  41.8 1.2 %collective-permute-done.6.refs_2_ = f32[8,16,128]{2,1,0:T(8,128)S(1)} collective-permute-done((f32[8,16,128]{2,1,0:T(8,128)S(1)}, f32[8,16,128]{2,1,0:T(8,128)S(1)}, u32[]{:S(2)}, u32[]{:S(2)}) %collective-permute-start.6) | collective-permute-done | bytes 65568 | tf_op jit(solution)/shard_map/ppermute | solution.py:491
  44.4 27.6 %middle.1 = (f32[32,256,512]{2,1,0:T(8,128)}, f32[32,256,512]{2,1,0:T(8,128)S(1)}, f32[4,9,16,128]{3,2,1,0:T(8,128)S(1)}, f32[4,9,16,128]{3,2,1,0:T(8,128)S(1)}) custom-call(f32[32]{0:T(128)S(1)} %copy-done.2, f32[32]{0:T(128)S(1)} %copy-done.3, f32[8,16,128]{2,1,0:T(8,128)S(1)} %add.216.refs_0_, ...), custom_call_target="tpu_custom_call", output_to_operand_aliasing={{1}: (10, {})} | custom-call | flops 2000000000 | bytes 1048576 | tf_op jit(solution)/shard_map/middle/pallas_call | solution.py:601
  72.4 1.2 %collective-permute-done.12 = f32[4,9,16,128]{3,2,1,0:T(8,128)S(1)} collective-permute-done((f32[4,9,16,128]{3,2,1,0:T(8,128)S(1)}, f32[4,9,16,128]{3,2,1,0:T(8,128)S(1)}, u32[]{:S(2)}, u32[]{:S(2)}) %collective-permute-start.12) | collective-permute-done | bytes 294944 | tf_op jit(solution)/shard_map/ppermute | solution.py:486
  73.7 3.3 %collective-permute-start.15 = (f32[9,16,128]{2,1,0:T(8,128)S(1)}, f32[9,16,128]{2,1,0:T(8,128)S(1)}, u32[]{:S(2)}, u32[]{:S(2)}) collective-permute-start(f32[9,16,128]{2,1,0:T(8,128)S(1)} %get-tuple-element.40), channel_id=1, source_target_pairs={{0,12},{4,0},{8,4},{12,8},{1,13},{5,1},{9,5},{13,9},{2,14},{6,2},{... | collective-permute-start | bytes 221192 | tf_op jit(solution)/shard_map/ppermute | solution.py:496
  77.6 2.1 %collective-permute-done.15 = f32[9,16,128]{2,1,0:T(8,128)S(1)} collective-permute-done((f32[9,16,128]{2,1,0:T(8,128)S(1)}, f32[9,16,128]{2,1,0:T(8,128)S(1)}, u32[]{:S(2)}, u32[]{:S(2)}) %collective-permute-start.15) | collective-permute-done | bytes 73760 | tf_op jit(solution)/shard_map/ppermute | solution.py:496
  79.7 4.6 %collective-permute-done.14 = f32[9,16,128]{2,1,0:T(8,128)S(1)} collective-permute-done((f32[9,16,128]{2,1,0:T(8,128)S(1)}, f32[9,16,128]{2,1,0:T(8,128)S(1)}, u32[]{:S(2)}, u32[]{:S(2)}) %collective-permute-start.14) | collective-permute-done | bytes 73760 | tf_op jit(solution)/shard_map/ppermute | solution.py:496
  84.3 1.5 %collective-permute-start.16 = (f32[8,16,128]{2,1,0:T(8,128)S(1)}, f32[8,16,128]{2,1,0:T(8,128)S(1)}, u32[]{:S(2)}, u32[]{:S(2)}) collective-permute-start(f32[8,16,128]{2,1,0:T(8,128)S(1)} %slice.56.own_ref), channel_id=1, source_target_pairs={{0,2},{2,0},{1,3},{3,1},{4,6},{6,4},{5,7},{7,5},{8,10},{10,8},{9,1... | collective-permute-start | bytes 196616 | tf_op jit(solution)/shard_map/ppermute | solution.py:486
  85.9 3.4 %prefetch.3.w_ref = f32[32,16,2,16,64]{4,3,2,1,0:T(8,128)S(1)} custom-call(f32[9,16,128]{2,1,0:T(8,128)S(1)} %get-tuple-element.39.after_ref, f32[32,256,512]{2,1,0:T(8,128)S(1)} %get-tuple-element.30.held_ref.refs_8_, f32[32,16,2,16,64]{4,3,2,1,0:T(8,128)} %bitcast.52), custom_call_target="tpu_custom_call" | custom-call | flops 400000000 | bytes 1048576 | tf_op jit(solution)/shard_map/prefetch/pallas_call | solution.py:441
  89.3 3.6 %back.1 = (f32[8,16,128]{2,1,0:T(8,128)S(1)}, f32[16,2,16,64]{3,2,1,0:T(8,128)S(1)}) custom-call(s32[4]{0:T(128)S(1)} %pad_add_fusion.place_ref, f32[8,16,128]{2,1,0:T(8,128)S(1)} %slice.56.own_ref, f32[8,16,128]{2,1,0:T(8,128)S(1)} %collective-permute-done.16.peer_ref, f32[32,16,2,16,64]{4,3,2,1,0:T(8,128)S(1)} %prefetch.3.w_ref, s32[2,64]{1,0:T(2,128)S(1)} %bitcast.50, ...), custom_call_target="tpu_custom_call" | custom-call | flops 300000000 | bytes 1048576 | tf_op jit(solution)/shard_map/back/pallas_call | solution.py:627
  93.2 2.2 %collective-permute-start.18 = (f32[8,16,128]{2,1,0:T(8,128)S(1)}, f32[8,16,128]{2,1,0:T(8,128)S(1)}, u32[]{:S(2)}, u32[]{:S(2)}) collective-permute-start(f32[8,16,128]{2,1,0:T(8,128)S(1)} %get-tuple-element.34.refs_0_), channel_id=1, source_target_pairs={{8,0},{12,4},{0,8},{4,12},{9,1},{13,5},{1,9},{5,13},{10,2},{14,6},... | collective-permute-start | bytes 196616 | tf_op jit(solution)/shard_map/ppermute | solution.py:491
  95.4 2.4 %collective-permute-start.17 = (f32[8,16,128]{2,1,0:T(8,128)S(1)}, f32[8,16,128]{2,1,0:T(8,128)S(1)}, u32[]{:S(2)}, u32[]{:S(2)}) collective-permute-start(f32[8,16,128]{2,1,0:T(8,128)S(1)} %get-tuple-element.34.refs_0_), channel_id=1, source_target_pairs={{4,0},{8,4},{12,8},{0,12},{5,1},{9,5},{13,9},{1,13},{6,2},{10,6},{... | collective-permute-start | bytes 196616 | tf_op jit(solution)/shard_map/ppermute | solution.py:491
  97.7 5.1 %outer.1 = f32[32,16,2,16,64]{4,3,2,1,0:T(8,128)} custom-call(s32[4]{0:T(128)S(1)} %pad_add_fusion.place_ref, f32[8,16,128]{2,1,0:T(8,128)S(1)} %get-tuple-element.32.spec_ref, f32[16,2,16,64]{3,2,1,0:T(8,128)S(1)} %get-tuple-element.33.gm_ref, s32[1,64]{1,0:T(1,128)S(1)} %bitcast.48, bf16[256,1024]{1,0:T(8,128)(2,1)S(1)} %fusion.pick_ref, ...), custom_call_target="tpu_custom_call" | custom-call | flops 400000000 | bytes 1048576 | tf_op jit(solution)/shard_map/outer/pallas_call | solution.py:639
  104.8 9.3 %last.1 = f32[32,256,512]{2,1,0:T(8,128)} custom-call(f32[32]{0:T(128)S(1)} %copy-done.2, f32[8,16,128]{2,1,0:T(8,128)S(1)} %get-tuple-element.34.refs_0_, f32[8,16,128]{2,1,0:T(8,128)S(1)} %collective-permute-done.17.refs_1_, f32[8,16,128]{2,1,0:T(8,128)S(1)} %collective-permute-done.18.refs_2_, f32[8,16,128]{2,1,0:T(8,128)S(1)} %collective-permute-done.19.refs_3_, ...), custom_call_target="tpu_custom_call" | custom-call | flops 700000000 | bytes 1048576 | tf_op jit(solution)/shard_map/last/pallas_call | solution.py:651
  (83 shorter events, 8.2 us)
Async XLA Ops:
  13.5 1.8 %collective-permute-start = (f32[4,8,16,128]{3,2,1,0:T(8,128)S(1)}, f32[4,8,16,128]{3,2,1,0:T(8,128)S(1)}, u32[]{:S(2)}, u32[]{:S(2)}) collective-permute-start(f32[4,8,16,128]{3,2,1,0:T(8,128)S(1)} %get-tuple-element.23), channel_id=1, source_target_pairs={{0,1},{1,0},{2,3},{3,2},{4,5},{5,4},{6,7},{7,6},{8,9},{9,8},{10,11... | collective-permute-start | bytes 786440 | tf_op jit(solution)/shard_map/ppermute | solution.py:486
  15.3 9.4 %collective-permute-start.3 = (f32[8,16,128]{2,1,0:T(8,128)S(1)}, f32[8,16,128]{2,1,0:T(8,128)S(1)}, u32[]{:S(2)}, u32[]{:S(2)}) collective-permute-start(f32[8,16,128]{2,1,0:T(8,128)S(1)} %get-tuple-element.45), channel_id=1, source_target_pairs={{0,12},{4,0},{8,4},{12,8},{1,13},{5,1},{9,5},{13,9},{2,14},{6,2},{... | collective-permute-start | bytes 196616 | tf_op jit(solution)/shard_map/ppermute | solution.py:496
  20.3 6.8 %collective-permute-start.2 = (f32[8,16,128]{2,1,0:T(8,128)S(1)}, f32[8,16,128]{2,1,0:T(8,128)S(1)}, u32[]{:S(2)}, u32[]{:S(2)}) collective-permute-start(f32[8,16,128]{2,1,0:T(8,128)S(1)} %get-tuple-element.46), channel_id=1, source_target_pairs={{0,8},{4,12},{8,0},{12,4},{1,9},{5,13},{9,1},{13,5},{2,10},{6,14},... | collective-permute-start | bytes 196616 | tf_op jit(solution)/shard_map/ppermute | solution.py:496
  20.3 6.8 %collective-permute-start.1 = (f32[8,16,128]{2,1,0:T(8,128)S(1)}, f32[8,16,128]{2,1,0:T(8,128)S(1)}, u32[]{:S(2)}, u32[]{:S(2)}) collective-permute-start(f32[8,16,128]{2,1,0:T(8,128)S(1)} %get-tuple-element.47), channel_id=1, source_target_pairs={{0,4},{4,8},{8,12},{12,0},{1,5},{5,9},{9,13},{13,1},{2,6},{6,10},{... | collective-permute-start | bytes 196616 | tf_op jit(solution)/shard_map/ppermute | solution.py:496
  31.2 4.3 %collective-permute-start.4 = (f32[8,16,128]{2,1,0:T(8,128)S(1)}, f32[8,16,128]{2,1,0:T(8,128)S(1)}, u32[]{:S(2)}, u32[]{:S(2)}) collective-permute-start(f32[8,16,128]{2,1,0:T(8,128)S(1)} %get-tuple-element.26), channel_id=1, source_target_pairs={{0,2},{2,0},{1,3},{3,1},{4,6},{6,4},{5,7},{7,5},{8,10},{10,8},{9,1... | collective-permute-start | bytes 196616 | tf_op jit(solution)/shard_map/ppermute | solution.py:486
  35.6 6.2 %collective-permute-start.7 = (f32[8,16,128]{2,1,0:T(8,128)S(1)}, f32[8,16,128]{2,1,0:T(8,128)S(1)}, u32[]{:S(2)}, u32[]{:S(2)}) collective-permute-start(f32[8,16,128]{2,1,0:T(8,128)S(1)} %add.216.refs_0_), channel_id=1, source_target_pairs={{12,0},{0,4},{4,8},{8,12},{13,1},{1,5},{5,9},{9,13},{14,2},{2,6},{... | collective-permute-start | bytes 196616 | tf_op jit(solution)/shard_map/ppermute | solution.py:491
  35.8 7.1 %collective-permute-start.6 = (f32[8,16,128]{2,1,0:T(8,128)S(1)}, f32[8,16,128]{2,1,0:T(8,128)S(1)}, u32[]{:S(2)}, u32[]{:S(2)}) collective-permute-start(f32[8,16,128]{2,1,0:T(8,128)S(1)} %add.216.refs_0_), channel_id=1, source_target_pairs={{8,0},{12,4},{0,8},{4,12},{9,1},{13,5},{1,9},{5,13},{10,2},{14,6},... | collective-permute-start | bytes 196616 | tf_op jit(solution)/shard_map/ppermute | solution.py:491
  38.1 4.9 %collective-permute-start.5 = (f32[8,16,128]{2,1,0:T(8,128)S(1)}, f32[8,16,128]{2,1,0:T(8,128)S(1)}, u32[]{:S(2)}, u32[]{:S(2)}) collective-permute-start(f32[8,16,128]{2,1,0:T(8,128)S(1)} %add.216.refs_0_), channel_id=1, source_target_pairs={{4,0},{8,4},{12,8},{0,12},{5,1},{9,5},{13,9},{1,13},{6,2},{10,6},{... | collective-permute-start | bytes 196616 | tf_op jit(solution)/shard_map/ppermute | solution.py:491
  40.4 3.2 %collective-permute-start.8 = (f32[8,16,128]{2,1,0:T(8,128)S(1)}, f32[8,16,128]{2,1,0:T(8,128)S(1)}, u32[]{:S(2)}, u32[]{:S(2)}) collective-permute-start(f32[8,16,128]{2,1,0:T(8,128)S(1)} %add.216.refs_0_), channel_id=1, source_target_pairs={{0,1},{1,0},{2,3},{3,2},{4,5},{5,4},{6,7},{7,6},{8,9},{9,8},{10,11... | collective-permute-start | bytes 196616 | tf_op jit(solution)/shard_map/ppermute | solution.py:486
  41.8 1.8 %collective-permute-start.11 = (f32[8,16,128]{2,1,0:T(8,128)S(1)}, f32[8,16,128]{2,1,0:T(8,128)S(1)}, u32[]{:S(2)}, u32[]{:S(2)}) collective-permute-start(f32[8,16,128]{2,1,0:T(8,128)S(1)} %collective-permute-done.7.refs_3_), channel_id=1, source_target_pairs={{0,1},{1,0},{2,3},{3,2},{4,5},{5,4},{6,7},{7,6},{8,9},{9,8},{10,11... | collective-permute-start | bytes 196616 | tf_op jit(solution)/shard_map/ppermute | solution.py:486
  42.9 1.3 %collective-permute-start.10 = (f32[8,16,128]{2,1,0:T(8,128)S(1)}, f32[8,16,128]{2,1,0:T(8,128)S(1)}, u32[]{:S(2)}, u32[]{:S(2)}) collective-permute-start(f32[8,16,128]{2,1,0:T(8,128)S(1)} %collective-permute-done.6.refs_2_), channel_id=1, source_target_pairs={{0,1},{1,0},{2,3},{3,2},{4,5},{5,4},{6,7},{7,6},{8,9},{9,8},{10,11... | collective-permute-start | bytes 196616 | tf_op jit(solution)/shard_map/ppermute | solution.py:486
  43.0 1.4 %collective-permute-start.9 = (f32[8,16,128]{2,1,0:T(8,128)S(1)}, f32[8,16,128]{2,1,0:T(8,128)S(1)}, u32[]{:S(2)}, u32[]{:S(2)}) collective-permute-start(f32[8,16,128]{2,1,0:T(8,128)S(1)} %collective-permute-done.5.refs_1_), channel_id=1, source_target_pairs={{0,1},{1,0},{2,3},{3,2},{4,5},{5,4},{6,7},{7,6},{8,9},{9,8},{10,11... | collective-permute-start | bytes 196616 | tf_op jit(solution)/shard_map/ppermute | solution.py:486
  72.0 1.6 %collective-permute-start.12 = (f32[4,9,16,128]{3,2,1,0:T(8,128)S(1)}, f32[4,9,16,128]{3,2,1,0:T(8,128)S(1)}, u32[]{:S(2)}, u32[]{:S(2)}) collective-permute-start(f32[4,9,16,128]{3,2,1,0:T(8,128)S(1)} %get-tuple-element.29), channel_id=1, source_target_pairs={{0,1},{1,0},{2,3},{3,2},{4,5},{5,4},{6,7},{7,6},{8,9},{9,8},{10,11... | collective-permute-start | bytes 884744 | tf_op jit(solution)/shard_map/ppermute | solution.py:486
  73.7 6.0 %collective-permute-start.15 = (f32[9,16,128]{2,1,0:T(8,128)S(1)}, f32[9,16,128]{2,1,0:T(8,128)S(1)}, u32[]{:S(2)}, u32[]{:S(2)}) collective-permute-start(f32[9,16,128]{2,1,0:T(8,128)S(1)} %get-tuple-element.40), channel_id=1, source_target_pairs={{0,12},{4,0},{8,4},{12,8},{1,13},{5,1},{9,5},{13,9},{2,14},{6,2},{... | collective-permute-start | bytes 221192 | tf_op jit(solution)/shard_map/ppermute | solution.py:496
  77.0 7.3 %collective-permute-start.14 = (f32[9,16,128]{2,1,0:T(8,128)S(1)}, f32[9,16,128]{2,1,0:T(8,128)S(1)}, u32[]{:S(2)}, u32[]{:S(2)}) collective-permute-start(f32[9,16,128]{2,1,0:T(8,128)S(1)} %get-tuple-element.41), channel_id=1, source_target_pairs={{0,8},{4,12},{8,0},{12,4},{1,9},{5,13},{9,1},{13,5},{2,10},{6,14},... | collective-permute-start | bytes 221192 | tf_op jit(solution)/shard_map/ppermute | solution.py:496
  77.0 7.3 %collective-permute-start.13 = (f32[9,16,128]{2,1,0:T(8,128)S(1)}, f32[9,16,128]{2,1,0:T(8,128)S(1)}, u32[]{:S(2)}, u32[]{:S(2)}) collective-permute-start(f32[9,16,128]{2,1,0:T(8,128)S(1)} %get-tuple-element.42), channel_id=1, source_target_pairs={{0,4},{4,8},{8,12},{12,0},{1,5},{5,9},{9,13},{13,1},{2,6},{6,10},{... | collective-permute-start | bytes 221192 | tf_op jit(solution)/shard_map/ppermute | solution.py:496
  84.3 4.9 %collective-permute-start.16 = (f32[8,16,128]{2,1,0:T(8,128)S(1)}, f32[8,16,128]{2,1,0:T(8,128)S(1)}, u32[]{:S(2)}, u32[]{:S(2)}) collective-permute-start(f32[8,16,128]{2,1,0:T(8,128)S(1)} %slice.56.own_ref), channel_id=1, source_target_pairs={{0,2},{2,0},{1,3},{3,1},{4,6},{6,4},{5,7},{7,5},{8,10},{10,8},{9,1... | collective-permute-start | bytes 196616 | tf_op jit(solution)/shard_map/ppermute | solution.py:486
  92.9 9.9 %collective-permute-start.19 = (f32[8,16,128]{2,1,0:T(8,128)S(1)}, f32[8,16,128]{2,1,0:T(8,128)S(1)}, u32[]{:S(2)}, u32[]{:S(2)}) collective-permute-start(f32[8,16,128]{2,1,0:T(8,128)S(1)} %get-tuple-element.34.refs_0_), channel_id=1, source_target_pairs={{12,0},{0,4},{4,8},{8,12},{13,1},{1,5},{5,9},{9,13},{14,2},{2,6},{... | collective-permute-start | bytes 196616 | tf_op jit(solution)/shard_map/ppermute | solution.py:491
  93.2 9.6 %collective-permute-start.18 = (f32[8,16,128]{2,1,0:T(8,128)S(1)}, f32[8,16,128]{2,1,0:T(8,128)S(1)}, u32[]{:S(2)}, u32[]{:S(2)}) collective-permute-start(f32[8,16,128]{2,1,0:T(8,128)S(1)} %get-tuple-element.34.refs_0_), channel_id=1, source_target_pairs={{8,0},{12,4},{0,8},{4,12},{9,1},{13,5},{1,9},{5,13},{10,2},{14,6},... | collective-permute-start | bytes 196616 | tf_op jit(solution)/shard_map/ppermute | solution.py:491
  95.4 7.4 %collective-permute-start.17 = (f32[8,16,128]{2,1,0:T(8,128)S(1)}, f32[8,16,128]{2,1,0:T(8,128)S(1)}, u32[]{:S(2)}, u32[]{:S(2)}) collective-permute-start(f32[8,16,128]{2,1,0:T(8,128)S(1)} %get-tuple-element.34.refs_0_), channel_id=1, source_target_pairs={{4,0},{8,4},{12,8},{0,12},{5,1},{9,5},{13,9},{1,13},{6,2},{10,6},{... | collective-permute-start | bytes 196616 | tf_op jit(solution)/shard_map/ppermute | solution.py:491
  102.8 1.6 %collective-permute-start.20 = (f32[8,16,128]{2,1,0:T(8,128)S(1)}, f32[8,16,128]{2,1,0:T(8,128)S(1)}, u32[]{:S(2)}, u32[]{:S(2)}) collective-permute-start(f32[8,16,128]{2,1,0:T(8,128)S(1)} %get-tuple-element.34.refs_0_), channel_id=1, source_target_pairs={{0,1},{1,0},{2,3},{3,2},{4,5},{5,4},{6,7},{7,6},{8,9},{9,8},{10,11... | collective-permute-start | bytes 196616 | tf_op jit(solution)/shard_map/ppermute | solution.py:486
  102.9 1.5 %collective-permute-start.21 = (f32[8,16,128]{2,1,0:T(8,128)S(1)}, f32[8,16,128]{2,1,0:T(8,128)S(1)}, u32[]{:S(2)}, u32[]{:S(2)}) collective-permute-start(f32[8,16,128]{2,1,0:T(8,128)S(1)} %collective-permute-done.17.refs_1_), channel_id=1, source_target_pairs={{0,1},{1,0},{2,3},{3,2},{4,5},{5,4},{6,7},{7,6},{8,9},{9,8},{10,11... | collective-permute-start | bytes 196616 | tf_op jit(solution)/shard_map/ppermute | solution.py:486
  103.4 1.3 %collective-permute-start.22 = (f32[8,16,128]{2,1,0:T(8,128)S(1)}, f32[8,16,128]{2,1,0:T(8,128)S(1)}, u32[]{:S(2)}, u32[]{:S(2)}) collective-permute-start(f32[8,16,128]{2,1,0:T(8,128)S(1)} %collective-permute-done.18.refs_2_), channel_id=1, source_target_pairs={{0,1},{1,0},{2,3},{3,2},{4,5},{5,4},{6,7},{7,6},{8,9},{9,8},{10,11... | collective-permute-start | bytes 196616 | tf_op jit(solution)/shard_map/ppermute | solution.py:486
  103.5 1.3 %collective-permute-start.23 = (f32[8,16,128]{2,1,0:T(8,128)S(1)}, f32[8,16,128]{2,1,0:T(8,128)S(1)}, u32[]{:S(2)}, u32[]{:S(2)}) collective-permute-start(f32[8,16,128]{2,1,0:T(8,128)S(1)} %collective-permute-done.19.refs_3_), channel_id=1, source_target_pairs={{0,1},{1,0},{2,3},{3,2},{4,5},{5,4},{6,7},{7,6},{8,9},{9,8},{10,11... | collective-permute-start | bytes 196616 | tf_op jit(solution)/shard_map/ppermute | solution.py:486
  (4 other events, 50.8 us)

commit v3 on v2

--- a/solution.py
+++ b/solution.py
@@ -44,7 +44,7 @@
     second = jnp.stack([-sin, -cos], axis=2).reshape(geo.cols, -1)
     first_h, first_l = split_table(first)
     second_h, second_l = split_table(second)
-    forward_cols = jnp.concatenate([first_h, first_l, second_h, second_l], axis=1)
+    forward_cols = jnp.concatenate([first_h, first_l], axis=1)
     inverse_cols = jnp.stack(
         [
             jnp.concatenate([high.T, high.T, low.T, low.T], axis=0)
@@ -57,7 +57,7 @@
     half = geo.slabs * geo.kx // 2
     wave = jnp.where(place < half, place, place - 2 * half)
     theta = angles(wave % geo.all_rows, row_cell, geo.all_rows)
-    forward_h, forward_l = split_table(jnp.concatenate([jnp.cos(theta), jnp.sin(theta)], axis=1))
+    forward_h, forward_l = split_table(jnp.concatenate([jnp.cos(theta), jnp.sin(theta)], axis=0))
     forward_rows = jnp.concatenate([forward_h, forward_l], axis=0)
     kept = jnp.arange(geo.fold // 2, dtype=jnp.int32)
     theta = angles(row_cell, kept, geo.all_rows)
@@ -78,16 +78,19 @@
     return lax.broadcasted_iota(jnp.int32, shape, 1) // width
 
 
-def pair_spectra(first, second, row_tab):
-    kx_all = row_tab.shape[0] // 2
-    pair = jnp.concatenate(
-        [jnp.concatenate([a[:, :LANES], a[:, LANES:]], axis=0) for a in (first, second)], axis=1
-    )
-    high, low = split(pair)
+def pair_spectra(first, second, row_tab, freq):
+    sides = row_tab.shape[0] // 2
+    high, low = split(jnp.concatenate([first, second], axis=1))
     both = mm(row_tab, high)
-    total = both[:kx_all] + both[kx_all:] + mm(row_tab[:kx_all], low)
-    halves = [total[:, lane : lane + LANES] for lane in (0, LANES)]
-    return [one + pltpu.roll(one, 64, 1) for one in halves]
+    total = both[:sides] + both[sides:] + mm(row_tab[:sides], low)
+    out = []
+    for lane in (0, LANES):
+        one = total[:, lane : lane + LANES]
+        one = one + pltpu.roll(one, 64, 1)
+        cos, sin = one[: sides // 2], one[sides // 2 :]
+        real = lane_group(sin.shape, freq) % 2 == 0
+        out.append(cos + jnp.where(real, pltpu.roll(sin, LANES - freq, 1), -pltpu.roll(sin, freq, 1)))
+    return out
 
 
 def write_spectra(doubled, own_ref, other_ref, group):
@@ -109,7 +112,19 @@
         other_ref[q, group] = other[q * kx : (q + 1) * kx]
 
 
-def forward_kernel(place_ref, x_ref, col_ref, row_ref, own_ref, other_ref, keep_ref, sems):
+def emitting(part_ref, row_ref, own_ref, other_ref, at, freq):
+    held = {}
+
+    def pair(k):
+        held[k] = pair_spectra(part_ref[2 * k], part_ref[2 * k + 1], row_ref[...], freq)
+
+    def write():
+        write_spectra(held[0] + held[1], own_ref, other_ref, at)
+
+    return [functools.partial(pair, 0), functools.partial(pair, 1), write]
+
+
+def forward_kernel(place_ref, x_ref, col_ref, row_ref, own_ref, other_ref, keep_ref, sems, part_ref, *, freq):
     del place_ref
     step = pl.program_id(0)
 
@@ -119,16 +134,29 @@
 
     @pl.when(step == 0)
     def _():
-        for at in range(sems.shape[0]):
+        for at in range(FORWARD_AHEAD):
             fetching(at).start()
 
+    @pl.when(step + FORWARD_AHEAD < pl.num_programs(0))
+    def _():
+        fetching(step + FORWARD_AHEAD).start()
+
+    @pl.when(step == 0)
+    def _():
+        part_ref[...] = jnp.zeros_like(part_ref)
+
     fetching(step).wait()
-    parts = []
+    emits = emitting(part_ref, row_ref, own_ref, other_ref, jnp.maximum(step - 1, 0), freq)
     for c in range(4):
+        if c < len(emits):
+            emits[c]()
         high, low = split(keep_ref[step * 4 + c])
-        parts.append(mm(high, col_ref[...]) + mm(low, col_ref[...]))
-    doubled = pair_spectra(*parts[:2], row_ref[...]) + pair_spectra(*parts[2:], row_ref[...])
-    write_spectra(doubled, own_ref, other_ref, step)
+        part_ref[c] = mm(high, col_ref[...]) + mm(low, col_ref[...])
+
+    @pl.when(step == pl.num_programs(0) - 1)
+    def _():
+        for task in emitting(part_ref, row_ref, own_ref, other_ref, step, freq):
+            task()
 
 
 def fold_modes(piece_refs, step, fold_ref):
@@ -166,18 +194,32 @@
     return jnp.concatenate([high, low, high, rest], axis=0)
 
 
-def stack_modes(piece_refs, step, fold_ref, inv_col_ref):
-    folded = fold_modes(piece_refs, step, fold_ref)
-    half = folded.shape[0] // 2
-    rows = [line_up(folded, c) for c in range(4)]
-    sides = [spread_columns(rows, side, inv_col_ref) for side in (0, 1)]
-    return [stack_operand(*(s[c * half : (c + 1) * half] for s in sides)) for c in range(4)]
+def preparing(piece_refs, at, fold_ref, inv_col_ref, wide_ref, ready, biases):
+    held = {}
+    half = fold_ref.shape[0] // 2
+
+    def begin():
+        held["folded"] = fold_modes(piece_refs, at, fold_ref)
+
+    def line(c):
+        held[c] = line_up(held["folded"], c)
+
+    def spread(side):
+        wide_ref[side] = spread_columns([held[c] for c in range(4)], side, inv_col_ref)
+
+    def stack(c):
+        plus, minus = (wide_ref[side, c * half : (c + 1) * half] for side in (0, 1))
+        ready[c] = stack_operand(plus, minus, None if biases is None else biases[c])
+
+    early = [begin] + [functools.partial(line, c) for c in range(4)]
+    early += [functools.partial(spread, side) for side in (0, 1)]
+    return early, [functools.partial(stack, c) for c in range(4)]
 
 
 CHUNK = 16
 
 
-def middle_kernel(skip_ref, bias_ref, *refs, pieces):
+def middle_kernel(place_ref, skip_ref, bias_ref, *refs, pieces, freq):
     piece_refs = refs[:pieces]
     x_ref, ct_ref, fold_ref, inv_col_ref, inv_row_ref, col_ref, row_ref = refs[pieces : pieces + 7]
     out_ref, gs_ref, own_ref, other_ref, ready, wide_ref, branch, high_ref, low_ref, part_ref = refs[pieces + 7 :]
@@ -185,49 +227,24 @@
     last = pl.num_programs(0) - 1
     rows, cols = x_ref.shape[1:]
     sums = own_ref.shape[1] - 1
-    half = fold_ref.shape[0] // 2
-
-    def preparing(at):
-        held = {}
-
-        def begin():
-            held["folded"] = fold_modes(piece_refs, at, fold_ref)
-
-        def line(c):
-            held[c] = line_up(held["folded"], c)
-
-        def spread(side):
-            wide_ref[side] = spread_columns([held[c] for c in range(4)], side, inv_col_ref)
-
-        def stack(c):
-            plus, minus = (wide_ref[side, c * half : (c + 1) * half] for side in (0, 1))
-            ready[c] = stack_operand(plus, minus, bias_ref[at * 4 + c])
-
-        early = [begin] + [functools.partial(line, c) for c in range(4)]
-        early += [functools.partial(spread, side) for side in (0, 1)]
-        return early, [functools.partial(stack, c) for c in range(4)]
-
-    def emitting(at):
-        held = {}
-
-        def pair(k):
-            held[k] = pair_spectra(part_ref[2 * k], part_ref[2 * k + 1], row_ref[...])
-
-        def write():
-            write_spectra(held[0] + held[1], own_ref, other_ref, at)
-
-        return [functools.partial(pair, 0), functools.partial(pair, 1), write]
+
+    def prepare_group(at):
+        biases = [bias_ref[at * 4 + c] for c in range(4)]
+        return preparing(piece_refs, at, fold_ref, inv_col_ref, wide_ref, ready, biases)
+
+    def emit_group(at):
+        return emitting(part_ref, row_ref, own_ref, other_ref, at, freq)
 
     @pl.when(step == 0)
     def _():
-        early, late = preparing(0)
+        early, late = prepare_group(0)
         for task in early + late:
             task()
         part_ref[...] = jnp.zeros_like(part_ref)
         own_ref[0, sums] = jnp.zeros(own_ref.shape[2:], F32)
 
-    early, late = preparing(jnp.minimum(step + 1, last))
-    emits = emitting(jnp.maximum(step - 1, 0))
+    early, late = prepare_group(jnp.minimum(step + 1, last))
+    emits = emit_group(jnp.maximum(step - 1, 0))
     chunks = rows // CHUNK
     plan = {(0, 1): emits[0], (0, 5): emits[1], (0, 10): emits[2]}
     for k, task in enumerate(early):
@@ -242,7 +259,6 @@
         channel = step * 4 + c
         skip = skip_ref[channel]
         gate = jnp.zeros((CHUNK, cols), F32)
-        bias = jnp.zeros((CHUNK, cols), F32)
         for k in range(chunks):
             r = k * CHUNK
             if (c, k) in plan:
@@ -262,36 +278,65 @@
             grad = ct_ref[c, r : r + CHUNK] * slope
             gs_ref[channel, r : r + CHUNK] = grad
             gate = gate + grad * x
-            bias = bias + grad
             top = grad.astype(BF16)
             high_ref[c, r : r + CHUNK] = top
             low_ref[c, r : r + CHUNK] = (grad - top.astype(F32)).astype(BF16)
-        for at, total in ((0, gate), (1, bias)):
-            line = jnp.sum(total, axis=0, keepdims=True)
-            value = jnp.sum(sum(line[:, k : k + LANES] for k in range(0, cols, LANES)), axis=1, keepdims=True)
-            tile = jnp.where((row == at) & (lane == channel), jnp.broadcast_to(value, tile.shape), tile)
+        line = jnp.sum(gate, axis=0, keepdims=True)
+        value = jnp.sum(sum(line[:, k : k + LANES] for k in range(0, cols, LANES)), axis=1, keepdims=True)
+        tile = jnp.where((row == 0) & (lane == channel), jnp.broadcast_to(value, tile.shape), tile)
     part_ref[3] = mm(high_ref[3], col_ref[...]) + mm(low_ref[3], col_ref[...])
     own_ref[0, sums] = tile
 
     @pl.when(step == last)
     def _():
-        for task in emitting(last):
+        for task in emit_group(last):
             task()
+        whole_sums = tile
+        for g in range(sums):
+            lines = [ref[place_ref[4], g][0:1, :] for ref in (own_ref, other_ref)]
+            line = jnp.where(place_ref[0] == 0, lines[0], lines[1])
+            for c in range(4):
+                value = jnp.broadcast_to(line[:, 2 * freq * c : 2 * freq * c + 1], tile.shape)
+                whole_sums = jnp.where((row == 1) & (lane == g * 4 + c), value, whole_sums)
         for q in range(own_ref.shape[0]):
-            own_ref[q, sums] = tile
-            other_ref[q, sums] = tile
+            own_ref[q, sums] = whole_sums
+            other_ref[q, sums] = whole_sums
 
 
 def last_kernel(skip_ref, *refs, pieces):
     piece_refs = refs[:pieces]
-    gs_ref, fold_ref, inv_col_ref, inv_row_ref, out_ref = refs[pieces:]
+    gs_ref, fold_ref, inv_col_ref, inv_row_ref, out_ref, made_ref, sems, ready, wide_ref = refs[pieces:]
     step = pl.program_id(0)
-    block = out_ref.shape[0]
-    for first in range(0, block, 4):
-        stacked = stack_modes(piece_refs, step * (block // 4) + first // 4, fold_ref, inv_col_ref)
-        for c in range(4):
-            channel = step * block + first + c
-            out_ref[first + c] = mm(inv_row_ref[...], stacked[c]) + skip_ref[channel] * gs_ref[channel]
+    last = pl.num_programs(0) - 1
+
+    def storing(at):
+        four = pl.ds(at * 4, 4)
+        return pltpu.make_async_copy(made_ref.at[four], out_ref.at[four], sems.at[at])
+
+    def prepare_group(at):
+        return preparing(piece_refs, at, fold_ref, inv_col_ref, wide_ref, ready, None)
+
+    @pl.when(step == 0)
+    def _():
+        early, late = prepare_group(0)
+        for task in early + late:
+            task()
+
+    early, late = prepare_group(jnp.minimum(step + 1, last))
+    turns = [early[:1], early[1:5], early[5:], []]
+    for c in range(4):
+        channel = step * 4 + c
+        made_ref[channel] = mm(inv_row_ref[...], ready[c]) + skip_ref[channel] * gs_ref[channel]
+        for task in turns[c]:
+            task()
+    for task in late:
+        task()
+    storing(step).start()
+
+    @pl.when(step == last)
+    def _():
+        for at in range(sems.shape[0]):
+            storing(at).wait()
 
 
 def limits_mask(place_ref, limit_ref, y, kx, kx_all, scale_cells, shape):
@@ -474,7 +519,8 @@
             and self.freq == 16
             and self.kx_all == 64
             and self.kx % 8 == 0
-            and self.channels % 8 == 0
+            and self.channels % 4 == 0
+            and self.channels <= LANES
             and self.rows % 16 == 0
             and self.cols % LANES == 0
             and 3 * self.fold <= 256
@@ -504,10 +550,10 @@
 
 
 FORWARD_LIMIT = 16 << 20
+FORWARD_AHEAD = 2
 MIX_LIMIT = 16 << 20
 MIDDLE_LIMIT = 24 << 20
-LAST_LIMIT = 24 << 20
-LAST_GROUPS = 2
+LAST_LIMIT = 28 << 20
 
 
 def cost(micros):
@@ -555,17 +601,17 @@
     field_spec = pl.BlockSpec((4, rows, cols), lambda s: (s, 0, 0))
     piece = (groups, geo.kx, LANES)
     piece_shape = jax.ShapeDtypeStruct(piece, F32)
-    place = jnp.stack([geo.mode * geo.freq, geo.slab * geo.kx, geo.chan * channels, geo.chan]).astype(jnp.int32)
+    place = jnp.stack([geo.mode * geo.freq, geo.slab * geo.kx, geo.chan * channels, geo.chan, -geo.slab % geo.slabs]).astype(jnp.int32)
     limits = jnp.transpose(mode_limit)
     widths = width_limit[None, :]
 
     own, other, kept = pl.pallas_call(
-        forward_kernel,
+        functools.partial(forward_kernel, freq=geo.freq),
         grid=(groups,),
         in_specs=[SMEM, ANYWHERE, VMEM, VMEM],
         out_specs=[VMEM] * 3,
         out_shape=[jax.ShapeDtypeStruct((geo.slabs,) + piece, F32)] * 2 + [pltpu.VMEM(field, F32)],
-        scratch_shapes=[pltpu.SemaphoreType.DMA((groups,))],
+        scratch_shapes=[pltpu.SemaphoreType.DMA((groups,)), pltpu.VMEM((4, rows, LANES), F32)],
         compiler_params=params(FORWARD_LIMIT),
         cost_estimate=cost(6),
         name="forward",
@@ -597,11 +643,11 @@
     pieces = gather_halves(gather_slabs(mine + swap(theirs, "chan"), geo))
 
     wide = jax.ShapeDtypeStruct((geo.slabs, groups + 1) + piece[1:], F32)
-    fields = len(pieces) + 2
+    fields = len(pieces) + 3
     output, grad_sum, own, other = pl.pallas_call(
-        functools.partial(middle_kernel, pieces=len(pieces)),
+        functools.partial(middle_kernel, pieces=len(pieces), freq=geo.freq),
         grid=(groups,),
-        in_specs=[SMEM, SMEM] + [VMEM] * (len(pieces) + 1) + [field_spec] + [VMEM] * 5,
+        in_specs=[SMEM] * 3 + [VMEM] * (len(pieces) + 1) + [field_spec] + [VMEM] * 5,
         out_specs=[field_spec, VMEM, VMEM, VMEM],
         out_shape=[jax.ShapeDtypeStruct(field, F32), pltpu.VMEM(field, F32), wide, wide],
         scratch_shapes=[
@@ -610,17 +656,18 @@
             pltpu.VMEM((4, rows, cols), F32),
             pltpu.VMEM((4, rows, cols), BF16),
             pltpu.VMEM((4, rows, cols), BF16),
-            pltpu.VMEM((4, rows, 2 * LANES), F32),
+            pltpu.VMEM((4, rows, LANES), F32),
         ],
         input_output_aliases={fields: 1},
         compiler_params=params(MIDDLE_LIMIT),
         cost_estimate=cost(20),
         name="middle",
     )(
-        skip_gain, channel_bias, *pieces, resident(kept), streamed(cotangent), fold, inv_cols, inv_rows, fwd_cols, fwd_rows
+        place, skip_gain, channel_bias, *pieces, resident(kept), streamed(cotangent), fold, inv_cols, inv_rows, fwd_cols, fwd_rows
     )
     parts = reduce_spectrum(own, other, geo)
     near_weight = prefetch(weight, parts[0], grad_sum)
+    parts, near_weight = lax.optimization_barrier((parts, near_weight))
     grads = parts[0] + parts[1] + parts[2] + parts[3]
     sums = grads[groups]
     grads = grads[:groups]
@@ -650,10 +697,16 @@
     pieces = gather_halves(near)
     field_grad = pl.pallas_call(
         functools.partial(last_kernel, pieces=len(pieces)),
-        grid=(groups // LAST_GROUPS,),
+        grid=(groups,),
         in_specs=[SMEM] + [VMEM] * (len(pieces) + 4),
-        out_specs=pl.BlockSpec((4 * LAST_GROUPS, rows, cols), lambda s: (s, 0, 0)),
+        out_specs=ANYWHERE,
         out_shape=jax.ShapeDtypeStruct(field, F32),
+        scratch_shapes=[
+            pltpu.VMEM(field, F32),
+            pltpu.SemaphoreType.DMA((groups,)),
+            pltpu.VMEM((4, 256, cols), BF16),
+            pltpu.VMEM((2, 2 * geo.fold, cols), F32),
+        ],
         compiler_params=params(LAST_LIMIT),
         cost_estimate=cost(7),
         name="last",

time: 114 us -> 110 us (0.965)
  Pallas kernels: 68 us -> 63.9 us
    ppermute x6, waiting for transfers between devices: 9.01 us -> 5.61 us  [send(): return lax.ppermute(x, name, [(i, (i + distance) % n) for i in range(n)])]
    ppermute x12, waiting for transfers between devices: 5.18 us -> 7.97 us  [swap(): return lax.ppermute(x, name, [(i, (i + 1) % n) for i in range(n)])]
    pallas_call x2, Pallas kernels: 39.1 us -> 36.6 us  [the longest x1 26.9 us: fast_local(): pl.pallas_call(functools.partial(middle_kernel, pieces=len(pieces), freq=...]
    pallas_call x1, Pallas kernels: 9.34 us -> 7.76 us  [fast_local(): pl.pallas_call(functools.partial(last_kernel, pieces=len(pieces)), grid=(...]
  transfers between devices with their start and end apart: 24 -> 24, of which waited for: 11 -> 11; matrix products, arithmetic and copies ran while one was open for 2% -> 2% of each run, Pallas kernels for 10% -> 11%
where the time goes in v3:
time: 110 us; the launch traced here: 109 us
  Pallas kernels  63.9 us (58%)
  starting transfers between devices  25.1 us (23%)
  waiting for transfers between devices  16.1 us (15%)
  other arithmetic  2.28 us (2%)
    pallas_call x1, Pallas kernels, fast_local(): pl.pallas_call(functools.partial(middle_kernel, pieces=len(pieces), freq=...  26.9 us
    ppermute x6, starting transfers between devices, send(): return lax.ppermute(x, name, [(i, (i + distance) % n) for i in range(n)])  9.9 us
    pallas_call x1, Pallas kernels, fast_local(): pl.pallas_call(functools.partial(forward_kernel, freq=geo.freq), grid=(gr...  9.67 us
    ppermute x6, starting transfers between devices, fetch(): return lax.ppermute(x, name, [((i + distance) % n, i) for i in range(n)])  9.53 us
    ppermute x12, waiting for transfers between devices, swap(): return lax.ppermute(x, name, [(i, (i + 1) % n) for i in range(n)])  7.97 us
    pallas_call x1, Pallas kernels, fast_local(): pl.pallas_call(functools.partial(last_kernel, pieces=len(pieces)), grid=(...  7.76 us
    pallas_call x2, Pallas kernels, prefetch(): pl.pallas_call(prefetch_kernel, in_specs=[anywhere] * 3, out_specs=anywhe...  6.79 us
    ppermute x12, starting transfers between devices, swap(): return lax.ppermute(x, name, [(i, (i + 1) % n) for i in range(n)])  5.67 us
  transfers between devices with their start and end apart: 24, of which 11 were waited for; matrix products, arithmetic and copies ran while one was open for 2% of the time, Pallas kernels for 11%

profile of v3, /device:TPU:0, one launch (start us, length us, event | category | flops | bytes accessed | tf_op | source)
XLA Modules:
  0.0 109.4 jit_solution(13075931904748903769)
XLA Ops:
  2.0 9.7 %forward.1 = (f32[4,8,16,128]{3,2,1,0:T(8,128)S(1)}, f32[4,8,16,128]{3,2,1,0:T(8,128)S(1)}, f32[32,256,512]{2,1,0:T(8,128)S(1)}) custom-call(s32[5]{0:T(128)S(1)} %stack.42.place_ref, f32[32,256,512]{2,1,0:T(8,128)} %x_ref.1, bf16[512,128]{1,0:T(8,128)(2,1)S(1)} %copy.13.col_ref.refs_13_, bf16[256,256]{1,0:T(8,128)(2,1)S(1)} %pad_maximum_fusion.4.row_ref.refs_14_), custom_call_target="tpu_custom_call" | custom-call | flops 600000000 | bytes 1048576 | tf_op jit(solution)/shard_map/forward/pallas_call | solution.py:608
  13.5 5.0 %collective-permute-start.3 = (f32[8,16,128]{2,1,0:T(8,128)S(1)}, f32[8,16,128]{2,1,0:T(8,128)S(1)}, u32[]{:S(2)}, u32[]{:S(2)}) collective-permute-start(f32[8,16,128]{2,1,0:T(8,128)S(1)} %get-tuple-element.55), channel_id=1, source_target_pairs={{0,12},{4,0},{8,4},{12,8},{1,13},{5,1},{9,5},{13,9},{2,14},{6,2},{... | collective-permute-start | bytes 196616 | tf_op jit(solution)/shard_map/ppermute | solution.py:542
  18.5 1.0 collective-permute-start.1
  19.5 3.4 %prefetch.2.w_ref = f32[32,16,2,16,64]{4,3,2,1,0:T(8,128)S(1)} custom-call(f32[8,16,128]{2,1,0:T(8,128)S(1)} %get-tuple-element.58.after_ref.r0, f32[32,256,512]{2,1,0:T(8,128)S(1)} %get-tuple-element.29.held_ref.refs_8_, f32[32,16,2,16,64]{4,3,2,1,0:T(8,128)} %bitcast.50), custom_call_target="tpu_custom_call" | custom-call | flops 400000000 | bytes 1048576 | tf_op jit(solution)/shard_map/prefetch/pallas_call | solution.py:486
  23.0 2.3 %collective-permute-done.2.r2 = f32[8,16,128]{2,1,0:T(8,128)S(1)} collective-permute-done((f32[8,16,128]{2,1,0:T(8,128)S(1)}, f32[8,16,128]{2,1,0:T(8,128)S(1)}, u32[]{:S(2)}, u32[]{:S(2)}) %collective-permute-start.2) | collective-permute-done | bytes 65568 | tf_op jit(solution)/shard_map/ppermute | solution.py:542
  25.3 4.1 %mix.1 = (f32[8,16,128]{2,1,0:T(8,128)S(1)}, f32[8,16,128]{2,1,0:T(8,128)S(1)}, f32[8,16,128]{2,1,0:T(8,128)S(1)}) custom-call(s32[5]{0:T(128)S(1)} %stack.42.place_ref, f32[8,16,128]{2,1,0:T(8,128)S(1)} %get-tuple-element.58.after_ref.r0, f32[8,16,128]{2,1,0:T(8,128)S(1)} %collective-permute-done.1.r1, f32[8,16,128]{2,1,0:T(8,128)S(1)} %collective-permute-done.2.r2, ...), custom_call_target="tpu_custom_call" | custom-call | flops 300000000 | bytes 1048576 | tf_op jit(solution)/shard_map/mix/pallas_call | solution.py:632
  29.4 1.6 %collective-permute-start.4 = (f32[8,16,128]{2,1,0:T(8,128)S(1)}, f32[8,16,128]{2,1,0:T(8,128)S(1)}, u32[]{:S(2)}, u32[]{:S(2)}) collective-permute-start(f32[8,16,128]{2,1,0:T(8,128)S(1)} %get-tuple-element.31), channel_id=1, source_target_pairs={{0,2},{2,0},{1,3},{3,1},{4,6},{6,4},{5,7},{7,5},{8,10},{10,8},{9,1... | collective-permute-start | bytes 196616 | tf_op jit(solution)/shard_map/ppermute | solution.py:532
  31.0 2.8 %collective-permute-done.4 = f32[8,16,128]{2,1,0:T(8,128)S(1)} collective-permute-done((f32[8,16,128]{2,1,0:T(8,128)S(1)}, f32[8,16,128]{2,1,0:T(8,128)S(1)}, u32[]{:S(2)}, u32[]{:S(2)}) %collective-permute-start.4) | collective-permute-done | bytes 65568 | tf_op jit(solution)/shard_map/ppermute | solution.py:532
  34.0 2.2 %collective-permute-start.6 = (f32[8,16,128]{2,1,0:T(8,128)S(1)}, f32[8,16,128]{2,1,0:T(8,128)S(1)}, u32[]{:S(2)}, u32[]{:S(2)}) collective-permute-start(f32[8,16,128]{2,1,0:T(8,128)S(1)} %add.221.refs_0_), channel_id=1, source_target_pairs={{8,0},{12,4},{0,8},{4,12},{9,1},{13,5},{1,9},{5,13},{10,2},{14,6},... | collective-permute-start | bytes 196616 | tf_op jit(solution)/shard_map/ppermute | solution.py:537
  36.2 2.2 %collective-permute-start.5 = (f32[8,16,128]{2,1,0:T(8,128)S(1)}, f32[8,16,128]{2,1,0:T(8,128)S(1)}, u32[]{:S(2)}, u32[]{:S(2)}) collective-permute-start(f32[8,16,128]{2,1,0:T(8,128)S(1)} %add.221.refs_0_), channel_id=1, source_target_pairs={{4,0},{8,4},{12,8},{0,12},{5,1},{9,5},{13,9},{1,13},{6,2},{10,6},{... | collective-permute-start | bytes 196616 | tf_op jit(solution)/shard_map/ppermute | solution.py:537
  38.6 1.4 %collective-permute-done.7.refs_3_ = f32[8,16,128]{2,1,0:T(8,128)S(1)} collective-permute-done((f32[8,16,128]{2,1,0:T(8,128)S(1)}, f32[8,16,128]{2,1,0:T(8,128)S(1)}, u32[]{:S(2)}, u32[]{:S(2)}) %collective-permute-start.7) | collective-permute-done | bytes 65568 | tf_op jit(solution)/shard_map/ppermute | solution.py:537
  40.0 1.2 %collective-permute-done.6.refs_2_ = f32[8,16,128]{2,1,0:T(8,128)S(1)} collective-permute-done((f32[8,16,128]{2,1,0:T(8,128)S(1)}, f32[8,16,128]{2,1,0:T(8,128)S(1)}, u32[]{:S(2)}, u32[]{:S(2)}) %collective-permute-start.6) | collective-permute-done | bytes 65568 | tf_op jit(solution)/shard_map/ppermute | solution.py:537
  42.6 26.9 %middle.1 = (f32[32,256,512]{2,1,0:T(8,128)}, f32[32,256,512]{2,1,0:T(8,128)S(1)}, f32[4,9,16,128]{3,2,1,0:T(8,128)S(1)}, f32[4,9,16,128]{3,2,1,0:T(8,128)S(1)}) custom-call(s32[5]{0:T(128)S(1)} %stack.42.place_ref, f32[32]{0:T(128)S(1)} %copy-done.2, f32[32]{0:T(128)S(1)} %copy-done.3, ...), custom_call_target="tpu_custom_call", output_to_operand_aliasing={{1}: (11, {})} | custom-call | flops 2000000000 | bytes 1048576 | tf_op jit(solution)/shard_map/middle/pallas_call | solution.py:647
  69.8 1.2 %collective-permute-done.12 = f32[4,9,16,128]{3,2,1,0:T(8,128)S(1)} collective-permute-done((f32[4,9,16,128]{3,2,1,0:T(8,128)S(1)}, f32[4,9,16,128]{3,2,1,0:T(8,128)S(1)}, u32[]{:S(2)}, u32[]{:S(2)}) %collective-permute-start.12) | collective-permute-done | bytes 294944 | tf_op jit(solution)/shard_map/ppermute | solution.py:532
  71.1 3.3 %collective-permute-start.15 = (f32[9,16,128]{2,1,0:T(8,128)S(1)}, f32[9,16,128]{2,1,0:T(8,128)S(1)}, u32[]{:S(2)}, u32[]{:S(2)}) collective-permute-start(f32[9,16,128]{2,1,0:T(8,128)S(1)} %get-tuple-element.49), channel_id=1, source_target_pairs={{0,12},{4,0},{8,4},{12,8},{1,13},{5,1},{9,5},{13,9},{2,14},{6,2},{... | collective-permute-start | bytes 221192 | tf_op jit(solution)/shard_map/ppermute | solution.py:542
  75.1 3.4 %prefetch.3.w_ref = f32[32,16,2,16,64]{4,3,2,1,0:T(8,128)S(1)} custom-call(f32[9,16,128]{2,1,0:T(8,128)S(1)} %get-tuple-element.36.after_ref, f32[32,256,512]{2,1,0:T(8,128)S(1)} %get-tuple-element.35.held_ref.refs_8_, f32[32,16,2,16,64]{4,3,2,1,0:T(8,128)} %bitcast.51), custom_call_target="tpu_custom_call" | custom-call | flops 400000000 | bytes 1048576 | tf_op jit(solution)/shard_map/prefetch/pallas_call | solution.py:486
  78.5 3.3 %collective-permute-done.14 = f32[9,16,128]{2,1,0:T(8,128)S(1)} collective-permute-done((f32[9,16,128]{2,1,0:T(8,128)S(1)}, f32[9,16,128]{2,1,0:T(8,128)S(1)}, u32[]{:S(2)}, u32[]{:S(2)}) %collective-permute-start.14) | collective-permute-done | bytes 73760 | tf_op jit(solution)/shard_map/ppermute | solution.py:542
  81.8 1.6 %collective-permute-start.16 = (f32[8,16,128]{2,1,0:T(8,128)S(1)}, f32[8,16,128]{2,1,0:T(8,128)S(1)}, u32[]{:S(2)}, u32[]{:S(2)}) collective-permute-start(f32[8,16,128]{2,1,0:T(8,128)S(1)} %slice.56.own_ref), channel_id=1, source_target_pairs={{0,2},{2,0},{1,3},{3,1},{4,6},{6,4},{5,7},{7,5},{8,10},{10,8},{9,1... | collective-permute-start | bytes 196616 | tf_op jit(solution)/shard_map/ppermute | solution.py:532
  83.4 2.8 %collective-permute-done.16.peer_ref = f32[8,16,128]{2,1,0:T(8,128)S(1)} collective-permute-done((f32[8,16,128]{2,1,0:T(8,128)S(1)}, f32[8,16,128]{2,1,0:T(8,128)S(1)}, u32[]{:S(2)}, u32[]{:S(2)}) %collective-permute-start.16) | collective-permute-done | bytes 65568 | tf_op jit(solution)/shard_map/ppermute | solution.py:532
  86.1 3.6 %back.1 = (f32[8,16,128]{2,1,0:T(8,128)S(1)}, f32[16,2,16,64]{3,2,1,0:T(8,128)S(1)}) custom-call(s32[5]{0:T(128)S(1)} %stack.42.place_ref, f32[8,16,128]{2,1,0:T(8,128)S(1)} %slice.56.own_ref, f32[8,16,128]{2,1,0:T(8,128)S(1)} %collective-permute-done.16.peer_ref, f32[32,16,2,16,64]{4,3,2,1,0:T(8,128)S(1)} %prefetch.3.w_ref, s32[2,64]{1,0:T(2,128)S(1)} %bitcast.49, ...), custom_call_target="tpu_custom_call" | custom-call | flops 300000000 | bytes 1048576 | tf_op jit(solution)/shard_map/back/pallas_call | solution.py:674
  90.0 2.2 %collective-permute-start.18 = (f32[8,16,128]{2,1,0:T(8,128)S(1)}, f32[8,16,128]{2,1,0:T(8,128)S(1)}, u32[]{:S(2)}, u32[]{:S(2)}) collective-permute-start(f32[8,16,128]{2,1,0:T(8,128)S(1)} %get-tuple-element.44.refs_0_), channel_id=1, source_target_pairs={{8,0},{12,4},{0,8},{4,12},{9,1},{13,5},{1,9},{5,13},{10,2},{14,6},... | collective-permute-start | bytes 196616 | tf_op jit(solution)/shard_map/ppermute | solution.py:537
  92.2 2.4 %collective-permute-start.17 = (f32[8,16,128]{2,1,0:T(8,128)S(1)}, f32[8,16,128]{2,1,0:T(8,128)S(1)}, u32[]{:S(2)}, u32[]{:S(2)}) collective-permute-start(f32[8,16,128]{2,1,0:T(8,128)S(1)} %get-tuple-element.44.refs_0_), channel_id=1, source_target_pairs={{4,0},{8,4},{12,8},{0,12},{5,1},{9,5},{13,9},{1,13},{6,2},{10,6},{... | collective-permute-start | bytes 196616 | tf_op jit(solution)/shard_map/ppermute | solution.py:537
  94.6 5.1 %outer.1 = f32[32,16,2,16,64]{4,3,2,1,0:T(8,128)} custom-call(s32[5]{0:T(128)S(1)} %stack.42.place_ref, f32[8,16,128]{2,1,0:T(8,128)S(1)} %get-tuple-element.42.spec_ref, f32[16,2,16,64]{3,2,1,0:T(8,128)S(1)} %get-tuple-element.43.gm_ref, s32[1,64]{1,0:T(1,128)S(1)} %bitcast.47, bf16[256,1024]{1,0:T(8,128)(2,1)S(1)} %fusion.pick_ref, ...), custom_call_target="tpu_custom_call" | custom-call | flops 400000000 | bytes 1048576 | tf_op jit(solution)/shard_map/outer/pallas_call | solution.py:686
  101.6 7.8 %last.1 = f32[32,256,512]{2,1,0:T(8,128)} custom-call(f32[32]{0:T(128)S(1)} %copy-done.2, f32[8,16,128]{2,1,0:T(8,128)S(1)} %get-tuple-element.44.refs_0_, f32[8,16,128]{2,1,0:T(8,128)S(1)} %collective-permute-done.17.refs_1_, f32[8,16,128]{2,1,0:T(8,128)S(1)} %collective-permute-done.18.refs_2_, f32[8,16,128]{2,1,0:T(8,128)S(1)} %collective-permute-done.19.refs_3_, ...), custom_call_target="tpu_custom_call" | custom-call | flops 700000000 | bytes 1048576 | tf_op jit(solution)/shard_map/last/pallas_call | solution.py:698
  (83 shorter events, 8.2 us)
Async XLA Ops:
  11.7 1.8 %collective-permute-start = (f32[4,8,16,128]{3,2,1,0:T(8,128)S(1)}, f32[4,8,16,128]{3,2,1,0:T(8,128)S(1)}, u32[]{:S(2)}, u32[]{:S(2)}) collective-permute-start(f32[4,8,16,128]{3,2,1,0:T(8,128)S(1)} %get-tuple-element.28), channel_id=1, source_target_pairs={{0,1},{1,0},{2,3},{3,2},{4,5},{5,4},{6,7},{7,6},{8,9},{9,8},{10,11... | collective-permute-start | bytes 786440 | tf_op jit(solution)/shard_map/ppermute | solution.py:532
  13.5 9.5 %collective-permute-start.3 = (f32[8,16,128]{2,1,0:T(8,128)S(1)}, f32[8,16,128]{2,1,0:T(8,128)S(1)}, u32[]{:S(2)}, u32[]{:S(2)}) collective-permute-start(f32[8,16,128]{2,1,0:T(8,128)S(1)} %get-tuple-element.55), channel_id=1, source_target_pairs={{0,12},{4,0},{8,4},{12,8},{1,13},{5,1},{9,5},{13,9},{2,14},{6,2},{... | collective-permute-start | bytes 196616 | tf_op jit(solution)/shard_map/ppermute | solution.py:542
  18.5 6.8 %collective-permute-start.2 = (f32[8,16,128]{2,1,0:T(8,128)S(1)}, f32[8,16,128]{2,1,0:T(8,128)S(1)}, u32[]{:S(2)}, u32[]{:S(2)}) collective-permute-start(f32[8,16,128]{2,1,0:T(8,128)S(1)} %get-tuple-element.56), channel_id=1, source_target_pairs={{0,8},{4,12},{8,0},{12,4},{1,9},{5,13},{9,1},{13,5},{2,10},{6,14},... | collective-permute-start | bytes 196616 | tf_op jit(solution)/shard_map/ppermute | solution.py:542
  18.5 6.8 %collective-permute-start.1 = (f32[8,16,128]{2,1,0:T(8,128)S(1)}, f32[8,16,128]{2,1,0:T(8,128)S(1)}, u32[]{:S(2)}, u32[]{:S(2)}) collective-permute-start(f32[8,16,128]{2,1,0:T(8,128)S(1)} %get-tuple-element.57), channel_id=1, source_target_pairs={{0,4},{4,8},{8,12},{12,0},{1,5},{5,9},{9,13},{13,1},{2,6},{6,10},{... | collective-permute-start | bytes 196616 | tf_op jit(solution)/shard_map/ppermute | solution.py:542
  29.4 4.3 %collective-permute-start.4 = (f32[8,16,128]{2,1,0:T(8,128)S(1)}, f32[8,16,128]{2,1,0:T(8,128)S(1)}, u32[]{:S(2)}, u32[]{:S(2)}) collective-permute-start(f32[8,16,128]{2,1,0:T(8,128)S(1)} %get-tuple-element.31), channel_id=1, source_target_pairs={{0,2},{2,0},{1,3},{3,1},{4,6},{6,4},{5,7},{7,5},{8,10},{10,8},{9,1... | collective-permute-start | bytes 196616 | tf_op jit(solution)/shard_map/ppermute | solution.py:532
  33.8 6.2 %collective-permute-start.7 = (f32[8,16,128]{2,1,0:T(8,128)S(1)}, f32[8,16,128]{2,1,0:T(8,128)S(1)}, u32[]{:S(2)}, u32[]{:S(2)}) collective-permute-start(f32[8,16,128]{2,1,0:T(8,128)S(1)} %add.221.refs_0_), channel_id=1, source_target_pairs={{12,0},{0,4},{4,8},{8,12},{13,1},{1,5},{5,9},{9,13},{14,2},{2,6},{... | collective-permute-start | bytes 196616 | tf_op jit(solution)/shard_map/ppermute | solution.py:537
  34.0 7.1 %collective-permute-start.6 = (f32[8,16,128]{2,1,0:T(8,128)S(1)}, f32[8,16,128]{2,1,0:T(8,128)S(1)}, u32[]{:S(2)}, u32[]{:S(2)}) collective-permute-start(f32[8,16,128]{2,1,0:T(8,128)S(1)} %add.221.refs_0_), channel_id=1, source_target_pairs={{8,0},{12,4},{0,8},{4,12},{9,1},{13,5},{1,9},{5,13},{10,2},{14,6},... | collective-permute-start | bytes 196616 | tf_op jit(solution)/shard_map/ppermute | solution.py:537
  36.2 4.9 %collective-permute-start.5 = (f32[8,16,128]{2,1,0:T(8,128)S(1)}, f32[8,16,128]{2,1,0:T(8,128)S(1)}, u32[]{:S(2)}, u32[]{:S(2)}) collective-permute-start(f32[8,16,128]{2,1,0:T(8,128)S(1)} %add.221.refs_0_), channel_id=1, source_target_pairs={{4,0},{8,4},{12,8},{0,12},{5,1},{9,5},{13,9},{1,13},{6,2},{10,6},{... | collective-permute-start | bytes 196616 | tf_op jit(solution)/shard_map/ppermute | solution.py:537
  38.5 3.2 %collective-permute-start.8 = (f32[8,16,128]{2,1,0:T(8,128)S(1)}, f32[8,16,128]{2,1,0:T(8,128)S(1)}, u32[]{:S(2)}, u32[]{:S(2)}) collective-permute-start(f32[8,16,128]{2,1,0:T(8,128)S(1)} %add.221.refs_0_), channel_id=1, source_target_pairs={{0,1},{1,0},{2,3},{3,2},{4,5},{5,4},{6,7},{7,6},{8,9},{9,8},{10,11... | collective-permute-start | bytes 196616 | tf_op jit(solution)/shard_map/ppermute | solution.py:532
  40.0 1.8 %collective-permute-start.11 = (f32[8,16,128]{2,1,0:T(8,128)S(1)}, f32[8,16,128]{2,1,0:T(8,128)S(1)}, u32[]{:S(2)}, u32[]{:S(2)}) collective-permute-start(f32[8,16,128]{2,1,0:T(8,128)S(1)} %collective-permute-done.7.refs_3_), channel_id=1, source_target_pairs={{0,1},{1,0},{2,3},{3,2},{4,5},{5,4},{6,7},{7,6},{8,9},{9,8},{10,11... | collective-permute-start | bytes 196616 | tf_op jit(solution)/shard_map/ppermute | solution.py:532
  41.1 1.3 %collective-permute-start.10 = (f32[8,16,128]{2,1,0:T(8,128)S(1)}, f32[8,16,128]{2,1,0:T(8,128)S(1)}, u32[]{:S(2)}, u32[]{:S(2)}) collective-permute-start(f32[8,16,128]{2,1,0:T(8,128)S(1)} %collective-permute-done.6.refs_2_), channel_id=1, source_target_pairs={{0,1},{1,0},{2,3},{3,2},{4,5},{5,4},{6,7},{7,6},{8,9},{9,8},{10,11... | collective-permute-start | bytes 196616 | tf_op jit(solution)/shard_map/ppermute | solution.py:532
  41.2 1.4 %collective-permute-start.9 = (f32[8,16,128]{2,1,0:T(8,128)S(1)}, f32[8,16,128]{2,1,0:T(8,128)S(1)}, u32[]{:S(2)}, u32[]{:S(2)}) collective-permute-start(f32[8,16,128]{2,1,0:T(8,128)S(1)} %collective-permute-done.5.refs_1_), channel_id=1, source_target_pairs={{0,1},{1,0},{2,3},{3,2},{4,5},{5,4},{6,7},{7,6},{8,9},{9,8},{10,11... | collective-permute-start | bytes 196616 | tf_op jit(solution)/shard_map/ppermute | solution.py:532
  69.5 1.6 %collective-permute-start.12 = (f32[4,9,16,128]{3,2,1,0:T(8,128)S(1)}, f32[4,9,16,128]{3,2,1,0:T(8,128)S(1)}, u32[]{:S(2)}, u32[]{:S(2)}) collective-permute-start(f32[4,9,16,128]{3,2,1,0:T(8,128)S(1)} %get-tuple-element.34), channel_id=1, source_target_pairs={{0,1},{1,0},{2,3},{3,2},{4,5},{5,4},{6,7},{7,6},{8,9},{9,8},{10,11... | collective-permute-start | bytes 884744 | tf_op jit(solution)/shard_map/ppermute | solution.py:532
  71.1 7.3 %collective-permute-start.15 = (f32[9,16,128]{2,1,0:T(8,128)S(1)}, f32[9,16,128]{2,1,0:T(8,128)S(1)}, u32[]{:S(2)}, u32[]{:S(2)}) collective-permute-start(f32[9,16,128]{2,1,0:T(8,128)S(1)} %get-tuple-element.49), channel_id=1, source_target_pairs={{0,12},{4,0},{8,4},{12,8},{1,13},{5,1},{9,5},{13,9},{2,14},{6,2},{... | collective-permute-start | bytes 221192 | tf_op jit(solution)/shard_map/ppermute | solution.py:542
  74.4 7.3 %collective-permute-start.14 = (f32[9,16,128]{2,1,0:T(8,128)S(1)}, f32[9,16,128]{2,1,0:T(8,128)S(1)}, u32[]{:S(2)}, u32[]{:S(2)}) collective-permute-start(f32[9,16,128]{2,1,0:T(8,128)S(1)} %get-tuple-element.50), channel_id=1, source_target_pairs={{0,8},{4,12},{8,0},{12,4},{1,9},{5,13},{9,1},{13,5},{2,10},{6,14},... | collective-permute-start | bytes 221192 | tf_op jit(solution)/shard_map/ppermute | solution.py:542
  74.4 7.3 %collective-permute-start.13 = (f32[9,16,128]{2,1,0:T(8,128)S(1)}, f32[9,16,128]{2,1,0:T(8,128)S(1)}, u32[]{:S(2)}, u32[]{:S(2)}) collective-permute-start(f32[9,16,128]{2,1,0:T(8,128)S(1)} %get-tuple-element.51), channel_id=1, source_target_pairs={{0,4},{4,8},{8,12},{12,0},{1,5},{5,9},{9,13},{13,1},{2,6},{6,10},{... | collective-permute-start | bytes 221192 | tf_op jit(solution)/shard_map/ppermute | solution.py:542
  81.8 4.3 %collective-permute-start.16 = (f32[8,16,128]{2,1,0:T(8,128)S(1)}, f32[8,16,128]{2,1,0:T(8,128)S(1)}, u32[]{:S(2)}, u32[]{:S(2)}) collective-permute-start(f32[8,16,128]{2,1,0:T(8,128)S(1)} %slice.56.own_ref), channel_id=1, source_target_pairs={{0,2},{2,0},{1,3},{3,1},{4,6},{6,4},{5,7},{7,5},{8,10},{10,8},{9,1... | collective-permute-start | bytes 196616 | tf_op jit(solution)/shard_map/ppermute | solution.py:532
  89.7 9.9 %collective-permute-start.19 = (f32[8,16,128]{2,1,0:T(8,128)S(1)}, f32[8,16,128]{2,1,0:T(8,128)S(1)}, u32[]{:S(2)}, u32[]{:S(2)}) collective-permute-start(f32[8,16,128]{2,1,0:T(8,128)S(1)} %get-tuple-element.44.refs_0_), channel_id=1, source_target_pairs={{12,0},{0,4},{4,8},{8,12},{13,1},{1,5},{5,9},{9,13},{14,2},{2,6},{... | collective-permute-start | bytes 196616 | tf_op jit(solution)/shard_map/ppermute | solution.py:537
  90.0 9.6 %collective-permute-start.18 = (f32[8,16,128]{2,1,0:T(8,128)S(1)}, f32[8,16,128]{2,1,0:T(8,128)S(1)}, u32[]{:S(2)}, u32[]{:S(2)}) collective-permute-start(f32[8,16,128]{2,1,0:T(8,128)S(1)} %get-tuple-element.44.refs_0_), channel_id=1, source_target_pairs={{8,0},{12,4},{0,8},{4,12},{9,1},{13,5},{1,9},{5,13},{10,2},{14,6},... | collective-permute-start | bytes 196616 | tf_op jit(solution)/shard_map/ppermute | solution.py:537
  92.2 7.4 %collective-permute-start.17 = (f32[8,16,128]{2,1,0:T(8,128)S(1)}, f32[8,16,128]{2,1,0:T(8,128)S(1)}, u32[]{:S(2)}, u32[]{:S(2)}) collective-permute-start(f32[8,16,128]{2,1,0:T(8,128)S(1)} %get-tuple-element.44.refs_0_), channel_id=1, source_target_pairs={{4,0},{8,4},{12,8},{0,12},{5,1},{9,5},{13,9},{1,13},{6,2},{10,6},{... | collective-permute-start | bytes 196616 | tf_op jit(solution)/shard_map/ppermute | solution.py:537
  99.6 1.6 %collective-permute-start.20 = (f32[8,16,128]{2,1,0:T(8,128)S(1)}, f32[8,16,128]{2,1,0:T(8,128)S(1)}, u32[]{:S(2)}, u32[]{:S(2)}) collective-permute-start(f32[8,16,128]{2,1,0:T(8,128)S(1)} %get-tuple-element.44.refs_0_), channel_id=1, source_target_pairs={{0,1},{1,0},{2,3},{3,2},{4,5},{5,4},{6,7},{7,6},{8,9},{9,8},{10,11... | collective-permute-start | bytes 196616 | tf_op jit(solution)/shard_map/ppermute | solution.py:532
  99.7 1.5 %collective-permute-start.21 = (f32[8,16,128]{2,1,0:T(8,128)S(1)}, f32[8,16,128]{2,1,0:T(8,128)S(1)}, u32[]{:S(2)}, u32[]{:S(2)}) collective-permute-start(f32[8,16,128]{2,1,0:T(8,128)S(1)} %collective-permute-done.17.refs_1_), channel_id=1, source_target_pairs={{0,1},{1,0},{2,3},{3,2},{4,5},{5,4},{6,7},{7,6},{8,9},{9,8},{10,11... | collective-permute-start | bytes 196616 | tf_op jit(solution)/shard_map/ppermute | solution.py:532
  100.2 1.3 %collective-permute-start.22 = (f32[8,16,128]{2,1,0:T(8,128)S(1)}, f32[8,16,128]{2,1,0:T(8,128)S(1)}, u32[]{:S(2)}, u32[]{:S(2)}) collective-permute-start(f32[8,16,128]{2,1,0:T(8,128)S(1)} %collective-permute-done.18.refs_2_), channel_id=1, source_target_pairs={{0,1},{1,0},{2,3},{3,2},{4,5},{5,4},{6,7},{7,6},{8,9},{9,8},{10,11... | collective-permute-start | bytes 196616 | tf_op jit(solution)/shard_map/ppermute | solution.py:532
  100.3 1.3 %collective-permute-start.23 = (f32[8,16,128]{2,1,0:T(8,128)S(1)}, f32[8,16,128]{2,1,0:T(8,128)S(1)}, u32[]{:S(2)}, u32[]{:S(2)}) collective-permute-start(f32[8,16,128]{2,1,0:T(8,128)S(1)} %collective-permute-done.19.refs_3_), channel_id=1, source_target_pairs={{0,1},{1,0},{2,3},{3,2},{4,5},{5,4},{6,7},{7,6},{8,9},{9,8},{10,11... | collective-permute-start | bytes 196616 | tf_op jit(solution)/shard_map/ppermute | solution.py:532
  (4 other events, 50.8 us)

commit v4 on v3

--- a/solution.py
+++ b/solution.py
@@ -232,6 +232,9 @@
         biases = [bias_ref[at * 4 + c] for c in range(4)]
         return preparing(piece_refs, at, fold_ref, inv_col_ref, wide_ref, ready, biases)
 
+    def transform(c):
+        part_ref[c] = mm(high_ref[c], col_ref[...]) + mm(low_ref[c], col_ref[...])
+
     def emit_group(at):
         return emitting(part_ref, row_ref, own_ref, other_ref, at, freq)
 
@@ -241,12 +244,14 @@
         for task in early + late:
             task()
         part_ref[...] = jnp.zeros_like(part_ref)
+        high_ref[3] = jnp.zeros_like(high_ref[3])
+        low_ref[3] = jnp.zeros_like(low_ref[3])
         own_ref[0, sums] = jnp.zeros(own_ref.shape[2:], F32)
 
     early, late = prepare_group(jnp.minimum(step + 1, last))
     emits = emit_group(jnp.maximum(step - 1, 0))
     chunks = rows // CHUNK
-    plan = {(0, 1): emits[0], (0, 5): emits[1], (0, 10): emits[2]}
+    plan = {(0, 2): emits[0], (0, 6): emits[1], (0, 11): emits[2]}
     for k, task in enumerate(early):
         plan[(1 + k // 4, 2 + 3 * (k % 4))] = task
     for k, task in enumerate(late):
@@ -266,7 +271,9 @@
             if k == 0 and c < 3:
                 branch[c + 1] = mm(inv_row_ref[...], ready[c + 1])
             if k == 1 and c > 0:
-                part_ref[c - 1] = mm(high_ref[c - 1], col_ref[...]) + mm(low_ref[c - 1], col_ref[...])
+                transform(c - 1)
+            if k == 0 and c == 0:
+                transform(3)
             x = x_ref[channel, r : r + CHUNK]
             v = branch[c, r : r + CHUNK] + skip * x
             q = v * v
@@ -284,11 +291,11 @@
         line = jnp.sum(gate, axis=0, keepdims=True)
         value = jnp.sum(sum(line[:, k : k + LANES] for k in range(0, cols, LANES)), axis=1, keepdims=True)
         tile = jnp.where((row == 0) & (lane == channel), jnp.broadcast_to(value, tile.shape), tile)
-    part_ref[3] = mm(high_ref[3], col_ref[...]) + mm(low_ref[3], col_ref[...])
     own_ref[0, sums] = tile
 
     @pl.when(step == last)
     def _():
+        transform(3)
         for task in emit_group(last):
             task()
         whole_sums = tile
@@ -550,7 +557,7 @@
 
 
 FORWARD_LIMIT = 16 << 20
-FORWARD_AHEAD = 2
+FORWARD_AHEAD = 3
 MIX_LIMIT = 16 << 20
 MIDDLE_LIMIT = 24 << 20
 LAST_LIMIT = 28 << 20

time: 110 us -> 108 us (0.982)
  Pallas kernels: 63.9 us -> 62.2 us
    pallas_call x1, Pallas kernels: 26.9 us -> 25.3 us  [fast_local(): pl.pallas_call(functools.partial(middle_kernel, pieces=len(pieces), freq=...]
where the time goes in v4:
time: 108 us
  Pallas kernels  62.2 us (58%)
  starting transfers between devices  25.1 us (23%)
  waiting for transfers between devices  16.1 us (15%)
  other arithmetic  2.28 us (2%)
    pallas_call x1, Pallas kernels, fast_local(): pl.pallas_call(functools.partial(middle_kernel, pieces=len(pieces), freq=...  25.3 us
    ppermute x6, starting transfers between devices, send(): return lax.ppermute(x, name, [(i, (i + distance) % n) for i in range(n)])  9.9 us
    pallas_call x1, Pallas kernels, fast_local(): pl.pallas_call(functools.partial(forward_kernel, freq=geo.freq), grid=(gr...  9.65 us
    ppermute x6, starting transfers between devices, fetch(): return lax.ppermute(x, name, [((i + distance) % n, i) for i in range(n)])  9.53 us
    ppermute x12, waiting for transfers between devices, swap(): return lax.ppermute(x, name, [(i, (i + 1) % n) for i in range(n)])  7.96 us
    pallas_call x1, Pallas kernels, fast_local(): pl.pallas_call(functools.partial(last_kernel, pieces=len(pieces)), grid=(...  7.76 us
    pallas_call x2, Pallas kernels, prefetch(): pl.pallas_call(prefetch_kernel, in_specs=[anywhere] * 3, out_specs=anywhe...  6.79 us
    ppermute x12, starting transfers between devices, swap(): return lax.ppermute(x, name, [(i, (i + 1) % n) for i in range(n)])  5.68 us
  transfers between devices with their start and end apart: 24, of which 11 were waited for; matrix products, arithmetic and copies ran while one was open for 2% of the time, Pallas kernels for 11%

profile of v4, /device:TPU:0, one launch (start us, length us, event | category | flops | bytes accessed | tf_op | source)
XLA Modules:
  0.0 107.7 jit_solution(413694494743950597)
XLA Ops:
  2.0 9.7 %forward.1 = (f32[4,8,16,128]{3,2,1,0:T(8,128)S(1)}, f32[4,8,16,128]{3,2,1,0:T(8,128)S(1)}, f32[32,256,512]{2,1,0:T(8,128)S(1)}) custom-call(s32[5]{0:T(128)S(1)} %stack.42.place_ref, f32[32,256,512]{2,1,0:T(8,128)} %x_ref.1, bf16[512,128]{1,0:T(8,128)(2,1)S(1)} %copy.13.col_ref.refs_13_, bf16[256,256]{1,0:T(8,128)(2,1)S(1)} %pad_maximum_fusion.4.row_ref.refs_14_), custom_call_target="tpu_custom_call" | custom-call | flops 600000000 | bytes 1048576 | tf_op jit(solution)/shard_map/forward/pallas_call | solution.py:615
  13.5 5.0 %collective-permute-start.3 = (f32[8,16,128]{2,1,0:T(8,128)S(1)}, f32[8,16,128]{2,1,0:T(8,128)S(1)}, u32[]{:S(2)}, u32[]{:S(2)}) collective-permute-start(f32[8,16,128]{2,1,0:T(8,128)S(1)} %get-tuple-element.55), channel_id=1, source_target_pairs={{0,12},{4,0},{8,4},{12,8},{1,13},{5,1},{9,5},{13,9},{2,14},{6,2},{... | collective-permute-start | bytes 196616 | tf_op jit(solution)/shard_map/ppermute | solution.py:549
  18.5 1.0 collective-permute-start.1
  19.5 3.4 %prefetch.2.w_ref = f32[32,16,2,16,64]{4,3,2,1,0:T(8,128)S(1)} custom-call(f32[8,16,128]{2,1,0:T(8,128)S(1)} %get-tuple-element.58.after_ref.r0, f32[32,256,512]{2,1,0:T(8,128)S(1)} %get-tuple-element.29.held_ref.refs_8_, f32[32,16,2,16,64]{4,3,2,1,0:T(8,128)} %bitcast.50), custom_call_target="tpu_custom_call" | custom-call | flops 400000000 | bytes 1048576 | tf_op jit(solution)/shard_map/prefetch/pallas_call | solution.py:493
  23.0 2.3 %collective-permute-done.2.r2 = f32[8,16,128]{2,1,0:T(8,128)S(1)} collective-permute-done((f32[8,16,128]{2,1,0:T(8,128)S(1)}, f32[8,16,128]{2,1,0:T(8,128)S(1)}, u32[]{:S(2)}, u32[]{:S(2)}) %collective-permute-start.2) | collective-permute-done | bytes 65568 | tf_op jit(solution)/shard_map/ppermute | solution.py:549
  25.3 4.1 %mix.1 = (f32[8,16,128]{2,1,0:T(8,128)S(1)}, f32[8,16,128]{2,1,0:T(8,128)S(1)}, f32[8,16,128]{2,1,0:T(8,128)S(1)}) custom-call(s32[5]{0:T(128)S(1)} %stack.42.place_ref, f32[8,16,128]{2,1,0:T(8,128)S(1)} %get-tuple-element.58.after_ref.r0, f32[8,16,128]{2,1,0:T(8,128)S(1)} %collective-permute-done.1.r1, f32[8,16,128]{2,1,0:T(8,128)S(1)} %collective-permute-done.2.r2, ...), custom_call_target="tpu_custom_call" | custom-call | flops 300000000 | bytes 1048576 | tf_op jit(solution)/shard_map/mix/pallas_call | solution.py:639
  29.4 1.6 %collective-permute-start.4 = (f32[8,16,128]{2,1,0:T(8,128)S(1)}, f32[8,16,128]{2,1,0:T(8,128)S(1)}, u32[]{:S(2)}, u32[]{:S(2)}) collective-permute-start(f32[8,16,128]{2,1,0:T(8,128)S(1)} %get-tuple-element.31), channel_id=1, source_target_pairs={{0,2},{2,0},{1,3},{3,1},{4,6},{6,4},{5,7},{7,5},{8,10},{10,8},{9,1... | collective-permute-start | bytes 196616 | tf_op jit(solution)/shard_map/ppermute | solution.py:539
  31.0 2.8 %collective-permute-done.4 = f32[8,16,128]{2,1,0:T(8,128)S(1)} collective-permute-done((f32[8,16,128]{2,1,0:T(8,128)S(1)}, f32[8,16,128]{2,1,0:T(8,128)S(1)}, u32[]{:S(2)}, u32[]{:S(2)}) %collective-permute-start.4) | collective-permute-done | bytes 65568 | tf_op jit(solution)/shard_map/ppermute | solution.py:539
  34.0 2.2 %collective-permute-start.6 = (f32[8,16,128]{2,1,0:T(8,128)S(1)}, f32[8,16,128]{2,1,0:T(8,128)S(1)}, u32[]{:S(2)}, u32[]{:S(2)}) collective-permute-start(f32[8,16,128]{2,1,0:T(8,128)S(1)} %add.221.refs_0_), channel_id=1, source_target_pairs={{8,0},{12,4},{0,8},{4,12},{9,1},{13,5},{1,9},{5,13},{10,2},{14,6},... | collective-permute-start | bytes 196616 | tf_op jit(solution)/shard_map/ppermute | solution.py:544
  36.2 2.2 %collective-permute-start.5 = (f32[8,16,128]{2,1,0:T(8,128)S(1)}, f32[8,16,128]{2,1,0:T(8,128)S(1)}, u32[]{:S(2)}, u32[]{:S(2)}) collective-permute-start(f32[8,16,128]{2,1,0:T(8,128)S(1)} %add.221.refs_0_), channel_id=1, source_target_pairs={{4,0},{8,4},{12,8},{0,12},{5,1},{9,5},{13,9},{1,13},{6,2},{10,6},{... | collective-permute-start | bytes 196616 | tf_op jit(solution)/shard_map/ppermute | solution.py:544
  38.6 1.4 %collective-permute-done.7.refs_3_ = f32[8,16,128]{2,1,0:T(8,128)S(1)} collective-permute-done((f32[8,16,128]{2,1,0:T(8,128)S(1)}, f32[8,16,128]{2,1,0:T(8,128)S(1)}, u32[]{:S(2)}, u32[]{:S(2)}) %collective-permute-start.7) | collective-permute-done | bytes 65568 | tf_op jit(solution)/shard_map/ppermute | solution.py:544
  40.0 1.2 %collective-permute-done.6.refs_2_ = f32[8,16,128]{2,1,0:T(8,128)S(1)} collective-permute-done((f32[8,16,128]{2,1,0:T(8,128)S(1)}, f32[8,16,128]{2,1,0:T(8,128)S(1)}, u32[]{:S(2)}, u32[]{:S(2)}) %collective-permute-start.6) | collective-permute-done | bytes 65568 | tf_op jit(solution)/shard_map/ppermute | solution.py:544
  42.6 25.3 %middle.1 = (f32[32,256,512]{2,1,0:T(8,128)}, f32[32,256,512]{2,1,0:T(8,128)S(1)}, f32[4,9,16,128]{3,2,1,0:T(8,128)S(1)}, f32[4,9,16,128]{3,2,1,0:T(8,128)S(1)}) custom-call(s32[5]{0:T(128)S(1)} %stack.42.place_ref, f32[32]{0:T(128)S(1)} %copy-done.2, f32[32]{0:T(128)S(1)} %copy-done.3, ...), custom_call_target="tpu_custom_call", output_to_operand_aliasing={{1}: (11, {})} | custom-call | flops 2000000000 | bytes 1048576 | tf_op jit(solution)/shard_map/middle/pallas_call | solution.py:654
  68.2 1.2 %collective-permute-done.12 = f32[4,9,16,128]{3,2,1,0:T(8,128)S(1)} collective-permute-done((f32[4,9,16,128]{3,2,1,0:T(8,128)S(1)}, f32[4,9,16,128]{3,2,1,0:T(8,128)S(1)}, u32[]{:S(2)}, u32[]{:S(2)}) %collective-permute-start.12) | collective-permute-done | bytes 294944 | tf_op jit(solution)/shard_map/ppermute | solution.py:539
  69.5 3.3 %collective-permute-start.15 = (f32[9,16,128]{2,1,0:T(8,128)S(1)}, f32[9,16,128]{2,1,0:T(8,128)S(1)}, u32[]{:S(2)}, u32[]{:S(2)}) collective-permute-start(f32[9,16,128]{2,1,0:T(8,128)S(1)} %get-tuple-element.49), channel_id=1, source_target_pairs={{0,12},{4,0},{8,4},{12,8},{1,13},{5,1},{9,5},{13,9},{2,14},{6,2},{... | collective-permute-start | bytes 221192 | tf_op jit(solution)/shard_map/ppermute | solution.py:549
  73.4 3.4 %prefetch.3.w_ref = f32[32,16,2,16,64]{4,3,2,1,0:T(8,128)S(1)} custom-call(f32[9,16,128]{2,1,0:T(8,128)S(1)} %get-tuple-element.36.after_ref, f32[32,256,512]{2,1,0:T(8,128)S(1)} %get-tuple-element.35.held_ref.refs_8_, f32[32,16,2,16,64]{4,3,2,1,0:T(8,128)} %bitcast.51), custom_call_target="tpu_custom_call" | custom-call | flops 400000000 | bytes 1048576 | tf_op jit(solution)/shard_map/prefetch/pallas_call | solution.py:493
  76.8 3.3 %collective-permute-done.14 = f32[9,16,128]{2,1,0:T(8,128)S(1)} collective-permute-done((f32[9,16,128]{2,1,0:T(8,128)S(1)}, f32[9,16,128]{2,1,0:T(8,128)S(1)}, u32[]{:S(2)}, u32[]{:S(2)}) %collective-permute-start.14) | collective-permute-done | bytes 73760 | tf_op jit(solution)/shard_map/ppermute | solution.py:549
  80.1 1.6 %collective-permute-start.16 = (f32[8,16,128]{2,1,0:T(8,128)S(1)}, f32[8,16,128]{2,1,0:T(8,128)S(1)}, u32[]{:S(2)}, u32[]{:S(2)}) collective-permute-start(f32[8,16,128]{2,1,0:T(8,128)S(1)} %slice.56.own_ref), channel_id=1, source_target_pairs={{0,2},{2,0},{1,3},{3,1},{4,6},{6,4},{5,7},{7,5},{8,10},{10,8},{9,1... | collective-permute-start | bytes 196616 | tf_op jit(solution)/shard_map/ppermute | solution.py:539
  81.7 2.8 %collective-permute-done.16.peer_ref = f32[8,16,128]{2,1,0:T(8,128)S(1)} collective-permute-done((f32[8,16,128]{2,1,0:T(8,128)S(1)}, f32[8,16,128]{2,1,0:T(8,128)S(1)}, u32[]{:S(2)}, u32[]{:S(2)}) %collective-permute-start.16) | collective-permute-done | bytes 65568 | tf_op jit(solution)/shard_map/ppermute | solution.py:539
  84.5 3.6 %back.1 = (f32[8,16,128]{2,1,0:T(8,128)S(1)}, f32[16,2,16,64]{3,2,1,0:T(8,128)S(1)}) custom-call(s32[5]{0:T(128)S(1)} %stack.42.place_ref, f32[8,16,128]{2,1,0:T(8,128)S(1)} %slice.56.own_ref, f32[8,16,128]{2,1,0:T(8,128)S(1)} %collective-permute-done.16.peer_ref, f32[32,16,2,16,64]{4,3,2,1,0:T(8,128)S(1)} %prefetch.3.w_ref, s32[2,64]{1,0:T(2,128)S(1)} %bitcast.49, ...), custom_call_target="tpu_custom_call" | custom-call | flops 300000000 | bytes 1048576 | tf_op jit(solution)/shard_map/back/pallas_call | solution.py:681
  88.3 2.2 %collective-permute-start.18 = (f32[8,16,128]{2,1,0:T(8,128)S(1)}, f32[8,16,128]{2,1,0:T(8,128)S(1)}, u32[]{:S(2)}, u32[]{:S(2)}) collective-permute-start(f32[8,16,128]{2,1,0:T(8,128)S(1)} %get-tuple-element.44.refs_0_), channel_id=1, source_target_pairs={{8,0},{12,4},{0,8},{4,12},{9,1},{13,5},{1,9},{5,13},{10,2},{14,6},... | collective-permute-start | bytes 196616 | tf_op jit(solution)/shard_map/ppermute | solution.py:544
  90.5 2.4 %collective-permute-start.17 = (f32[8,16,128]{2,1,0:T(8,128)S(1)}, f32[8,16,128]{2,1,0:T(8,128)S(1)}, u32[]{:S(2)}, u32[]{:S(2)}) collective-permute-start(f32[8,16,128]{2,1,0:T(8,128)S(1)} %get-tuple-element.44.refs_0_), channel_id=1, source_target_pairs={{4,0},{8,4},{12,8},{0,12},{5,1},{9,5},{13,9},{1,13},{6,2},{10,6},{... | collective-permute-start | bytes 196616 | tf_op jit(solution)/shard_map/ppermute | solution.py:544
  92.9 5.1 %outer.1 = f32[32,16,2,16,64]{4,3,2,1,0:T(8,128)} custom-call(s32[5]{0:T(128)S(1)} %stack.42.place_ref, f32[8,16,128]{2,1,0:T(8,128)S(1)} %get-tuple-element.42.spec_ref, f32[16,2,16,64]{3,2,1,0:T(8,128)S(1)} %get-tuple-element.43.gm_ref, s32[1,64]{1,0:T(1,128)S(1)} %bitcast.47, bf16[256,1024]{1,0:T(8,128)(2,1)S(1)} %fusion.pick_ref, ...), custom_call_target="tpu_custom_call" | custom-call | flops 400000000 | bytes 1048576 | tf_op jit(solution)/shard_map/outer/pallas_call | solution.py:693
  99.9 7.8 %last.1 = f32[32,256,512]{2,1,0:T(8,128)} custom-call(f32[32]{0:T(128)S(1)} %copy-done.2, f32[8,16,128]{2,1,0:T(8,128)S(1)} %get-tuple-element.44.refs_0_, f32[8,16,128]{2,1,0:T(8,128)S(1)} %collective-permute-done.17.refs_1_, f32[8,16,128]{2,1,0:T(8,128)S(1)} %collective-permute-done.18.refs_2_, f32[8,16,128]{2,1,0:T(8,128)S(1)} %collective-permute-done.19.refs_3_, ...), custom_call_target="tpu_custom_call" | custom-call | flops 700000000 | bytes 1048576 | tf_op jit(solution)/shard_map/last/pallas_call | solution.py:705
  (83 shorter events, 8.2 us)
Async XLA Ops:
  11.7 1.8 %collective-permute-start = (f32[4,8,16,128]{3,2,1,0:T(8,128)S(1)}, f32[4,8,16,128]{3,2,1,0:T(8,128)S(1)}, u32[]{:S(2)}, u32[]{:S(2)}) collective-permute-start(f32[4,8,16,128]{3,2,1,0:T(8,128)S(1)} %get-tuple-element.28), channel_id=1, source_target_pairs={{0,1},{1,0},{2,3},{3,2},{4,5},{5,4},{6,7},{7,6},{8,9},{9,8},{10,11... | collective-permute-start | bytes 786440 | tf_op jit(solution)/shard_map/ppermute | solution.py:539
  13.5 9.5 %collective-permute-start.3 = (f32[8,16,128]{2,1,0:T(8,128)S(1)}, f32[8,16,128]{2,1,0:T(8,128)S(1)}, u32[]{:S(2)}, u32[]{:S(2)}) collective-permute-start(f32[8,16,128]{2,1,0:T(8,128)S(1)} %get-tuple-element.55), channel_id=1, source_target_pairs={{0,12},{4,0},{8,4},{12,8},{1,13},{5,1},{9,5},{13,9},{2,14},{6,2},{... | collective-permute-start | bytes 196616 | tf_op jit(solution)/shard_map/ppermute | solution.py:549
  18.5 6.8 %collective-permute-start.2 = (f32[8,16,128]{2,1,0:T(8,128)S(1)}, f32[8,16,128]{2,1,0:T(8,128)S(1)}, u32[]{:S(2)}, u32[]{:S(2)}) collective-permute-start(f32[8,16,128]{2,1,0:T(8,128)S(1)} %get-tuple-element.56), channel_id=1, source_target_pairs={{0,8},{4,12},{8,0},{12,4},{1,9},{5,13},{9,1},{13,5},{2,10},{6,14},... | collective-permute-start | bytes 196616 | tf_op jit(solution)/shard_map/ppermute | solution.py:549
  18.5 6.8 %collective-permute-start.1 = (f32[8,16,128]{2,1,0:T(8,128)S(1)}, f32[8,16,128]{2,1,0:T(8,128)S(1)}, u32[]{:S(2)}, u32[]{:S(2)}) collective-permute-start(f32[8,16,128]{2,1,0:T(8,128)S(1)} %get-tuple-element.57), channel_id=1, source_target_pairs={{0,4},{4,8},{8,12},{12,0},{1,5},{5,9},{9,13},{13,1},{2,6},{6,10},{... | collective-permute-start | bytes 196616 | tf_op jit(solution)/shard_map/ppermute | solution.py:549
  29.4 4.3 %collective-permute-start.4 = (f32[8,16,128]{2,1,0:T(8,128)S(1)}, f32[8,16,128]{2,1,0:T(8,128)S(1)}, u32[]{:S(2)}, u32[]{:S(2)}) collective-permute-start(f32[8,16,128]{2,1,0:T(8,128)S(1)} %get-tuple-element.31), channel_id=1, source_target_pairs={{0,2},{2,0},{1,3},{3,1},{4,6},{6,4},{5,7},{7,5},{8,10},{10,8},{9,1... | collective-permute-start | bytes 196616 | tf_op jit(solution)/shard_map/ppermute | solution.py:539
  33.7 6.2 %collective-permute-start.7 = (f32[8,16,128]{2,1,0:T(8,128)S(1)}, f32[8,16,128]{2,1,0:T(8,128)S(1)}, u32[]{:S(2)}, u32[]{:S(2)}) collective-permute-start(f32[8,16,128]{2,1,0:T(8,128)S(1)} %add.221.refs_0_), channel_id=1, source_target_pairs={{12,0},{0,4},{4,8},{8,12},{13,1},{1,5},{5,9},{9,13},{14,2},{2,6},{... | collective-permute-start | bytes 196616 | tf_op jit(solution)/shard_map/ppermute | solution.py:544
  34.0 7.2 %collective-permute-start.6 = (f32[8,16,128]{2,1,0:T(8,128)S(1)}, f32[8,16,128]{2,1,0:T(8,128)S(1)}, u32[]{:S(2)}, u32[]{:S(2)}) collective-permute-start(f32[8,16,128]{2,1,0:T(8,128)S(1)} %add.221.refs_0_), channel_id=1, source_target_pairs={{8,0},{12,4},{0,8},{4,12},{9,1},{13,5},{1,9},{5,13},{10,2},{14,6},... | collective-permute-start | bytes 196616 | tf_op jit(solution)/shard_map/ppermute | solution.py:544
  36.2 4.9 %collective-permute-start.5 = (f32[8,16,128]{2,1,0:T(8,128)S(1)}, f32[8,16,128]{2,1,0:T(8,128)S(1)}, u32[]{:S(2)}, u32[]{:S(2)}) collective-permute-start(f32[8,16,128]{2,1,0:T(8,128)S(1)} %add.221.refs_0_), channel_id=1, source_target_pairs={{4,0},{8,4},{12,8},{0,12},{5,1},{9,5},{13,9},{1,13},{6,2},{10,6},{... | collective-permute-start | bytes 196616 | tf_op jit(solution)/shard_map/ppermute | solution.py:544
  38.5 3.2 %collective-permute-start.8 = (f32[8,16,128]{2,1,0:T(8,128)S(1)}, f32[8,16,128]{2,1,0:T(8,128)S(1)}, u32[]{:S(2)}, u32[]{:S(2)}) collective-permute-start(f32[8,16,128]{2,1,0:T(8,128)S(1)} %add.221.refs_0_), channel_id=1, source_target_pairs={{0,1},{1,0},{2,3},{3,2},{4,5},{5,4},{6,7},{7,6},{8,9},{9,8},{10,11... | collective-permute-start | bytes 196616 | tf_op jit(solution)/shard_map/ppermute | solution.py:539
  40.0 1.8 %collective-permute-start.11 = (f32[8,16,128]{2,1,0:T(8,128)S(1)}, f32[8,16,128]{2,1,0:T(8,128)S(1)}, u32[]{:S(2)}, u32[]{:S(2)}) collective-permute-start(f32[8,16,128]{2,1,0:T(8,128)S(1)} %collective-permute-done.7.refs_3_), channel_id=1, source_target_pairs={{0,1},{1,0},{2,3},{3,2},{4,5},{5,4},{6,7},{7,6},{8,9},{9,8},{10,11... | collective-permute-start | bytes 196616 | tf_op jit(solution)/shard_map/ppermute | solution.py:539
  41.1 1.3 %collective-permute-start.10 = (f32[8,16,128]{2,1,0:T(8,128)S(1)}, f32[8,16,128]{2,1,0:T(8,128)S(1)}, u32[]{:S(2)}, u32[]{:S(2)}) collective-permute-start(f32[8,16,128]{2,1,0:T(8,128)S(1)} %collective-permute-done.6.refs_2_), channel_id=1, source_target_pairs={{0,1},{1,0},{2,3},{3,2},{4,5},{5,4},{6,7},{7,6},{8,9},{9,8},{10,11... | collective-permute-start | bytes 196616 | tf_op jit(solution)/shard_map/ppermute | solution.py:539
  41.1 1.4 %collective-permute-start.9 = (f32[8,16,128]{2,1,0:T(8,128)S(1)}, f32[8,16,128]{2,1,0:T(8,128)S(1)}, u32[]{:S(2)}, u32[]{:S(2)}) collective-permute-start(f32[8,16,128]{2,1,0:T(8,128)S(1)} %collective-permute-done.5.refs_1_), channel_id=1, source_target_pairs={{0,1},{1,0},{2,3},{3,2},{4,5},{5,4},{6,7},{7,6},{8,9},{9,8},{10,11... | collective-permute-start | bytes 196616 | tf_op jit(solution)/shard_map/ppermute | solution.py:539
  67.8 1.6 %collective-permute-start.12 = (f32[4,9,16,128]{3,2,1,0:T(8,128)S(1)}, f32[4,9,16,128]{3,2,1,0:T(8,128)S(1)}, u32[]{:S(2)}, u32[]{:S(2)}) collective-permute-start(f32[4,9,16,128]{3,2,1,0:T(8,128)S(1)} %get-tuple-element.34), channel_id=1, source_target_pairs={{0,1},{1,0},{2,3},{3,2},{4,5},{5,4},{6,7},{7,6},{8,9},{9,8},{10,11... | collective-permute-start | bytes 884744 | tf_op jit(solution)/shard_map/ppermute | solution.py:539
  69.5 7.3 %collective-permute-start.15 = (f32[9,16,128]{2,1,0:T(8,128)S(1)}, f32[9,16,128]{2,1,0:T(8,128)S(1)}, u32[]{:S(2)}, u32[]{:S(2)}) collective-permute-start(f32[9,16,128]{2,1,0:T(8,128)S(1)} %get-tuple-element.49), channel_id=1, source_target_pairs={{0,12},{4,0},{8,4},{12,8},{1,13},{5,1},{9,5},{13,9},{2,14},{6,2},{... | collective-permute-start | bytes 221192 | tf_op jit(solution)/shard_map/ppermute | solution.py:549
  72.7 7.3 %collective-permute-start.14 = (f32[9,16,128]{2,1,0:T(8,128)S(1)}, f32[9,16,128]{2,1,0:T(8,128)S(1)}, u32[]{:S(2)}, u32[]{:S(2)}) collective-permute-start(f32[9,16,128]{2,1,0:T(8,128)S(1)} %get-tuple-element.50), channel_id=1, source_target_pairs={{0,8},{4,12},{8,0},{12,4},{1,9},{5,13},{9,1},{13,5},{2,10},{6,14},... | collective-permute-start | bytes 221192 | tf_op jit(solution)/shard_map/ppermute | solution.py:549
  72.7 7.3 %collective-permute-start.13 = (f32[9,16,128]{2,1,0:T(8,128)S(1)}, f32[9,16,128]{2,1,0:T(8,128)S(1)}, u32[]{:S(2)}, u32[]{:S(2)}) collective-permute-start(f32[9,16,128]{2,1,0:T(8,128)S(1)} %get-tuple-element.51), channel_id=1, source_target_pairs={{0,4},{4,8},{8,12},{12,0},{1,5},{5,9},{9,13},{13,1},{2,6},{6,10},{... | collective-permute-start | bytes 221192 | tf_op jit(solution)/shard_map/ppermute | solution.py:549
  80.1 4.3 %collective-permute-start.16 = (f32[8,16,128]{2,1,0:T(8,128)S(1)}, f32[8,16,128]{2,1,0:T(8,128)S(1)}, u32[]{:S(2)}, u32[]{:S(2)}) collective-permute-start(f32[8,16,128]{2,1,0:T(8,128)S(1)} %slice.56.own_ref), channel_id=1, source_target_pairs={{0,2},{2,0},{1,3},{3,1},{4,6},{6,4},{5,7},{7,5},{8,10},{10,8},{9,1... | collective-permute-start | bytes 196616 | tf_op jit(solution)/shard_map/ppermute | solution.py:539
  88.1 9.9 %collective-permute-start.19 = (f32[8,16,128]{2,1,0:T(8,128)S(1)}, f32[8,16,128]{2,1,0:T(8,128)S(1)}, u32[]{:S(2)}, u32[]{:S(2)}) collective-permute-start(f32[8,16,128]{2,1,0:T(8,128)S(1)} %get-tuple-element.44.refs_0_), channel_id=1, source_target_pairs={{12,0},{0,4},{4,8},{8,12},{13,1},{1,5},{5,9},{9,13},{14,2},{2,6},{... | collective-permute-start | bytes 196616 | tf_op jit(solution)/shard_map/ppermute | solution.py:544
  88.3 9.6 %collective-permute-start.18 = (f32[8,16,128]{2,1,0:T(8,128)S(1)}, f32[8,16,128]{2,1,0:T(8,128)S(1)}, u32[]{:S(2)}, u32[]{:S(2)}) collective-permute-start(f32[8,16,128]{2,1,0:T(8,128)S(1)} %get-tuple-element.44.refs_0_), channel_id=1, source_target_pairs={{8,0},{12,4},{0,8},{4,12},{9,1},{13,5},{1,9},{5,13},{10,2},{14,6},... | collective-permute-start | bytes 196616 | tf_op jit(solution)/shard_map/ppermute | solution.py:544
  90.5 7.4 %collective-permute-start.17 = (f32[8,16,128]{2,1,0:T(8,128)S(1)}, f32[8,16,128]{2,1,0:T(8,128)S(1)}, u32[]{:S(2)}, u32[]{:S(2)}) collective-permute-start(f32[8,16,128]{2,1,0:T(8,128)S(1)} %get-tuple-element.44.refs_0_), channel_id=1, source_target_pairs={{4,0},{8,4},{12,8},{0,12},{5,1},{9,5},{13,9},{1,13},{6,2},{10,6},{... | collective-permute-start | bytes 196616 | tf_op jit(solution)/shard_map/ppermute | solution.py:544
  98.0 1.6 %collective-permute-start.20 = (f32[8,16,128]{2,1,0:T(8,128)S(1)}, f32[8,16,128]{2,1,0:T(8,128)S(1)}, u32[]{:S(2)}, u32[]{:S(2)}) collective-permute-start(f32[8,16,128]{2,1,0:T(8,128)S(1)} %get-tuple-element.44.refs_0_), channel_id=1, source_target_pairs={{0,1},{1,0},{2,3},{3,2},{4,5},{5,4},{6,7},{7,6},{8,9},{9,8},{10,11... | collective-permute-start | bytes 196616 | tf_op jit(solution)/shard_map/ppermute | solution.py:539
  98.0 1.5 %collective-permute-start.21 = (f32[8,16,128]{2,1,0:T(8,128)S(1)}, f32[8,16,128]{2,1,0:T(8,128)S(1)}, u32[]{:S(2)}, u32[]{:S(2)}) collective-permute-start(f32[8,16,128]{2,1,0:T(8,128)S(1)} %collective-permute-done.17.refs_1_), channel_id=1, source_target_pairs={{0,1},{1,0},{2,3},{3,2},{4,5},{5,4},{6,7},{7,6},{8,9},{9,8},{10,11... | collective-permute-start | bytes 196616 | tf_op jit(solution)/shard_map/ppermute | solution.py:539
  98.5 1.3 %collective-permute-start.22 = (f32[8,16,128]{2,1,0:T(8,128)S(1)}, f32[8,16,128]{2,1,0:T(8,128)S(1)}, u32[]{:S(2)}, u32[]{:S(2)}) collective-permute-start(f32[8,16,128]{2,1,0:T(8,128)S(1)} %collective-permute-done.18.refs_2_), channel_id=1, source_target_pairs={{0,1},{1,0},{2,3},{3,2},{4,5},{5,4},{6,7},{7,6},{8,9},{9,8},{10,11... | collective-permute-start | bytes 196616 | tf_op jit(solution)/shard_map/ppermute | solution.py:539
  98.6 1.3 %collective-permute-start.23 = (f32[8,16,128]{2,1,0:T(8,128)S(1)}, f32[8,16,128]{2,1,0:T(8,128)S(1)}, u32[]{:S(2)}, u32[]{:S(2)}) collective-permute-start(f32[8,16,128]{2,1,0:T(8,128)S(1)} %collective-permute-done.19.refs_3_), channel_id=1, source_target_pairs={{0,1},{1,0},{2,3},{3,2},{4,5},{5,4},{6,7},{7,6},{8,9},{9,8},{10,11... | collective-permute-start | bytes 196616 | tf_op jit(solution)/shard_map/ppermute | solution.py:539
  (4 other events, 50.8 us)
